TPU v7x, 256 devices: a whole 4x4x8 slice. The times are simulated.
256 devices in a mesh: view: 16 (over z, core), tile: 16 (over y, x).
Axes of the slice: x: 4, y: 4, z: 8, core: 2. Of those that a mesh axis runs over, the one named last changes fastest.
Arguments:
- params: float32 [59, 262144], P(None, ('view', 'tile')), may hold values from -25 to 25, as said below
- first: float32 [59, 262144], P(None, ('view', 'tile')), may hold values from -0.3 to 0.3
- second: float32 [59, 262144], P(None, ('view', 'tile')), may hold values from 0.0001 to 0.01
- visible: int32 [16, 16384], P(None, ('view', 'tile')), may hold values from 0 to 1023, as said below
- cameras: float32 [16, 11], replicated, as said below
- tile_lists: int32 [16, 32, 1024], P('view', 'tile'), may hold values from 0 to 16383
- tile_blocks: int32 [16, 32], P('view', 'tile'), may hold values from 1 to 8, as said below
- targets: float32 [16, 3, 8192], P('view', None, 'tile'), may hold values from 0 to 1
Outputs:
- new_params: float32 [59, 262144], P(None, ('view', 'tile'))
- new_first: float32 [59, 262144], P(None, ('view', 'tile'))
- new_second: float32 [59, 262144], P(None, ('view', 'tile'))
- rendered: float32 [16, 3, 8192], P('view', None, 'tile')
Inputs may be any that keep to these rules, and one draw needn't show every extreme that they name: `visible`: for each view and each owner (a run of 64 entries), distinct local columns of that owner. `tile_blocks`: number of live blocks of 128 entries at the head of each tile's list; the first tile of every view has all 8. `params`: rows 0 to 2 in -25 to 25; rows 3 to 5 in -6 to 2.5; row 6 in 1 to 2; rows 7 to 9 in -1 to 1; row 10 in -7.5 to -5.5; rows 11 to 58 in -1.2 to 1.2. `cameras`: column 0 in 0.5 to 1, columns 1 to 3 in -1 to 1, columns 4 and 5 in -0.3 to 0.3, column 6 in 6 to 9; focal lengths 0.7 to 1.1 times the larger side of the window of 128 by 64 pixels; the principal point within 8 pixels of the window's middle.
All inputs are finite; a program needn't handle non-finite values.
Results may differ from a plain program's by a relative error of at most 0.0003.
Values sent between devices are 32-bit elements; how exact they have to be, the bound alone decides.
No kernel may reach another device: no remote copies, remote signals or barrier semaphores. Data moves between devices by JAX's collectives and lax.ppermute only.
A program may use at most 128 MiB of HBM per device.

v0:
```python
import jax
import jax.numpy as jnp
from jax import lax
from jax.sharding import PartitionSpec as P

SIDE = 16
PIX = 256
BLOCK = 128
WIN_COLS = 8


harm_zero = 0.28209479177387814
harm_one = 0.4886025119029199
harm_two = (
    1.0925484305920792,
    -1.0925484305920792,
    0.31539156525252005,
    -1.0925484305920792,
    0.5462742152960396,
)
harm_three = (
    -0.5900435899266435,
    2.890611442640554,
    -0.4570457994644658,
    0.3731763325901154,
    -0.4570457994644658,
    1.445305721320277,
    -0.5900435899266435,
)
learn_rate = 0.05
beta_first = 0.9
beta_second = 0.999
adam_eps = 1e-08
blur_add = 0.3


def laid_out(parts, dim):
    shape = list(parts.shape[1:])
    shape[dim] *= parts.shape[0]
    return jnp.moveaxis(parts, 0, dim).reshape(shape)


def copy_for_each(array, axis):
    peers = lax.axis_size(axis)
    return lax.all_to_all(
        jnp.broadcast_to(array[None], (peers, *array.shape)), axis, 0, 0, tiled=True
    )


def gather_directly(array, axis, dim):
    return laid_out(copy_for_each(array, axis), dim)


def split_up(array, dim, peers):
    before, after = (array.shape[:dim], array.shape[dim + 1 :])
    return jnp.moveaxis(array.reshape(*before, peers, -1, *after), dim, 0)


def summed_on_arrival(array, axis, dim):
    parts = split_up(array, dim, lax.axis_size(axis))
    arrived = lax.all_to_all(parts, axis, split_axis=0, concat_axis=0, tiled=True)
    return arrived.sum(axis=0)


def rotation(real_part, axis_one, axis_two, axis_three):
    inverse = lax.rsqrt(
        real_part * real_part + axis_one * axis_one + axis_two * axis_two + axis_three * axis_three
    )
    real_unit = real_part * inverse
    unit_one = axis_one * inverse
    unit_two = axis_two * inverse
    unit_three = axis_three * inverse
    return (
        (
            1.0 - 2.0 * (unit_two * unit_two + unit_three * unit_three),
            2.0 * (unit_one * unit_two - real_unit * unit_three),
            2.0 * (unit_one * unit_three + real_unit * unit_two),
        ),
        (
            2.0 * (unit_one * unit_two + real_unit * unit_three),
            1.0 - 2.0 * (unit_one * unit_one + unit_three * unit_three),
            2.0 * (unit_two * unit_three - real_unit * unit_one),
        ),
        (
            2.0 * (unit_one * unit_three - real_unit * unit_two),
            2.0 * (unit_two * unit_three + real_unit * unit_one),
            1.0 - 2.0 * (unit_one * unit_one + unit_two * unit_two),
        ),
    )


def harmonics(first_dir, second_dir, third_dir):
    sq_first = first_dir * first_dir
    sq_second = second_dir * second_dir
    sq_third = third_dir * third_dir
    return [
        harm_zero,
        -harm_one * second_dir,
        harm_one * third_dir,
        -harm_one * first_dir,
        harm_two[0] * first_dir * second_dir,
        harm_two[1] * second_dir * third_dir,
        harm_two[2] * (2.0 * sq_third - sq_first - sq_second),
        harm_two[3] * first_dir * third_dir,
        harm_two[4] * (sq_first - sq_second),
        harm_three[0] * second_dir * (3.0 * sq_first - sq_second),
        harm_three[1] * first_dir * second_dir * third_dir,
        harm_three[2] * second_dir * (4.0 * sq_third - sq_first - sq_second),
        harm_three[3] * third_dir * (2.0 * sq_third - 3.0 * sq_first - 3.0 * sq_second),
        harm_three[4] * first_dir * (4.0 * sq_third - sq_first - sq_second),
        harm_three[5] * third_dir * (sq_first - sq_second),
        harm_three[6] * first_dir * (sq_first - 3.0 * sq_second),
    ]


def project(raw, camera):
    camera_turn = rotation(camera[0], camera[1], camera[2], camera[3])
    shift_vec = (camera[4], camera[5], camera[6])
    focal_x = camera[7]
    focal_y = camera[8]
    position = (raw[0], raw[1], raw[2])
    viewed = [
        camera_turn[across][0] * position[0]
        + camera_turn[across][1] * position[1]
        + camera_turn[across][2] * position[2]
        + shift_vec[across]
        for across in range(3)
    ]
    inverse = 1.0 / viewed[2]
    mean_x = focal_x * viewed[0] * inverse + camera[9]
    mean_y = focal_y * viewed[1] * inverse + camera[10]
    gauss_turn = rotation(raw[6], raw[7], raw[8], raw[9])
    stretch = [jnp.exp(raw[3 + column]) for column in range(3)]
    jac_xx = focal_x * inverse
    jac_xz = -focal_x * viewed[0] * inverse * inverse
    jac_yy = focal_y * inverse
    jac_yz = -focal_y * viewed[1] * inverse * inverse
    leading_x = [
        jac_xx * camera_turn[0][column] + jac_xz * camera_turn[2][column] for column in range(3)
    ]
    leading_y = [
        jac_yy * camera_turn[1][column] + jac_yz * camera_turn[2][column] for column in range(3)
    ]
    axes_x = [
        (
            leading_x[0] * gauss_turn[0][column]
            + leading_x[1] * gauss_turn[1][column]
            + leading_x[2] * gauss_turn[2][column]
        )
        * stretch[column]
        for column in range(3)
    ]
    axes_y = [
        (
            leading_y[0] * gauss_turn[0][column]
            + leading_y[1] * gauss_turn[1][column]
            + leading_y[2] * gauss_turn[2][column]
        )
        * stretch[column]
        for column in range(3)
    ]
    cov_xx = axes_x[0] * axes_x[0] + axes_x[1] * axes_x[1] + axes_x[2] * axes_x[2] + blur_add
    cov_xy = axes_x[0] * axes_y[0] + axes_x[1] * axes_y[1] + axes_x[2] * axes_y[2]
    cov_yy = axes_y[0] * axes_y[0] + axes_y[1] * axes_y[1] + axes_y[2] * axes_y[2] + blur_add
    determ = cov_xx * cov_yy - cov_xy * cov_xy
    opacity = jax.nn.sigmoid(raw[10])
    camera_eye = [
        -(
            camera_turn[0][column] * shift_vec[0]
            + camera_turn[1][column] * shift_vec[1]
            + camera_turn[2][column] * shift_vec[2]
        )
        for column in range(3)
    ]
    offset = [position[column] - camera_eye[column] for column in range(3)]
    length = lax.rsqrt(offset[0] * offset[0] + offset[1] * offset[1] + offset[2] * offset[2])
    harmonic_terms = harmonics(offset[0] * length, offset[1] * length, offset[2] * length)
    colours = []
    for channel in range(3):
        total = 0.5 + jnp.zeros_like(opacity)
        for harmonic in range(16):
            total = total + raw[11 + 16 * channel + harmonic] * harmonic_terms[harmonic]
        colours.append(total)
    return jnp.stack(
        [mean_x, mean_y, cov_yy / determ, -cov_xy / determ, cov_xx / determ, opacity] + colours
    )


def composite(rows, anchor_x, anchor_y, count):
    pixel = jnp.arange(PIX, dtype=jnp.int32)
    pixel_x = (anchor_x + (pixel % SIDE).astype(jnp.float32) + 0.5)[:, None]
    pixel_y = (anchor_y + (pixel // SIDE).astype(jnp.float32) + 0.5)[:, None]
    ahead = (
        lax.broadcasted_iota(jnp.int32, (BLOCK, BLOCK), 0)
        < lax.broadcasted_iota(jnp.int32, (BLOCK, BLOCK), 1)
    ).astype(jnp.float32)
    current = (jnp.zeros((PIX,), jnp.float32), jnp.zeros((3, PIX), jnp.float32))
    for block in range(rows.shape[1] // BLOCK):
        piece = rows[:, block * BLOCK : (block + 1) * BLOCK]
        live = (block < count).astype(jnp.float32)

        def advance(holder, piece=piece, live=live):
            carried, image = holder
            delta_x = pixel_x - piece[0][None, :]
            delta_y = pixel_y - piece[1][None, :]
            power = (
                piece[2][None, :] * delta_x * delta_x
                + 2.0 * piece[3][None, :] * delta_x * delta_y
                + piece[4][None, :] * delta_y * delta_y
            )
            alpha = piece[5][None, :] * jnp.exp(-0.5 * power) * live
            decay = jnp.log1p(-alpha)
            before = (
                jnp.dot(
                    decay,
                    ahead,
                    precision=lax.Precision.HIGHEST,
                    preferred_element_type=jnp.float32,
                )
                + carried[:, None]
            )
            weight = alpha * jnp.exp(before)
            image = image + lax.dot_general(
                piece[6:9],
                weight,
                (((1,), (1,)), ((), ())),
                precision=lax.Precision.HIGHEST,
                preferred_element_type=jnp.float32,
            )
            return (carried + jnp.sum(decay, axis=1), image)

        current = advance(current)
    return current[1]


def shards(params, first, second, visible, cameras, tile_lists, tile_blocks, targets):
    views = lax.axis_size("view")
    own_rows = visible.shape[1]
    width_params = params.shape[0]
    flat_ids = visible.reshape(-1)
    picked = jnp.take(params, flat_ids, axis=1).reshape(width_params, views, own_rows)
    outgoing, pullback = jax.vjp(
        lambda source: jax.vmap(project, in_axes=(1, 0), out_axes=1)(source, cameras), picked
    )
    projected = lax.all_to_all(outgoing, "view", split_axis=1, concat_axis=1, tiled=True).reshape(
        outgoing.shape[0], views * own_rows
    )
    everyone = gather_directly(projected, "tile", 1)
    per_device = tile_lists.shape[1]
    lists = tile_lists[0]
    counts = tile_blocks[0]
    wanted = jnp.transpose(targets[0].reshape(3, per_device, PIX), (1, 0, 2))
    first_tile = lax.axis_index("tile") * per_device

    def one_tile(inputs):
        offset_tile, listed, count, goal = inputs
        global_tile = first_tile + offset_tile
        anchor_x = (global_tile % WIN_COLS * SIDE).astype(jnp.float32)
        anchor_y = (global_tile // WIN_COLS * SIDE).astype(jnp.float32)
        rows = jnp.take(everyone, listed, axis=1)
        image, pull = jax.vjp(lambda source: composite(source, anchor_x, anchor_y, count), rows)
        (rows_grad,) = pull(2.0 * (image - goal))
        return (image, rows_grad)

    images, row_grads = lax.map(
        one_tile, (jnp.arange(per_device, dtype=jnp.int32), lists, counts, wanted)
    )
    spread = jnp.transpose(row_grads, (1, 0, 2)).reshape(everyone.shape[0], -1)
    gathered_grad = jnp.zeros(everyone.shape, jnp.float32).at[:, lists.reshape(-1)].add(spread)
    mine = summed_on_arrival(gathered_grad, "tile", 1)
    arrived = lax.all_to_all(
        mine.reshape(mine.shape[0], views, own_rows),
        "view",
        split_axis=1,
        concat_axis=1,
        tiled=True,
    )
    (returned,) = pullback(arrived)
    grad = (
        jnp.zeros(params.shape, jnp.float32).at[:, flat_ids].add(returned.reshape(width_params, -1))
    )
    hits = jnp.zeros((params.shape[1],), jnp.float32).at[flat_ids].add(1.0)
    seen = (hits > 0.5)[None, :]
    moved_first = beta_first * first + (1.0 - beta_first) * grad
    moved_second = beta_second * second + (1.0 - beta_second) * grad * grad
    moved_params = params - learn_rate * moved_first / (jnp.sqrt(moved_second) + adam_eps)
    new_first = jnp.where(seen, moved_first, first)
    new_second = jnp.where(seen, moved_second, second)
    new_params = jnp.where(seen, moved_params, params)
    rendered = jnp.transpose(images, (1, 0, 2)).reshape(1, 3, per_device * PIX)
    return (new_params, new_first, new_second, rendered)


def solution(mesh):
    in_specs = (
        P(None, ("view", "tile")),
        P(None, ("view", "tile")),
        P(None, ("view", "tile")),
        P(None, ("view", "tile")),
        P(),
        P("view", "tile", None),
        P("view", "tile"),
        P("view", None, "tile"),
    )
    out_specs = (
        P(None, ("view", "tile")),
        P(None, ("view", "tile")),
        P(None, ("view", "tile")),
        P("view", None, "tile"),
    )
    return jax.shard_map(shards, mesh=mesh, in_specs=in_specs, out_specs=out_specs, check_vma=False)
```

profile of v0, /device:TPU:1, one launch (start us, length us, event | category | flops | bytes accessed | tf_op | source)
XLA Modules:
  0.0 200.0 jit_solution(12859663830820406313)
XLA Ops:
  0.7 0.8 reshape.23188
  1.4 0.8 reshape.23189
  2.2 1.2 copy.124
  3.4 2.8 %gather_fusion.1 = f32[1024,59]{1,0:T(8,128)S(1)} fusion(f32[59,1024]{0,1:T(8,128)S(1)} %copy.124, s32[1024]{0:T(1024)S(1)} %broadcast_clamp_fusion.1), kind=kCustom, calls=%fused_computation.1 | custom fusion | bytes 487424 | tf_op jit(solution)/shard_map/jit(_take)/gather | solution.py:241
  7.1 0.9 slice_multiply_fusion.11
  8.1 1.2 slice_reduce_fusion.40
  13.4 1.4 negate_reduce_fusion.2
  15.5 17.2 %all_to_all.20 = f32[16,1,576]{2,1,0:T(1,128)S(1)} all-to-all(f32[16,1,576]{2,1,0:T(1,128)S(1)} %reshape.23617), channel_id=1, replica_groups=mesh['view'=16,'tile'=16] {'view'}, dimensions={0} | all-to-all | bytes 73728 | tf_op jit(solution)/shard_map/all_to_all | solution.py:245
  32.7 0.5 broadcast.11473
  33.2 0.7 reduce.375
  34.1 1.1 broadcast_in_dim.384
  35.2 6.8 %all-to-all-start.1 = ((f32[16,9,1024]{2,1,0:T(8,128)}), f32[16,9,1024]{2,1,0:T(8,128)S(1)}, u32[]{:S(2)}, u32[]{:S(2)}) async-start(f32[16,9,1024]{2,1,0:T(8,128)} %broadcast_in_dim.384), calls=%async_computation.1 | async-start | bytes 2097152 | tf_op jit(solution)/shard_map/all_to_all | solution.py:45
  42.1 16.2 %all-to-all-done.1 = f32[16,9,1024]{2,1,0:T(8,128)S(1)} async-done(((f32[16,9,1024]{2,1,0:T(8,128)}), f32[16,9,1024]{2,1,0:T(8,128)S(1)}, u32[]{:S(2)}, u32[]{:S(2)}) %all-to-all-start.1) | async-done | bytes 589856 | tf_op jit(solution)/shard_map/all_to_all | solution.py:45
  58.3 4.7 %copy.132 = f32[9,16,1024]{0,2,1:T(8,128)} copy(f32[9,16,1024]{2,0,1:T(8,128)S(1)} %bitcast.315) | data formatting | bytes 1179648 | tf_op jit(solution)/shard_map/while | solution.py:265
  63.0 66.7 %while.15 = (s32[]{:T(128)}, f32[2,3,256]{2,1,0:T(4,128)S(1)}, f32[2,9,1024]{2,1,0:T(8,128)S(1)}, s32[2,1024]{1,0:T(2,128)S(1)}, f32[9,16384]{0,1:T(8,128)}, /*i...) while((s32[]{:T(128)}, f32[2,3,256]{2,1,0:T(4,128)S(1)}, ...), condition=%wide.region_64.65_spmd, body=%wide.region_1.64_spmd.sunk | while | flops 865354496 | bytes 8221440 | solution.py:265
  63.0 0.6 dynamic_slice.39
  64.3 6.2 %gather_fusion = f32[1024,9]{1,0:T(8,128)S(1)} fusion(f32[9,16384]{0,1:T(8,128)} %get-tuple-element.1008, s32[1024]{0:T(1024)S(1)} %broadcast_clamp_fusion.3), kind=kCustom, calls=%fused_computation.clone.1 | custom fusion | bytes 77824 | tf_op jit(solution)/shard_map/while/body/eval_jaxpr/jit(_take)/gather | solution.py:260
  70.7 0.7 slice_reduce_fusion.104
  71.4 0.6 dynamic_slice.38
  73.0 0.7 slice_reduce_fusion.103
  87.9 0.5 fusion.634
  89.2 0.5 fusion.636
  90.5 0.5 fusion.638
  91.8 0.5 fusion.640
  93.1 0.5 fusion.642
  96.2 0.6 dynamic_slice.39
  97.6 6.2 %gather_fusion = f32[1024,9]{1,0:T(8,128)S(1)} fusion(f32[9,16384]{0,1:T(8,128)} %get-tuple-element.1008, s32[1024]{0:T(1024)S(1)} %broadcast_clamp_fusion.3), kind=kCustom, calls=%fused_computation.clone.1 | custom fusion | bytes 77824 | tf_op jit(solution)/shard_map/while/body/eval_jaxpr/jit(_take)/gather | solution.py:260
  104.0 0.7 slice_reduce_fusion.104
  104.7 0.6 dynamic_slice.38
  106.2 0.7 slice_reduce_fusion.103
  121.1 0.5 fusion.634
  123.7 0.5 fusion.638
  126.3 0.5 fusion.642
  130.3 15.2 %scatter_custom_fusion.1 = f32[9,16384]{0,1:T(8,128)} fusion(s32[2048]{0:T(1024)S(1)} %bitcast.371, f32[2048,9]{1,0:T(8,128)S(1)} %copy.109, f32[]{:T(128)} %constant.260.clone.1), kind=kCustom, calls=%fused_computation.563 | custom fusion | flops 18432 | bytes 589828 | tf_op jit(solution)/shard_map/scatter-add | solution.py:269
  145.4 6.1 %copy.110 = f32[9,16,1024]{2,0,1:T(8,128)} copy(f32[9,16,1024]{0,2,1:T(8,128)} %bitcast.313) | data formatting | bytes 1179648 | tf_op jit(solution)/shard_map/reshape | solution.py:56
  151.6 4.5 %all-to-all-start.2 = ((f32[16,9,1024]{2,1,0:T(8,128)}), f32[16,9,1024]{2,1,0:T(8,128)S(1)}, u32[]{:S(2)}, u32[]{:S(2)}) async-start(f32[16,9,1024]{2,1,0:T(8,128)} %bitcast.75), calls=%async_computation.2 | async-start | bytes 2097152 | tf_op jit(solution)/shard_map/all_to_all | solution.py:61
  156.1 7.6 %scatter_custom_fusion = f32[1024]{0:T(1024)S(1)} fusion(s32[1024]{0:T(1024)S(1)} %bitcast.344, f32[1024]{0:T(1024)S(1)} %broadcast.10376, f32[]{:T(128)} %constant.260.clone.1), kind=kCustom, calls=%fused_computation.902 | custom fusion | flops 1024 | bytes 4100 | tf_op jit(solution)/shard_map/scatter-add | solution.py:282
  163.7 8.1 %all-to-all-done.2 = f32[16,9,1024]{2,1,0:T(8,128)S(1)} async-done(((f32[16,9,1024]{2,1,0:T(8,128)}), f32[16,9,1024]{2,1,0:T(8,128)S(1)}, u32[]{:S(2)}, u32[]{:S(2)}) %all-to-all-start.2) | async-done | bytes 589856 | tf_op jit(solution)/shard_map/all_to_all | solution.py:61
  172.4 0.7 reshape.23619
  173.1 6.2 %all-to-all-start.3 = ((f32[16,1,576]{2,1,0:T(1,128)}), f32[16,1,576]{2,1,0:T(1,128)S(1)}, u32[]{:S(2)}, u32[]{:S(2)}) async-start(f32[16,1,576]{2,1,0:T(1,128)} %reshape.23619), calls=%async_computation.3 | async-start | bytes 81920 | tf_op jit(solution)/shard_map/all_to_all | solution.py:271
  179.7 0.6 reshape.23195
  180.3 6.4 %all-to-all-done.3 = f32[16,1,576]{2,1,0:T(1,128)S(1)} async-done(((f32[16,1,576]{2,1,0:T(1,128)}), f32[16,1,576]{2,1,0:T(1,128)S(1)}, u32[]{:S(2)}, u32[]{:S(2)}) %all-to-all-start.3) | async-done | bytes 36896 | tf_op jit(solution)/shard_map/all_to_all | solution.py:271
  186.8 0.7 reduce.376
  188.9 6.1 %scatter_custom_fusion.2 = f32[59,1024]{0,1:T(8,128)S(1)} fusion(s32[1024]{0:T(1024)S(1)} %bitcast.345, f32[1024,59]{1,0:T(8,128)S(1)} %bitcast.319, f32[]{:T(128)} %constant.260.clone.1), kind=kCustom, calls=%fused_computation.573 | custom fusion | flops 60416 | bytes 241668 | tf_op jit(solution)/shard_map/scatter-add | solution.py:280
  195.1 1.2 fusion.349
  196.3 1.9 copy.129
  198.2 0.9 copy.130
  199.1 0.9 copy.131
  (299 shorter events, 41.0 us)
Async XLA Ops:
  0.6 41.4 %copy-start.3 = (f32[1,3,512]{2,0,1:T(1,128)S(1)}, f32[1,3,512]{2,0,1:T(1,128)}, u32[]{:S(2)}) copy-start(f32[1,3,512]{2,0,1:T(1,128)} %param.17) | copy-start | bytes 18436
  0.6 41.4 %copy-start.2 = (s32[1,2,1024]{2,1,0:T(2,128)S(1)}, s32[1,2,1024]{2,1,0:T(2,128)}, u32[]{:S(2)}) copy-start(s32[1,2,1024]{2,1,0:T(2,128)} %param.15) | copy-start | bytes 24580
  6.4 56.6 %copy-start.4 = (s32[1,2]{1,0:T(1,128)S(1)}, s32[1,2]{1,0:T(1,128)}, u32[]{:S(2)}) copy-start(s32[1,2]{1,0:T(1,128)} %param.16) | copy-start | bytes 28
  35.2 23.1 %all-to-all-start.1 = ((f32[16,9,1024]{2,1,0:T(8,128)}), f32[16,9,1024]{2,1,0:T(8,128)S(1)}, u32[]{:S(2)}, u32[]{:S(2)}) async-start(f32[16,9,1024]{2,1,0:T(8,128)} %broadcast_in_dim.384), calls=%async_computation.1 | async-start | bytes 2097152 | tf_op jit(solution)/shard_map/all_to_all | solution.py:45
  145.4 33.8 %copy-start = (f32[59,1024]{1,0:T(8,128)S(1)}, f32[59,1024]{1,0:T(8,128)}, u32[]{:S(2)}) copy-start(f32[59,1024]{1,0:T(8,128)} %param.11) | copy-start | bytes 724996
  145.4 34.1 %copy-start.1 = (f32[59,1024]{1,0:T(8,128)S(1)}, f32[59,1024]{1,0:T(8,128)}, u32[]{:S(2)}) copy-start(f32[59,1024]{1,0:T(8,128)} %param.12) | copy-start | bytes 724996
  151.6 20.3 %all-to-all-start.2 = ((f32[16,9,1024]{2,1,0:T(8,128)}), f32[16,9,1024]{2,1,0:T(8,128)S(1)}, u32[]{:S(2)}, u32[]{:S(2)}) async-start(f32[16,9,1024]{2,1,0:T(8,128)} %bitcast.75), calls=%async_computation.2 | async-start | bytes 2097152 | tf_op jit(solution)/shard_map/all_to_all | solution.py:61
  173.1 13.7 %all-to-all-start.3 = ((f32[16,1,576]{2,1,0:T(1,128)}), f32[16,1,576]{2,1,0:T(1,128)S(1)}, u32[]{:S(2)}, u32[]{:S(2)}) async-start(f32[16,1,576]{2,1,0:T(1,128)} %reshape.23619), calls=%async_computation.3 | async-start | bytes 81920 | tf_op jit(solution)/shard_map/all_to_all | solution.py:271
where the time goes:
time: 201 us; the launch traced here: 200 us
  other arithmetic  44.8 us (22%)
  local copies, waits for them, and re-layouts  44.3 us (22%)
  matrix products  31.4 us (16%)
  waiting for transfers between devices  30.7 us (15%)
  starting transfers between devices  17.4 us (9%)
  blocking collectives  17.2 us (9%)
  loops' own time  13.1 us (7%)
    dot_general x48, matrix products, advance(): lax.dot_general(piece[6:9], weight, (((1,), (1,)), ((), ())), precision=l...  18.1 us
    all_to_all x1, blocking collectives, shards(): lax.all_to_all(outgoing, 'view', split_axis=1, concat_axis=1, tiled=True)  17.2 us
    all_to_all x1, waiting for transfers between devices, copy_for_each(): lax.all_to_all(jnp.broadcast_to(array[None], (peers, *array.shape)), axis...  16.2 us
    scatter-add x1, other arithmetic, shards(): jnp.zeros(everyone.shape, jnp.float32).at[:, lists.reshape(-1)].add(spread)  15.2 us
    dot_general x32, matrix products, advance(): jnp.dot(decay, ahead, precision=lax.Precision.HIGHEST, preferred_element_...  13.3 us
    another operation x1, loops' own time, shards(): lax.map(one_tile, (jnp.arange(per_device, dtype=jnp.int32), lists, counts...  13.1 us
    gather x2, local copies, waits for them, and re-layouts, one_tile(): rows = jnp.take(everyone, listed, axis=1)  12.4 us
    all_to_all x1, waiting for transfers between devices, summed_on_arrival(): lax.all_to_all(parts, axis, split_axis=0, concat_axis=0, tiled=True)  8.11 us
  transfers between devices with their start and end apart: 3, of which 3 were waited for; matrix products, arithmetic and copies ran while one was open for 4% of the time, Pallas kernels for 0%

commit v1 on v0

v1 whole, which is shorter than its diff:
```python
import functools

import jax
import jax.numpy as jnp
from jax import lax
from jax.experimental import pallas as pl
from jax.experimental.pallas import tpu as pltpu
from jax.sharding import PartitionSpec as P

SIDE = 16
PIX = 256
BLOCK = 128
WIN_COLS = 8


harm_zero = 0.28209479177387814
harm_one = 0.4886025119029199
harm_two = (
    1.0925484305920792,
    -1.0925484305920792,
    0.31539156525252005,
    -1.0925484305920792,
    0.5462742152960396,
)
harm_three = (
    -0.5900435899266435,
    2.890611442640554,
    -0.4570457994644658,
    0.3731763325901154,
    -0.4570457994644658,
    1.445305721320277,
    -0.5900435899266435,
)
learn_rate = 0.05
beta_first = 0.9
beta_second = 0.999
adam_eps = 1e-08
blur_add = 0.3


def rotation(real_part, axis_one, axis_two, axis_three):
    inverse = lax.rsqrt(
        real_part * real_part + axis_one * axis_one + axis_two * axis_two + axis_three * axis_three
    )
    real_unit = real_part * inverse
    unit_one = axis_one * inverse
    unit_two = axis_two * inverse
    unit_three = axis_three * inverse
    return (
        (
            1.0 - 2.0 * (unit_two * unit_two + unit_three * unit_three),
            2.0 * (unit_one * unit_two - real_unit * unit_three),
            2.0 * (unit_one * unit_three + real_unit * unit_two),
        ),
        (
            2.0 * (unit_one * unit_two + real_unit * unit_three),
            1.0 - 2.0 * (unit_one * unit_one + unit_three * unit_three),
            2.0 * (unit_two * unit_three - real_unit * unit_one),
        ),
        (
            2.0 * (unit_one * unit_three - real_unit * unit_two),
            2.0 * (unit_two * unit_three + real_unit * unit_one),
            1.0 - 2.0 * (unit_one * unit_one + unit_two * unit_two),
        ),
    )


def harmonics(first_dir, second_dir, third_dir):
    sq_first = first_dir * first_dir
    sq_second = second_dir * second_dir
    sq_third = third_dir * third_dir
    return [
        harm_zero,
        -harm_one * second_dir,
        harm_one * third_dir,
        -harm_one * first_dir,
        harm_two[0] * first_dir * second_dir,
        harm_two[1] * second_dir * third_dir,
        harm_two[2] * (2.0 * sq_third - sq_first - sq_second),
        harm_two[3] * first_dir * third_dir,
        harm_two[4] * (sq_first - sq_second),
        harm_three[0] * second_dir * (3.0 * sq_first - sq_second),
        harm_three[1] * first_dir * second_dir * third_dir,
        harm_three[2] * second_dir * (4.0 * sq_third - sq_first - sq_second),
        harm_three[3] * third_dir * (2.0 * sq_third - 3.0 * sq_first - 3.0 * sq_second),
        harm_three[4] * first_dir * (4.0 * sq_third - sq_first - sq_second),
        harm_three[5] * third_dir * (sq_first - sq_second),
        harm_three[6] * first_dir * (sq_first - 3.0 * sq_second),
    ]


def project(raw, camera):
    camera_turn = rotation(camera[0], camera[1], camera[2], camera[3])
    shift_vec = (camera[4], camera[5], camera[6])
    focal_x = camera[7]
    focal_y = camera[8]
    position = (raw[0], raw[1], raw[2])
    viewed = [
        camera_turn[across][0] * position[0]
        + camera_turn[across][1] * position[1]
        + camera_turn[across][2] * position[2]
        + shift_vec[across]
        for across in range(3)
    ]
    inverse = 1.0 / viewed[2]
    mean_x = focal_x * viewed[0] * inverse + camera[9]
    mean_y = focal_y * viewed[1] * inverse + camera[10]
    gauss_turn = rotation(raw[6], raw[7], raw[8], raw[9])
    stretch = [jnp.exp(raw[3 + column]) for column in range(3)]
    jac_xx = focal_x * inverse
    jac_xz = -focal_x * viewed[0] * inverse * inverse
    jac_yy = focal_y * inverse
    jac_yz = -focal_y * viewed[1] * inverse * inverse
    leading_x = [
        jac_xx * camera_turn[0][column] + jac_xz * camera_turn[2][column] for column in range(3)
    ]
    leading_y = [
        jac_yy * camera_turn[1][column] + jac_yz * camera_turn[2][column] for column in range(3)
    ]
    axes_x = [
        (
            leading_x[0] * gauss_turn[0][column]
            + leading_x[1] * gauss_turn[1][column]
            + leading_x[2] * gauss_turn[2][column]
        )
        * stretch[column]
        for column in range(3)
    ]
    axes_y = [
        (
            leading_y[0] * gauss_turn[0][column]
            + leading_y[1] * gauss_turn[1][column]
            + leading_y[2] * gauss_turn[2][column]
        )
        * stretch[column]
        for column in range(3)
    ]
    cov_xx = axes_x[0] * axes_x[0] + axes_x[1] * axes_x[1] + axes_x[2] * axes_x[2] + blur_add
    cov_xy = axes_x[0] * axes_y[0] + axes_x[1] * axes_y[1] + axes_x[2] * axes_y[2]
    cov_yy = axes_y[0] * axes_y[0] + axes_y[1] * axes_y[1] + axes_y[2] * axes_y[2] + blur_add
    determ = cov_xx * cov_yy - cov_xy * cov_xy
    opacity = jax.nn.sigmoid(raw[10])
    camera_eye = [
        -(
            camera_turn[0][column] * shift_vec[0]
            + camera_turn[1][column] * shift_vec[1]
            + camera_turn[2][column] * shift_vec[2]
        )
        for column in range(3)
    ]
    offset = [position[column] - camera_eye[column] for column in range(3)]
    length = lax.rsqrt(offset[0] * offset[0] + offset[1] * offset[1] + offset[2] * offset[2])
    harmonic_terms = harmonics(offset[0] * length, offset[1] * length, offset[2] * length)
    colours = []
    for channel in range(3):
        total = 0.5 + jnp.zeros_like(opacity)
        for harmonic in range(16):
            total = total + raw[11 + 16 * channel + harmonic] * harmonic_terms[harmonic]
        colours.append(total)
    return [mean_x, mean_y, cov_yy / determ, -cov_xy / determ, cov_xx / determ, opacity] + colours


F32 = jnp.float32
BF16 = jnp.bfloat16
PARAMS = 59
ROWS = 64
LOG2E = 1.4426950408889634


def iota(shape, dim):
    return lax.broadcasted_iota(jnp.int32, shape, dim)


def parts_of(value, count):
    parts = []
    for _ in range(count):
        part = value.astype(BF16)
        parts.append(part)
        value = value - part.astype(F32)
    return parts


def mm(left, right, dims):
    return lax.dot_general(left, right, (dims, ((), ())), preferred_element_type=F32)


def stacked(rows, width):
    sub = iota((8, width), 0)
    out = jnp.zeros((8, width), F32)
    for place, row in enumerate(rows):
        out = jnp.where(sub == place, jnp.broadcast_to(row, (8, width)), out)
    return out


def seen_columns(ids_ref, first, width):
    row = jnp.concatenate(
        [ids_ref[first + step : first + step + 1, :] for step in range(width // 64)], axis=1
    )
    return (iota((1024, width), 0) == row).astype(BF16)


def camera_arrays(cameras_ref):
    view = 2 * iota((8, 128), 0) + (iota((8, 128), 1) >= 64).astype(jnp.int32)
    masks = [view == index for index in range(16)]
    arrays = []
    for field in range(11):
        array = jnp.full((8, 128), cameras_ref[0, field], F32)
        for index in range(1, 16):
            array = jnp.where(masks[index], cameras_ref[index, field], array)
        arrays.append(array)
    return arrays


def raw_rows(picked_ref):
    return [picked_ref[pl.ds(row, 8, stride=ROWS), :] for row in range(PARAMS)]


def project_kernel(ids_ref, cameras_ref, params_ref, picked_ref, send_ref, swap):
    params = params_ref[...]
    split = parts_of(params, 3)
    for pair in range(4):
        onehot = seen_columns(ids_ref, pair * 4, 256)
        picked = sum(mm(part, onehot, ((1,), (0,))) for part in split)
        picked_ref[pair * 128 : pair * 128 + PARAMS, :] = picked[:, :128]
        picked_ref[pair * 128 + 64 : pair * 128 + 64 + PARAMS, :] = picked[:, 128:]
    values = project(raw_rows(picked_ref), camera_arrays(cameras_ref))
    for place in range(8):
        swap[place * 8 : place * 8 + 8, :] = values[place]
    low = iota((8, 128), 1) < 64
    for pair in range(8):
        main = swap[pl.ds(pair, 8, stride=8), :]
        last = jnp.broadcast_to(values[8][pair : pair + 1, :], (8, 128))
        send_ref[2 * pair] = jnp.where(low, main, pltpu.roll(last, 64, 1))
        send_ref[2 * pair + 1] = jnp.where(low, pltpu.roll(main, 64, 1), last)


def unpack_pair(even, odd):
    low = iota((8, 128), 1) < 64
    main = jnp.where(low, even, pltpu.roll(odd, 64, 1))
    last = jnp.where(low, pltpu.roll(even, 64, 1), odd)
    return main, last[0:1, :]


def spread_kernel(arrived_ref, out_ref):
    for pair in range(8):
        main, last = unpack_pair(arrived_ref[2 * pair], arrived_ref[2 * pair + 1])
        for peer in range(16):
            out_ref[peer, pair * 8 : pair * 8 + 8, :] = main
            out_ref[peer, 64 + pair : 65 + pair, :] = last


def render_kernel(
    place_ref,
    counts_ref,
    lists_ref,
    targets_ref,
    everyone_ref,
    image_ref,
    out_ref,
    table,
    onehot,
    chosen,
    picked,
    alphas,
    weights,
    shades,
    scattered,
):
    count = 2048
    width = 256
    turn = (iota((128, 1024), 0) == (iota((128, 1024), 1) >> 3)).astype(BF16)
    pick_block = iota((8, 1024), 0) == (iota((8, 1024), 1) & 7)
    for tile in range(2):
        listed = lists_ref[tile]
        low_part = mm((listed & 127).astype(F32).astype(BF16), turn, ((1,), (0,)))
        high_part = mm((listed >> 7).astype(F32).astype(BF16), turn, ((1,), (0,)))
        low_row = jnp.sum(jnp.where(pick_block, low_part, 0.0), axis=0, keepdims=True)
        high_row = jnp.sum(jnp.where(pick_block, high_part, 0.0), axis=0, keepdims=True)
        low_row = low_row.astype(jnp.int32)
        high_row = high_row.astype(jnp.int32)
        lane_index = ((high_row >> 3) & 1) * 128 + low_row
        group_index = (high_row >> 4) * 8 + (high_row & 7)
        span = slice(tile * 1024, tile * 1024 + 1024)
        onehot[:, span] = (iota((256, 1024), 0) == lane_index).astype(BF16)
        chosen[:, span] = jnp.broadcast_to(group_index, (8, 1024))

    for half in range(8):
        for side in range(2):
            lanes = slice(side * 128, side * 128 + 128)
            main = parts_of(everyone_ref[2 * half + side, 0:64, :], 3)
            last = parts_of(everyone_ref[2 * half + side, 64:72, :], 3)
            for part in range(3):
                table[part, half * 64 : half * 64 + 64, lanes] = main[part]
                table[part, 512 + half * 8 : 520 + half * 8, lanes] = last[part]

    def gather_chunk(chunk, carry):
        lanes = pl.ds(pl.multiple_of(chunk * width, width), width)
        hot = onehot[:, lanes]
        found = mm(table[0], hot, ((1,), (0,)))
        found = found + mm(table[1], hot, ((1,), (0,)))
        found = found + mm(table[2], hot, ((1,), (0,)))
        group = chosen[:, lanes]
        main = jnp.zeros((8, width), F32)
        last = jnp.zeros((8, width), F32)
        sub = iota((8, width), 0)
        for half in range(8):
            for place in range(8):
                start = half * 64 + place * 8
                main = jnp.where(group == half * 8 + place, found[start : start + 8, :], main)
            last = jnp.where(
                group == half * 8 + sub, found[512 + half * 8 : 520 + half * 8, :], last
            )
        picked[0:8, lanes] = main
        picked[8:16, lanes] = jnp.broadcast_to(jnp.sum(last, axis=0, keepdims=True), (8, width))
        return carry

    lax.fori_loop(0, count // width, gather_chunk, 0)

    pixel = iota((8, PIX), 1)
    pixel_x = (pixel & (SIDE - 1)).astype(F32) + (0.5 - SIDE / 2)
    pixel_y = (pixel >> 4).astype(F32) + (0.5 - SIDE / 2)
    sub = iota((8, PIX), 0)
    basis = jnp.where(sub == 0, 1.0, 0.0)
    for place, row in enumerate(
        [pixel_x, pixel_y, pixel_x * pixel_x, pixel_x * pixel_y, pixel_y * pixel_y]
    ):
        basis = jnp.where(sub == place + 1, row, basis)
    blank = jnp.zeros((8, PIX), F32)
    basis_three = jnp.concatenate([basis, basis, basis, blank], axis=0).astype(BF16)
    basis_once = jnp.concatenate([basis, blank], axis=0).astype(BF16)

    def rows_of(tile):
        span = slice(tile * 1024, tile * 1024 + 1024)
        held = picked[:, span]
        global_tile = place_ref[0] * 2 + tile
        centre_x = (global_tile % WIN_COLS * SIDE + SIDE // 2).astype(F32)
        centre_y = (global_tile // WIN_COLS * SIDE + SIDE // 2).astype(F32)
        rows = [held[place : place + 1, :] for place in range(9)]
        rows[0] = rows[0] - centre_x
        rows[1] = rows[1] - centre_y
        return rows

    block = iota((1, 1024), 1) & 7
    blank_row = jnp.zeros((8, 1024), F32)
    colour_rows = []
    for tile in range(2):
        mean_x, mean_y, con_a, con_b, con_c, opacity, *colour = rows_of(tile)
        live = block < counts_ref[0, tile]
        slope_x = con_a * mean_x + con_b * mean_y
        slope_y = con_b * mean_x + con_c * mean_y
        scale = -0.5 * LOG2E
        level = scale * (slope_x * mean_x + slope_y * mean_y) + jnp.log(opacity) * LOG2E
        terms = [
            jnp.where(live, level, -1000.0),
            jnp.where(live, (-2.0 * scale) * slope_x, 0.0),
            jnp.where(live, (-2.0 * scale) * slope_y, 0.0),
            jnp.where(live, scale * con_a, 0.0),
            jnp.where(live, (2.0 * scale) * con_b, 0.0),
            jnp.where(live, scale * con_c, 0.0),
        ]
        split = [part.astype(F32) for part in parts_of(stacked(terms, 1024), 3)]
        coefficients = jnp.concatenate(split + [blank_row], axis=0).astype(BF16)
        alphas[tile] = mm(coefficients, basis_three, ((0,), (0,)))
        colour_rows.append(stacked(colour, 1024))

    steps = 8

    def advance(outer, held):
        held = list(held)
        for inner in range(steps):
            start = pl.multiple_of((outer * steps + inner) * 8, 8)
            for tile in range(2):
                alpha = jnp.exp2(alphas[tile, pl.ds(start, 8), :])
                weight = alpha * held[tile]
                held[tile] = held[tile] - weight
                alphas[tile, pl.ds(start, 8), :] = alpha
                weights[tile, pl.ds(start, 8), :] = weight
        return tuple(held)

    ones = jnp.ones((8, PIX), F32)
    left = lax.fori_loop(0, 128 // steps, advance, (ones, ones))

    behind = []
    ahead = []
    blame = []
    sub_wide = iota((8, 1024), 0)
    block_wide = iota((8, 1024), 1) & 7
    for tile in range(2):
        colour = colour_rows[tile]
        separate = []
        for channel in range(3):
            row = jnp.broadcast_to(colour[channel : channel + 1, :], (8, 1024))
            separate.append(jnp.where(sub_wide == block_wide, row, 0.0))
        fine, rough = parts_of(jnp.concatenate(separate, axis=0), 2)
        both = jnp.concatenate([fine.astype(F32), rough.astype(F32)], axis=0).astype(BF16)
        first_part, second_part = parts_of(weights[tile], 2)
        sums = mm(both, first_part, ((1,), (0,))) + mm(both, second_part, ((1,), (0,)))
        passed = left[tile]
        total = passed
        for shift in (1, 2, 4):
            total = total * jnp.where(sub >= shift, pltpu.roll(total, shift, 0), 1.0)
        before = jnp.where(sub >= 1, pltpu.roll(total, 1, 0), 1.0)
        ahead.append(before)
        value = jnp.zeros((8, PIX), F32)
        slopes = []
        for channel in range(3):
            own = sums[channel * 8 : channel * 8 + 8, :]
            own = own + sums[24 + channel * 8 : 32 + channel * 8, :]
            image = jnp.sum(own * before, axis=0, keepdims=True)
            lanes = slice(tile * PIX, tile * PIX + PIX)
            image_ref[channel : channel + 1, lanes] = image
            slope = 2.0 * (image - targets_ref[channel : channel + 1, lanes])
            slopes.append(slope)
            value = value + slope * own
        factor = passed
        for shift in (1, 2, 4):
            inside = sub < 8 - shift
            value = value + factor * jnp.where(inside, pltpu.roll(value, 8 - shift, 0), 0.0)
            factor = factor * jnp.where(inside, pltpu.roll(factor, 8 - shift, 0), 1.0)
        behind.append(jnp.where(sub < 7, pltpu.roll(value, 7, 0), 0.0))
        slope_parts = [part.astype(F32) for part in parts_of(stacked(slopes, PIX), 3)]
        colour_parts = [part.astype(F32) for part in parts_of(colour, 3)]
        pairs = [(0, 0), (0, 1), (1, 0), (1, 1), (0, 2), (2, 0)]
        left_side = jnp.concatenate([colour_parts[a] for a, _ in pairs], axis=0).astype(BF16)
        right_side = jnp.concatenate([slope_parts[b] for _, b in pairs], axis=0).astype(BF16)
        shades[tile] = mm(left_side, right_side, ((0,), (0,)))
        blame.append(jnp.concatenate(slope_parts[:2], axis=0).astype(BF16))

    def retreat(outer, held):
        held = list(held)
        for inner in range(steps):
            start = pl.multiple_of((127 - (outer * steps + inner)) * 8, 8)
            for tile in range(2):
                alpha = alphas[tile, pl.ds(start, 8), :]
                weight = weights[tile, pl.ds(start, 8), :] * ahead[tile]
                gap = shades[tile, pl.ds(start, 8), :] - held[tile]
                held[tile] = held[tile] + alpha * gap
                shades[tile, pl.ds(start, 8), :] = weight * gap
                weights[tile, pl.ds(start, 8), :] = weight
        return tuple(held)

    lax.fori_loop(0, 128 // steps, retreat, tuple(behind))

    for tile in range(2):
        moments = sum(
            mm(basis_once, part, ((1,), (1,))) for part in parts_of(shades[tile], 3)
        )
        tints = sum(mm(blame[tile], part, ((1,), (1,))) for part in parts_of(weights[tile], 2))
        tints = tints[0:8, :] + tints[8:16, :]
        mean_x, mean_y, con_a, con_b, con_c, opacity, *_ = rows_of(tile)
        sum_one, sum_x, sum_y, sum_xx, sum_xy, sum_yy = [
            moments[place : place + 1, :] for place in range(6)
        ]
        near_x = sum_x - mean_x * sum_one
        near_y = sum_y - mean_y * sum_one
        near_xx = sum_xx - mean_x * (sum_x + near_x)
        near_xy = sum_xy - mean_x * sum_y - mean_y * near_x
        near_yy = sum_yy - mean_y * (sum_y + near_y)
        grads = [
            con_a * near_x + con_b * near_y,
            con_b * near_x + con_c * near_y,
            -0.5 * near_xx,
            -near_xy,
            -0.5 * near_yy,
            sum_one / opacity,
            tints[0:1, :],
            tints[1:2, :],
        ]
        span = slice(tile * 1024, tile * 1024 + 1024)
        picked[0:8, span] = stacked(grads, 1024)
        picked[8:16, span] = jnp.broadcast_to(tints[2:3, :], (8, 1024))

    def scatter_chunk(chunk, carry):
        lanes = pl.ds(pl.multiple_of(chunk * width, width), width)
        group = chosen[:, lanes]
        sub = iota((8, width), 0)
        main = [part.astype(F32) for part in parts_of(picked[0:8, lanes], 2)]
        last = [part.astype(F32) for part in parts_of(picked[8:16, lanes], 2)]
        for part in range(2):
            for pair in range(32):
                rows = jnp.concatenate(
                    [jnp.where(group == 2 * pair + side, main[part], 0.0) for side in range(2)],
                    axis=0,
                )
                scattered[part, pair * 16 : pair * 16 + 16, lanes] = rows.astype(BF16)
            for pair in range(4):
                rows = jnp.concatenate(
                    [
                        jnp.where(group == (2 * pair + side) * 8 + sub, last[part], 0.0)
                        for side in range(2)
                    ],
                    axis=0,
                )
                scattered[part, 512 + pair * 16 : 528 + pair * 16, lanes] = rows.astype(BF16)
        return carry

    lax.fori_loop(0, count // width, scatter_chunk, 0)
    hot = onehot[...]
    summed = mm(scattered[0], hot, ((1,), (1,))) + mm(scattered[1], hot, ((1,), (1,)))
    for half in range(8):
        for side in range(2):
            lanes = slice(side * 128, side * 128 + 128)
            out_ref[2 * half + side, 0:64, :] = summed[half * 64 : half * 64 + 64, lanes]
            out_ref[2 * half + side, 64:72, :] = summed[
                512 + half * 8 : 520 + half * 8, lanes
            ]


def merge_kernel(arrived_ref, send_ref):
    low = iota((8, 128), 1) < 64
    total = arrived_ref[0]
    for peer in range(1, 16):
        total = total + arrived_ref[peer]
    for pair in range(8):
        main = total[pair * 8 : pair * 8 + 8, :]
        last = jnp.broadcast_to(total[64 + pair : 65 + pair, :], (8, 128))
        send_ref[2 * pair] = jnp.where(low, main, pltpu.roll(last, 64, 1))
        send_ref[2 * pair + 1] = jnp.where(low, pltpu.roll(main, 64, 1), last)


def update_kernel(
    ids_ref,
    cameras_ref,
    arrived_ref,
    picked_ref,
    params_ref,
    first_ref,
    second_ref,
    new_params_ref,
    new_first_ref,
    new_second_ref,
    swap,
    turned,
    onehot,
):
    lasts = []
    for pair in range(8):
        main, last = unpack_pair(arrived_ref[2 * pair], arrived_ref[2 * pair + 1])
        swap[pair * 8 : pair * 8 + 8, :] = main
        lasts.append(last)
    slopes = [swap[pl.ds(place, 8, stride=8), :] for place in range(8)]
    sub = iota((8, 128), 0)
    final = jnp.zeros((8, 128), F32)
    for pair in range(8):
        final = jnp.where(sub == pair, jnp.broadcast_to(lasts[pair], (8, 128)), final)
    slopes.append(final)
    cameras = camera_arrays(cameras_ref)
    _, pullback = jax.vjp(lambda source: project(source, cameras), raw_rows(picked_ref))
    (raw_grads,) = pullback(slopes)
    for row in range(PARAMS):
        turned[pl.ds(row, 8, stride=ROWS), :] = raw_grads[row]
    for row in range(PARAMS, ROWS):
        turned[pl.ds(row, 8, stride=ROWS), :] = jnp.ones((8, 128), F32)
    for pair in range(4):
        onehot[:, pair * 256 : pair * 256 + 256] = seen_columns(ids_ref, pair * 4, 256)
    wide = jnp.concatenate([turned[pair * ROWS : pair * ROWS + ROWS, :] for pair in range(8)], axis=1)
    hot = onehot[...]
    summed = sum(mm(part, hot, ((1,), (1,))) for part in parts_of(wide, 3))
    grad = summed[0:PARAMS, :]
    seen = summed[PARAMS : PARAMS + 1, :] > 0.5
    first = first_ref[...]
    second = second_ref[...]
    params = params_ref[...]
    moved_first = beta_first * first + (1.0 - beta_first) * grad
    moved_second = beta_second * second + (1.0 - beta_second) * grad * grad
    moved_params = params - learn_rate * moved_first / (jnp.sqrt(moved_second) + adam_eps)
    new_first_ref[...] = jnp.where(seen, moved_first, first)
    new_second_ref[...] = jnp.where(seen, moved_second, second)
    new_params_ref[...] = jnp.where(seen, moved_params, params)


SMEM = pl.BlockSpec(memory_space=pltpu.SMEM)
VMEM = pl.BlockSpec(memory_space=pltpu.VMEM)


def f32_shape(*shape):
    return jax.ShapeDtypeStruct(shape, F32)


def project_call(visible, cameras, params):
    return pl.pallas_call(
        project_kernel,
        out_shape=(f32_shape(512, 128), f32_shape(16, 8, 128)),
        in_specs=[VMEM, SMEM, VMEM],
        out_specs=(VMEM, VMEM),
        scratch_shapes=[pltpu.VMEM((64, 128), F32)],
        name="project",
    )(visible, cameras, params)


def spread_call(arrived):
    return pl.pallas_call(
        spread_kernel,
        out_shape=f32_shape(16, 72, 128),
        in_specs=[VMEM],
        out_specs=VMEM,
        name="spread",
    )(arrived)


def render_call(place, counts, lists, targets, everyone):
    return pl.pallas_call(
        render_kernel,
        out_shape=(f32_shape(3, 512), f32_shape(16, 72, 128)),
        in_specs=[SMEM, SMEM, VMEM, VMEM, VMEM],
        out_specs=(VMEM, VMEM),
        scratch_shapes=[
            pltpu.VMEM((3, 576, 256), BF16),
            pltpu.VMEM((256, 2048), BF16),
            pltpu.VMEM((8, 2048), jnp.int32),
            pltpu.VMEM((16, 2048), F32),
            pltpu.VMEM((2, 1024, 256), F32),
            pltpu.VMEM((2, 1024, 256), F32),
            pltpu.VMEM((2, 1024, 256), F32),
            pltpu.VMEM((2, 576, 2048), BF16),
        ],
        name="render",
    )(place, counts, lists, targets, everyone)


def merge_call(arrived):
    return pl.pallas_call(
        merge_kernel,
        out_shape=f32_shape(16, 8, 128),
        in_specs=[VMEM],
        out_specs=VMEM,
        name="merge",
    )(arrived)


def update_call(visible, cameras, arrived, picked, params, first, second):
    shape = f32_shape(*params.shape)
    return pl.pallas_call(
        update_kernel,
        out_shape=(shape, shape, shape),
        in_specs=[VMEM, SMEM, VMEM, VMEM, VMEM, VMEM, VMEM],
        out_specs=(VMEM, VMEM, VMEM),
        scratch_shapes=[
            pltpu.VMEM((64, 128), F32),
            pltpu.VMEM((512, 128), F32),
            pltpu.VMEM((1024, 1024), BF16),
        ],
        name="update",
    )(visible, cameras, arrived, picked, params, first, second)


def shards(params, first, second, visible, cameras, tile_lists, tile_blocks, targets):
    picked, outgoing = project_call(visible, cameras, params)
    arrived = lax.all_to_all(outgoing, "view", 0, 0, tiled=True)
    everyone = lax.all_to_all(spread_call(arrived), "tile", 0, 0, tiled=True)
    place = lax.axis_index("tile").astype(jnp.int32).reshape(1)
    image, sums = render_call(
        place, tile_blocks, tile_lists.reshape(2, 8, 128), targets[0], everyone
    )
    back = lax.all_to_all(sums, "tile", 0, 0, tiled=True)
    returned = lax.all_to_all(merge_call(back), "view", 0, 0, tiled=True)
    new_params, new_first, new_second = update_call(
        visible, cameras, returned, picked, params, first, second
    )
    return (new_params, new_first, new_second, image[None])


def solution(mesh):
    in_specs = (
        P(None, ("view", "tile")),
        P(None, ("view", "tile")),
        P(None, ("view", "tile")),
        P(None, ("view", "tile")),
        P(),
        P("view", "tile", None),
        P("view", "tile"),
        P("view", None, "tile"),
    )
    out_specs = (
        P(None, ("view", "tile")),
        P(None, ("view", "tile")),
        P(None, ("view", "tile")),
        P("view", None, "tile"),
    )
    return jax.shard_map(shards, mesh=mesh, in_specs=in_specs, out_specs=out_specs, check_vma=False)
```

time: 201 us -> 94 us (0.47)
  other arithmetic: 44.8 us -> 0 us
  local copies, waits for them, and re-layouts: 44.3 us -> 3.33 us
  matrix products: 31.4 us -> 0 us
  Pallas kernels: 0 us -> 26.2 us
  blocking collectives: 17.2 us -> 33.1 us
  waiting for transfers between devices: 30.7 us -> 17.5 us
  loops' own time: 13.1 us -> 0 us
  starting transfers between devices: 17.4 us -> 12.5 us
    dot_general x80 -> x0, matrix products: 31.4 us -> none  [the longest x48 18.1 us: advance(): lax.dot_general(piece[6:9], weight, (((1,), (1,)), ((), ())), precision=l...]
    scatter-add x3 -> x0, other arithmetic: 28.9 us -> none  [the longest x1 15.2 us: shards(): jnp.zeros(everyone.shape, jnp.float32).at[:, lists.reshape(-1)].add(spread)]
    pallas_call x0 -> x5, Pallas kernels: none -> 26.2 us  [the longest x1 14.7 us: render_call(): pl.pallas_call(render_kernel, out_shape=(f32_shape(3, 512), f32_shape(16,...]
    all_to_all x1 -> x2, blocking collectives: 17.2 us -> 33.1 us  [the longest x1 17.8 us: shards(): arrived = lax.all_to_all(outgoing, 'view', 0, 0, tiled=True)]
    gather x4 -> x0, local copies, waits for them, and re-layouts: 15.4 us -> none  [the longest x2 12.4 us: one_tile(): rows = jnp.take(everyone, listed, axis=1)]
    all_to_all x3 -> x2, waiting for transfers between devices: 30.7 us -> 17.5 us  [the longest x1 10.3 us: shards(): everyone = lax.all_to_all(spread_call(arrived), 'tile', 0, 0, tiled=True)]
    another operation x1 -> x0, loops' own time: 13.1 us -> none  [shards(): lax.map(one_tile, (jnp.arange(per_device, dtype=jnp.int32), lists, counts...]
    reshape x7 -> x0, local copies, waits for them, and re-layouts: 9.16 us -> none  [the longest x1 6.15 us: split_up(): return jnp.moveaxis(array.reshape(*before, peers, -1, *after), dim, 0)]
  transfers between devices with their start and end apart: 3 -> 2, of which waited for: 3 -> 2; matrix products, arithmetic and copies ran while one was open for 4% -> 2% of each run, Pallas kernels for 0% -> 0%
where the time goes in v1:
time: 94 us; the launch traced here: 93.3 us
  blocking collectives  33.1 us (35%)
  Pallas kernels  26.2 us (28%)
  waiting for transfers between devices  17.5 us (19%)
  starting transfers between devices  12.5 us (13%)
  local copies, waits for them, and re-layouts  3.33 us (4%)
    all_to_all x1, blocking collectives, shards(): arrived = lax.all_to_all(outgoing, 'view', 0, 0, tiled=True)  17.8 us
    all_to_all x1, blocking collectives, shards(): back = lax.all_to_all(sums, 'tile', 0, 0, tiled=True)  15.3 us
    pallas_call x1, Pallas kernels, render_call(): pl.pallas_call(render_kernel, out_shape=(f32_shape(3, 512), f32_shape(16,...  14.7 us
    all_to_all x1, waiting for transfers between devices, shards(): everyone = lax.all_to_all(spread_call(arrived), 'tile', 0, 0, tiled=True)  10.3 us
    all_to_all x1, waiting for transfers between devices, shards(): returned = lax.all_to_all(merge_call(back), 'view', 0, 0, tiled=True)  7.22 us
    all_to_all x1, starting transfers between devices, shards(): everyone = lax.all_to_all(spread_call(arrived), 'tile', 0, 0, tiled=True)  6.89 us
    all_to_all x1, starting transfers between devices, shards(): returned = lax.all_to_all(merge_call(back), 'view', 0, 0, tiled=True)  5.57 us
    pallas_call x1, Pallas kernels, update_call(): pl.pallas_call(update_kernel, out_shape=(shape, shape, shape), in_specs=[...  4.67 us
  transfers between devices with their start and end apart: 2, of which 2 were waited for; matrix products, arithmetic and copies ran while one was open for 2% of the time, Pallas kernels for 0%

profile of v1, /device:TPU:1, one launch (start us, length us, event | category | flops | bytes accessed | tf_op | source)
XLA Modules:
  0.0 93.3 jit_solution(9586598653964804483)
XLA Ops:
  0.6 3.3 %project.1 = (f32[512,128]{1,0:T(8,128)}, f32[16,8,128]{2,1,0:T(8,128)}) custom-call(s32[16,64]{1,0:T(8,128)} %ids_ref.3, f32[16,11]{1,0:T(8,128)} %cameras_ref.3, f32[59,1024]{1,0:T(8,128)} %params_ref.3), custom_call_target="tpu_custom_call" | custom-call | tf_op jit(solution)/shard_map/project/pallas_call | solution.py:581
  3.9 17.8 %all_to_all.20.arrived_ref = f32[16,8,128]{2,1,0:T(8,128)} all-to-all(f32[16,8,128]{2,1,0:T(8,128)} %get-tuple-element.11), channel_id=1, replica_groups=mesh['view'=16,'tile'=16] {'view'}, dimensions={0} | all-to-all | bytes 131072 | tf_op jit(solution)/shard_map/all_to_all | solution.py:649
  21.7 1.8 %spread.1 = f32[16,72,128]{2,1,0:T(8,128)} custom-call(f32[16,8,128]{2,1,0:T(8,128)} %all_to_all.20.arrived_ref), custom_call_target="tpu_custom_call" | custom-call | tf_op jit(solution)/shard_map/spread/pallas_call | solution.py:592
  23.5 0.0 copy-start.3
  23.5 6.9 %all-to-all-start.1 = ((f32[16,72,128]{2,1,0:T(8,128)}), f32[16,72,128]{2,1,0:T(8,128)S(1)}, u32[]{:S(2)}, u32[]{:S(2)}) async-start(f32[16,72,128]{2,1,0:T(8,128)} %spread.1), calls=%async_computation.1 | async-start | bytes 1179648 | tf_op jit(solution)/shard_map/all_to_all | solution.py:650
  30.4 0.0 copy-done.3
  30.4 0.0 copy-start.4
  30.4 0.6 copy.17
  31.0 0.1 copy-done.4
  31.1 0.6 copy.18
  31.7 10.3 %all-to-all-done.1.everyone_ref = f32[16,72,128]{2,1,0:T(8,128)S(1)} async-done(((f32[16,72,128]{2,1,0:T(8,128)}), f32[16,72,128]{2,1,0:T(8,128)S(1)}, u32[]{:S(2)}, u32[]{:S(2)}) %all-to-all-start.1) | async-done | bytes 589856 | tf_op jit(solution)/shard_map/all_to_all | solution.py:650
  42.0 0.0 copy-start
  42.0 0.8 copy-done
  42.9 14.7 %render.1 = (f32[3,512]{1,0:T(4,128)}, f32[16,72,128]{2,1,0:T(8,128)}) custom-call(s32[1]{0:T(128)} %bitcast.place_ref, s32[1,2]{1,0:T(1,128)} %counts_ref.1, s32[2,8,128]{2,1,0:T(8,128)} %bitcast.11, f32[3,512]{1,0:T(4,128)} %bitcast.10, f32[16,72,128]{2,1,0:T(8,128)} %copy-done), custom_call_target="tpu_custom_call" | custom-call | tf_op jit(solution)/shard_map/render/pallas_call | solution.py:602
  57.6 15.3 %all_to_all.21.arrived_ref = f32[16,72,128]{2,1,0:T(8,128)} all-to-all(f32[16,72,128]{2,1,0:T(8,128)} %get-tuple-element.12), channel_id=1, replica_groups=mesh['view'=16,'tile'=16] {'tile'}, dimensions={0} | all-to-all | bytes 1179648 | tf_op jit(solution)/shard_map/all_to_all | solution.py:655
  72.8 1.8 %merge.1 = f32[16,8,128]{2,1,0:T(8,128)} custom-call(f32[16,72,128]{2,1,0:T(8,128)} %all_to_all.21.arrived_ref), custom_call_target="tpu_custom_call" | custom-call | tf_op jit(solution)/shard_map/merge/pallas_call | solution.py:622
  74.6 0.0 copy-start.2
  74.6 5.6 %all-to-all-start.3 = ((f32[16,8,128]{2,1,0:T(8,128)}), f32[16,8,128]{2,1,0:T(8,128)S(1)}, u32[]{:S(2)}, u32[]{:S(2)}) async-start(f32[16,8,128]{2,1,0:T(8,128)} %merge.1), calls=%async_computation.3 | async-start | bytes 131072 | tf_op jit(solution)/shard_map/all_to_all | solution.py:656
  80.2 0.0 copy-done.2
  80.2 0.6 copy.12
  80.8 7.2 %all-to-all-done.3.arrived_ref = f32[16,8,128]{2,1,0:T(8,128)S(1)} async-done(((f32[16,8,128]{2,1,0:T(8,128)}), f32[16,8,128]{2,1,0:T(8,128)S(1)}, u32[]{:S(2)}, u32[]{:S(2)}) %all-to-all-start.3) | async-done | bytes 65568 | tf_op jit(solution)/shard_map/all_to_all | solution.py:656
  88.0 0.0 copy-start.1
  88.0 0.6 copy-done.1
  88.7 4.7 %update.1 = (f32[59,1024]{1,0:T(8,128)}, f32[59,1024]{1,0:T(8,128)}, f32[59,1024]{1,0:T(8,128)}) custom-call(s32[16,64]{1,0:T(8,128)} %ids_ref.3, f32[16,11]{1,0:T(8,128)} %cameras_ref.3, f32[16,8,128]{2,1,0:T(8,128)} %copy-done.1, f32[512,128]{1,0:T(8,128)} %get-tuple-element.13.picked_ref, f32[59,1024]{1,0:T(8,128)} %params_ref.3, f32[59,1024]{1,0:T(8,128)} %first_ref.1, ...), custom_call_target="tpu_custom_call" | custom-call | tf_op jit(solution)/shard_map/update/pallas_call | solution.py:633
Async XLA Ops:
  23.5 6.9 %copy-start.3 = (s32[1,2,1024]{2,1,0:T(2,128)S(1)}, s32[1,2,1024]{2,1,0:T(2,128)}, u32[]{:S(2)}) copy-start(s32[1,2,1024]{2,1,0:T(2,128)} %param.13) | copy-start | bytes 24580
  23.5 18.5 %all-to-all-start.1 = ((f32[16,72,128]{2,1,0:T(8,128)}), f32[16,72,128]{2,1,0:T(8,128)S(1)}, u32[]{:S(2)}, u32[]{:S(2)}) async-start(f32[16,72,128]{2,1,0:T(8,128)} %spread.1), calls=%async_computation.1 | async-start | bytes 1179648 | tf_op jit(solution)/shard_map/all_to_all | solution.py:650
  30.4 0.7 copy-start.4
  42.0 0.8 copy-start
  74.6 5.6 %copy-start.2 = (f32[3,512]{1,0:T(4,128)S(1)}, f32[3,512]{1,0:T(4,128)}, u32[]{:S(2)}) copy-start(f32[3,512]{1,0:T(4,128)} %get-tuple-element.17) | copy-start | bytes 18436
  74.6 13.4 %all-to-all-start.3 = ((f32[16,8,128]{2,1,0:T(8,128)}), f32[16,8,128]{2,1,0:T(8,128)S(1)}, u32[]{:S(2)}, u32[]{:S(2)}) async-start(f32[16,8,128]{2,1,0:T(8,128)} %merge.1), calls=%async_computation.3 | async-start | bytes 131072 | tf_op jit(solution)/shard_map/all_to_all | solution.py:656
  88.0 0.6 copy-start.1

commit v2 on v1

--- a/solution.py
+++ b/solution.py
@@ -257,8 +257,8 @@
     everyone_ref,
     image_ref,
     out_ref,
-    table,
     onehot,
+    lanes_of,
     chosen,
     picked,
     alphas,
@@ -267,54 +267,48 @@
     scattered,
 ):
     count = 2048
-    width = 256
     turn = (iota((128, 1024), 0) == (iota((128, 1024), 1) >> 3)).astype(BF16)
     pick_block = iota((8, 1024), 0) == (iota((8, 1024), 1) & 7)
     for tile in range(2):
-        listed = lists_ref[tile]
-        low_part = mm((listed & 127).astype(F32).astype(BF16), turn, ((1,), (0,)))
-        high_part = mm((listed >> 7).astype(F32).astype(BF16), turn, ((1,), (0,)))
+        blocks = [lists_ref[0, tile : tile + 1, start : start + 128] for start in range(0, 1024, 128)]
+        low_part = stacked([(row & 127).astype(F32) for row in blocks], 128)
+        high_part = stacked([(row >> 7).astype(F32) for row in blocks], 128)
+        low_part = mm(low_part.astype(BF16), turn, ((1,), (0,)))
+        high_part = mm(high_part.astype(BF16), turn, ((1,), (0,)))
         low_row = jnp.sum(jnp.where(pick_block, low_part, 0.0), axis=0, keepdims=True)
         high_row = jnp.sum(jnp.where(pick_block, high_part, 0.0), axis=0, keepdims=True)
         low_row = low_row.astype(jnp.int32)
         high_row = high_row.astype(jnp.int32)
         lane_index = ((high_row >> 3) & 1) * 128 + low_row
-        group_index = (high_row >> 4) * 8 + (high_row & 7)
         span = slice(tile * 1024, tile * 1024 + 1024)
         onehot[:, span] = (iota((256, 1024), 0) == lane_index).astype(BF16)
-        chosen[:, span] = jnp.broadcast_to(group_index, (8, 1024))
-
-    for half in range(8):
-        for side in range(2):
-            lanes = slice(side * 128, side * 128 + 128)
-            main = parts_of(everyone_ref[2 * half + side, 0:64, :], 3)
-            last = parts_of(everyone_ref[2 * half + side, 64:72, :], 3)
-            for part in range(3):
-                table[part, half * 64 : half * 64 + 64, lanes] = main[part]
-                table[part, 512 + half * 8 : 520 + half * 8, lanes] = last[part]
+        lanes_of[:, span] = jnp.broadcast_to(low_row, (8, 1024))
+        chosen[:, span] = jnp.broadcast_to(high_row, (8, 1024))
 
     def gather_chunk(chunk, carry):
-        lanes = pl.ds(pl.multiple_of(chunk * width, width), width)
-        hot = onehot[:, lanes]
-        found = mm(table[0], hot, ((1,), (0,)))
-        found = found + mm(table[1], hot, ((1,), (0,)))
-        found = found + mm(table[2], hot, ((1,), (0,)))
+        lanes = pl.ds(pl.multiple_of(chunk * 128, 128), 128)
+        lane = lanes_of[:, lanes]
         group = chosen[:, lanes]
-        main = jnp.zeros((8, width), F32)
-        last = jnp.zeros((8, width), F32)
-        sub = iota((8, width), 0)
-        for half in range(8):
+        sub = iota((8, 128), 0)
+        zero = jnp.zeros((8, 128), F32)
+        main = [zero, zero, zero, zero]
+        last = [zero, zero]
+        for peer in range(16):
             for place in range(8):
-                start = half * 64 + place * 8
-                main = jnp.where(group == half * 8 + place, found[start : start + 8, :], main)
-            last = jnp.where(
-                group == half * 8 + sub, found[512 + half * 8 : 520 + half * 8, :], last
-            )
-        picked[0:8, lanes] = main
-        picked[8:16, lanes] = jnp.broadcast_to(jnp.sum(last, axis=0, keepdims=True), (8, width))
+                found = jnp.take_along_axis(
+                    everyone_ref[peer, place * 8 : place * 8 + 8, :], lane, axis=1
+                )
+                chain = place % 4
+                main[chain] = jnp.where(group == peer * 8 + place, found, main[chain])
+            found = jnp.take_along_axis(everyone_ref[peer, 64:72, :], lane, axis=1)
+            last[peer % 2] = jnp.where(group == peer * 8 + sub, found, last[peer % 2])
+        picked[0:8, lanes] = (main[0] + main[1]) + (main[2] + main[3])
+        picked[8:16, lanes] = jnp.broadcast_to(
+            jnp.sum(last[0] + last[1], axis=0, keepdims=True), (8, 128)
+        )
         return carry
 
-    lax.fori_loop(0, count // width, gather_chunk, 0)
+    lax.fori_loop(0, count // 128, gather_chunk, 0)
 
     pixel = iota((8, PIX), 1)
     pixel_x = (pixel & (SIDE - 1)).astype(F32) + (0.5 - SIDE / 2)
@@ -372,7 +366,7 @@
             for tile in range(2):
                 alpha = jnp.exp2(alphas[tile, pl.ds(start, 8), :])
                 weight = alpha * held[tile]
-                held[tile] = held[tile] - weight
+                held[tile] = held[tile] * (1.0 - alpha)
                 alphas[tile, pl.ds(start, 8), :] = alpha
                 weights[tile, pl.ds(start, 8), :] = weight
         return tuple(held)
@@ -408,8 +402,8 @@
             own = own + sums[24 + channel * 8 : 32 + channel * 8, :]
             image = jnp.sum(own * before, axis=0, keepdims=True)
             lanes = slice(tile * PIX, tile * PIX + PIX)
-            image_ref[channel : channel + 1, lanes] = image
-            slope = 2.0 * (image - targets_ref[channel : channel + 1, lanes])
+            image_ref[channel, :, lanes] = image
+            slope = 2.0 * (image - targets_ref[channel, :, lanes])
             slopes.append(slope)
             value = value + slope * own
         factor = passed
@@ -433,9 +427,9 @@
             for tile in range(2):
                 alpha = alphas[tile, pl.ds(start, 8), :]
                 weight = weights[tile, pl.ds(start, 8), :] * ahead[tile]
-                gap = shades[tile, pl.ds(start, 8), :] - held[tile]
-                held[tile] = held[tile] + alpha * gap
-                shades[tile, pl.ds(start, 8), :] = weight * gap
+                shade = shades[tile, pl.ds(start, 8), :]
+                shades[tile, pl.ds(start, 8), :] = weight * (shade - held[tile])
+                held[tile] = held[tile] * (1.0 - alpha) + alpha * shade
                 weights[tile, pl.ds(start, 8), :] = weight
         return tuple(held)
 
@@ -470,31 +464,31 @@
         picked[0:8, span] = stacked(grads, 1024)
         picked[8:16, span] = jnp.broadcast_to(tints[2:3, :], (8, 1024))
 
+    wide = 256
+
     def scatter_chunk(chunk, carry):
-        lanes = pl.ds(pl.multiple_of(chunk * width, width), width)
+        lanes = pl.ds(pl.multiple_of(chunk * wide, wide), wide)
         group = chosen[:, lanes]
-        sub = iota((8, width), 0)
+        group = (group >> 4) * 8 + (group & 7)
+        sub = iota((8, wide), 0)
         main = [part.astype(F32) for part in parts_of(picked[0:8, lanes], 2)]
         last = [part.astype(F32) for part in parts_of(picked[8:16, lanes], 2)]
-        for part in range(2):
-            for pair in range(32):
-                rows = jnp.concatenate(
-                    [jnp.where(group == 2 * pair + side, main[part], 0.0) for side in range(2)],
-                    axis=0,
-                )
-                scattered[part, pair * 16 : pair * 16 + 16, lanes] = rows.astype(BF16)
-            for pair in range(4):
-                rows = jnp.concatenate(
-                    [
-                        jnp.where(group == (2 * pair + side) * 8 + sub, last[part], 0.0)
+        for pair in range(36):
+            for part in range(2):
+                if pair < 32:
+                    rows = [
+                        jnp.where(group == 2 * pair + side, main[part], 0.0) for side in range(2)
+                    ]
+                else:
+                    rows = [
+                        jnp.where(group == (2 * pair - 64 + side) * 8 + sub, last[part], 0.0)
                         for side in range(2)
-                    ],
-                    axis=0,
-                )
-                scattered[part, 512 + pair * 16 : 528 + pair * 16, lanes] = rows.astype(BF16)
+                    ]
+                rows = jnp.concatenate(rows, axis=0).astype(BF16)
+                scattered[part, pair * 16 : pair * 16 + 16, lanes] = rows
         return carry
 
-    lax.fori_loop(0, count // width, scatter_chunk, 0)
+    lax.fori_loop(0, count // wide, scatter_chunk, 0)
     hot = onehot[...]
     summed = mm(scattered[0], hot, ((1,), (1,))) + mm(scattered[1], hot, ((1,), (1,)))
     for half in range(8):
@@ -601,12 +595,12 @@
 def render_call(place, counts, lists, targets, everyone):
     return pl.pallas_call(
         render_kernel,
-        out_shape=(f32_shape(3, 512), f32_shape(16, 72, 128)),
+        out_shape=(f32_shape(3, 1, 512), f32_shape(16, 72, 128)),
         in_specs=[SMEM, SMEM, VMEM, VMEM, VMEM],
         out_specs=(VMEM, VMEM),
         scratch_shapes=[
-            pltpu.VMEM((3, 576, 256), BF16),
             pltpu.VMEM((256, 2048), BF16),
+            pltpu.VMEM((8, 2048), jnp.int32),
             pltpu.VMEM((8, 2048), jnp.int32),
             pltpu.VMEM((16, 2048), F32),
             pltpu.VMEM((2, 1024, 256), F32),
@@ -644,20 +638,26 @@
     )(visible, cameras, arrived, picked, params, first, second)
 
 
+def kept(array):
+    return pltpu.with_memory_space_constraint(array, pltpu.VMEM)
+
+
+def exchanged(array, axis):
+    return kept(lax.all_to_all(array, axis, 0, 0, tiled=True))
+
+
 def shards(params, first, second, visible, cameras, tile_lists, tile_blocks, targets):
     picked, outgoing = project_call(visible, cameras, params)
-    arrived = lax.all_to_all(outgoing, "view", 0, 0, tiled=True)
-    everyone = lax.all_to_all(spread_call(arrived), "tile", 0, 0, tiled=True)
+    everyone = exchanged(spread_call(exchanged(outgoing, "view")), "tile")
     place = lax.axis_index("tile").astype(jnp.int32).reshape(1)
     image, sums = render_call(
-        place, tile_blocks, tile_lists.reshape(2, 8, 128), targets[0], everyone
+        place, tile_blocks, tile_lists, jnp.transpose(targets, (1, 0, 2)), everyone
     )
-    back = lax.all_to_all(sums, "tile", 0, 0, tiled=True)
-    returned = lax.all_to_all(merge_call(back), "view", 0, 0, tiled=True)
+    returned = exchanged(merge_call(exchanged(sums, "tile")), "view")
     new_params, new_first, new_second = update_call(
-        visible, cameras, returned, picked, params, first, second
+        visible, cameras, returned, kept(picked), kept(params), kept(first), kept(second)
     )
-    return (new_params, new_first, new_second, image[None])
+    return (new_params, new_first, new_second, jnp.transpose(image, (1, 0, 2)))
 
 
 def solution(mesh):

time: 94 us -> 89 us (0.947)
  blocking collectives: 33.1 us -> 45.7 us
  waiting for transfers between devices: 17.5 us -> 11.6 us
  starting transfers between devices: 12.5 us -> 6.76 us
  local copies, waits for them, and re-layouts: 3.33 us -> 0.01 us
  Pallas kernels: 26.2 us -> 23.7 us
    all_to_all x2 -> x3, blocking collectives: 33.1 us -> 45.7 us  [exchanged(): return kept(lax.all_to_all(array, axis, 0, 0, tiled=True))]
    all_to_all x2 -> x1, waiting for transfers between devices: 17.5 us -> 11.6 us  [exchanged(): return kept(lax.all_to_all(array, axis, 0, 0, tiled=True))]
    all_to_all x2 -> x1, starting transfers between devices: 12.5 us -> 6.76 us  [exchanged(): return kept(lax.all_to_all(array, axis, 0, 0, tiled=True))]
    unnamed x13 -> x8, local copies, waits for them, and re-layouts: 3.33 us -> 0.01 us
    pallas_call x1, Pallas kernels: 1.8 us -> 0.73 us  [merge_call(): pl.pallas_call(merge_kernel, out_shape=f32_shape(16, 8, 128), in_specs=[V...]
  transfers between devices with their start and end apart: 2 -> 1, of which waited for: 2 -> 1; matrix products, arithmetic and copies ran while one was open for 2% -> 0% of each run, Pallas kernels for 0% -> 0%
where the time goes in v2:
time: 89 us; the launch traced here: 88.5 us
  blocking collectives  45.7 us (51%)
  Pallas kernels  23.7 us (27%)
  waiting for transfers between devices  11.6 us (13%)
  starting transfers between devices  6.76 us (8%)
    all_to_all x3, blocking collectives, exchanged(): return kept(lax.all_to_all(array, axis, 0, 0, tiled=True))  45.7 us
    pallas_call x1, Pallas kernels, render_call(): pl.pallas_call(render_kernel, out_shape=(f32_shape(3, 1, 512), f32_shape(...  14.4 us
    all_to_all x1, waiting for transfers between devices, exchanged(): return kept(lax.all_to_all(array, axis, 0, 0, tiled=True))  11.6 us
    all_to_all x1, starting transfers between devices, exchanged(): return kept(lax.all_to_all(array, axis, 0, 0, tiled=True))  6.76 us
    pallas_call x1, Pallas kernels, update_call(): pl.pallas_call(update_kernel, out_shape=(shape, shape, shape), in_specs=[...  4.34 us
    pallas_call x1, Pallas kernels, project_call(): pl.pallas_call(project_kernel, out_shape=(f32_shape(512, 128), f32_shape(...  3.26 us
  transfers between devices with their start and end apart: 1, of which 1 were waited for; matrix products, arithmetic and copies ran while one was open for 0% of the time, Pallas kernels for 0%

profile of v2, /device:TPU:1, one launch (start us, length us, event | category | flops | bytes accessed | tf_op | source)
XLA Modules:
  0.0 88.5 jit_solution(7188581549917804489)
XLA Ops:
  0.6 3.3 %project.1 = (f32[512,128]{1,0:T(8,128)}, f32[16,8,128]{2,1,0:T(8,128)}) custom-call(s32[16,64]{1,0:T(8,128)} %ids_ref.3, f32[16,11]{1,0:T(8,128)} %cameras_ref.3, f32[59,1024]{1,0:T(8,128)} %params_ref.3), custom_call_target="tpu_custom_call" | custom-call | tf_op jit(solution)/shard_map/project/pallas_call | solution.py:575
  3.9 17.7 %all_to_all.20.arrived_ref = f32[16,8,128]{2,1,0:T(8,128)S(1)} all-to-all(f32[16,8,128]{2,1,0:T(8,128)} %get-tuple-element.11), channel_id=1, replica_groups=mesh['view'=16,'tile'=16] {'view'}, dimensions={0} | all-to-all | bytes 131072 | tf_op jit(solution)/shard_map/all_to_all | solution.py:646
  21.6 1.0 %spread.1 = f32[16,72,128]{2,1,0:T(8,128)} custom-call(f32[16,8,128]{2,1,0:T(8,128)S(1)} %all_to_all.20.arrived_ref), custom_call_target="tpu_custom_call" | custom-call | tf_op jit(solution)/shard_map/spread/pallas_call | solution.py:586
  22.6 6.8 %all-to-all-start.1 = ((f32[16,72,128]{2,1,0:T(8,128)}), f32[16,72,128]{2,1,0:T(8,128)S(1)}, u32[]{:S(2)}, u32[]{:S(2)}) async-start(f32[16,72,128]{2,1,0:T(8,128)} %spread.1), calls=%async_computation.1 | async-start | bytes 1179648 | tf_op jit(solution)/shard_map/all_to_all | solution.py:646
  29.3 11.6 %all-to-all-done.1.everyone_ref = f32[16,72,128]{2,1,0:T(8,128)S(1)} async-done(((f32[16,72,128]{2,1,0:T(8,128)}), f32[16,72,128]{2,1,0:T(8,128)S(1)}, u32[]{:S(2)}, u32[]{:S(2)}) %all-to-all-start.1) | async-done | bytes 589856 | tf_op jit(solution)/shard_map/all_to_all | solution.py:646
  41.0 14.4 %render.1 = (f32[3,1,512]{2,1,0:T(1,128)}, f32[16,72,128]{2,1,0:T(8,128)}) custom-call(s32[1]{0:T(128)} %bitcast.place_ref, s32[1,2]{1,0:T(1,128)} %counts_ref.1, s32[1,2,1024]{2,1,0:T(2,128)} %lists_ref.1, f32[3,1,512]{2,1,0:T(1,128)} %bitcast.3, f32[16,72,128]{2,1,0:T(8,128)S(1)} %all-to-all-done.1.everyone_ref), custom_call_target="tpu_custom_call" | custom-call | tf_op jit(solution)/shard_map/render/pallas_call | solution.py:596
  55.4 0.0 copy-start.3
  55.4 14.7 %all_to_all.21.arrived_ref = f32[16,72,128]{2,1,0:T(8,128)S(1)} all-to-all(f32[16,72,128]{2,1,0:T(8,128)} %get-tuple-element.12), channel_id=1, replica_groups=mesh['view'=16,'tile'=16] {'tile'}, dimensions={0} | all-to-all | bytes 1179648 | tf_op jit(solution)/shard_map/all_to_all | solution.py:646
  70.1 0.0 copy-start
  70.1 0.0 copy-start.1
  70.1 0.0 copy-start.2
  70.1 0.7 merge.1
  70.8 13.2 %all_to_all.22.arrived_ref = f32[16,8,128]{2,1,0:T(8,128)S(1)} all-to-all(f32[16,8,128]{2,1,0:T(8,128)} %merge.1), channel_id=1, replica_groups=mesh['view'=16,'tile'=16] {'view'}, dimensions={0} | all-to-all | bytes 131072 | tf_op jit(solution)/shard_map/all_to_all | solution.py:646
  84.1 0.0 copy-done.3
  84.1 0.0 copy-done
  84.1 0.0 copy-done.1
  84.1 0.0 copy-done.2
  84.1 4.3 %update.1 = (f32[59,1024]{1,0:T(8,128)}, f32[59,1024]{1,0:T(8,128)}, f32[59,1024]{1,0:T(8,128)}) custom-call(s32[16,64]{1,0:T(8,128)} %ids_ref.3, f32[16,11]{1,0:T(8,128)} %cameras_ref.3, f32[16,8,128]{2,1,0:T(8,128)S(1)} %all_to_all.22.arrived_ref, f32[512,128]{1,0:T(8,128)S(1)} %copy-done.3, f32[59,1024]{1,0:T(8,128)S(1)} %copy-done, ...), custom_call_target="tpu_custom_call" | custom-call | tf_op jit(solution)/shard_map/update/pallas_call | solution.py:627
Async XLA Ops:
  22.6 18.4 %all-to-all-start.1 = ((f32[16,72,128]{2,1,0:T(8,128)}), f32[16,72,128]{2,1,0:T(8,128)S(1)}, u32[]{:S(2)}, u32[]{:S(2)}) async-start(f32[16,72,128]{2,1,0:T(8,128)} %spread.1), calls=%async_computation.1 | async-start | bytes 1179648 | tf_op jit(solution)/shard_map/all_to_all | solution.py:646
  55.4 28.7 %copy-start.3 = (f32[512,128]{1,0:T(8,128)S(1)}, f32[512,128]{1,0:T(8,128)}, u32[]{:S(2)}) copy-start(f32[512,128]{1,0:T(8,128)} %get-tuple-element.13.picked_ref) | copy-start | bytes 786436
  70.1 14.0 %copy-start = (f32[59,1024]{1,0:T(8,128)S(1)}, f32[59,1024]{1,0:T(8,128)}, u32[]{:S(2)}) copy-start(f32[59,1024]{1,0:T(8,128)} %params_ref.3) | copy-start | bytes 724996
  70.1 14.0 %copy-start.1 = (f32[59,1024]{1,0:T(8,128)S(1)}, f32[59,1024]{1,0:T(8,128)}, u32[]{:S(2)}) copy-start(f32[59,1024]{1,0:T(8,128)} %first_ref.1) | copy-start | bytes 724996
  70.1 14.0 %copy-start.2 = (f32[59,1024]{1,0:T(8,128)S(1)}, f32[59,1024]{1,0:T(8,128)}, u32[]{:S(2)}) copy-start(f32[59,1024]{1,0:T(8,128)} %second_ref.1) | copy-start | bytes 724996

commit v3 on v2

--- a/solution.py
+++ b/solution.py
@@ -215,14 +215,15 @@
     return [picked_ref[pl.ds(row, 8, stride=ROWS), :] for row in range(PARAMS)]
 
 
-def project_kernel(ids_ref, cameras_ref, params_ref, picked_ref, send_ref, swap):
-    params = params_ref[...]
-    split = parts_of(params, 3)
+def project_kernel(ids_ref, cameras_ref, params_ref, picked_ref, send_ref, split, swap):
+    for place, part in enumerate(parts_of(params_ref[...], 3)):
+        split[place * ROWS : place * ROWS + PARAMS, :] = part
     for pair in range(4):
         onehot = seen_columns(ids_ref, pair * 4, 256)
-        picked = sum(mm(part, onehot, ((1,), (0,))) for part in split)
-        picked_ref[pair * 128 : pair * 128 + PARAMS, :] = picked[:, :128]
-        picked_ref[pair * 128 + 64 : pair * 128 + 64 + PARAMS, :] = picked[:, 128:]
+        three = mm(split[...], onehot, ((1,), (0,)))
+        picked = three[0:ROWS] + three[ROWS : 2 * ROWS] + three[2 * ROWS :]
+        picked_ref[pair * 128 : pair * 128 + ROWS, :] = picked[:, :128]
+        picked_ref[pair * 128 + ROWS : pair * 128 + 2 * ROWS, :] = picked[:, 128:]
     values = project(raw_rows(picked_ref), camera_arrays(cameras_ref))
     for place in range(8):
         swap[place * 8 : place * 8 + 8, :] = values[place]
@@ -249,24 +250,9 @@
             out_ref[peer, 64 + pair : 65 + pair, :] = last
 
 
-def render_kernel(
-    place_ref,
-    counts_ref,
-    lists_ref,
-    targets_ref,
-    everyone_ref,
-    image_ref,
-    out_ref,
-    onehot,
-    lanes_of,
-    chosen,
-    picked,
-    alphas,
-    weights,
-    shades,
-    scattered,
-):
-    count = 2048
+def prepare_kernel(after_ref, ids_ref, lists_ref, columns_ref, onehot_ref, lanes_ref, groups_ref):
+    for pair in range(4):
+        columns_ref[:, pair * 256 : pair * 256 + 256] = seen_columns(ids_ref, pair * 4, 256)
     turn = (iota((128, 1024), 0) == (iota((128, 1024), 1) >> 3)).astype(BF16)
     pick_block = iota((8, 1024), 0) == (iota((8, 1024), 1) & 7)
     for tile in range(2):
@@ -281,10 +267,28 @@
         high_row = high_row.astype(jnp.int32)
         lane_index = ((high_row >> 3) & 1) * 128 + low_row
         span = slice(tile * 1024, tile * 1024 + 1024)
-        onehot[:, span] = (iota((256, 1024), 0) == lane_index).astype(BF16)
-        lanes_of[:, span] = jnp.broadcast_to(low_row, (8, 1024))
-        chosen[:, span] = jnp.broadcast_to(high_row, (8, 1024))
-
+        onehot_ref[:, span] = (iota((256, 1024), 0) == lane_index).astype(BF16)
+        lanes_ref[:, span] = jnp.broadcast_to(low_row, (8, 1024))
+        groups_ref[:, span] = jnp.broadcast_to(high_row, (8, 1024))
+
+
+def render_kernel(
+    place_ref,
+    counts_ref,
+    onehot,
+    lanes_of,
+    chosen,
+    targets_ref,
+    everyone_ref,
+    image_ref,
+    out_ref,
+    picked,
+    alphas,
+    weights,
+    shades,
+    summed,
+):
+    count = 2048
     def gather_chunk(chunk, carry):
         lanes = pl.ds(pl.multiple_of(chunk * 128, 128), 128)
         lane = lanes_of[:, lanes]
@@ -464,40 +468,36 @@
         picked[0:8, span] = stacked(grads, 1024)
         picked[8:16, span] = jnp.broadcast_to(tints[2:3, :], (8, 1024))
 
-    wide = 256
-
-    def scatter_chunk(chunk, carry):
-        lanes = pl.ds(pl.multiple_of(chunk * wide, wide), wide)
+    wide = 512
+    for chunk in range(count // wide):
+        lanes = slice(chunk * wide, chunk * wide + wide)
         group = chosen[:, lanes]
         group = (group >> 4) * 8 + (group & 7)
         sub = iota((8, wide), 0)
+        hot = onehot[:, lanes]
         main = [part.astype(F32) for part in parts_of(picked[0:8, lanes], 2)]
         last = [part.astype(F32) for part in parts_of(picked[8:16, lanes], 2)]
-        for pair in range(36):
-            for part in range(2):
-                if pair < 32:
-                    rows = [
-                        jnp.where(group == 2 * pair + side, main[part], 0.0) for side in range(2)
-                    ]
-                else:
-                    rows = [
-                        jnp.where(group == (2 * pair - 64 + side) * 8 + sub, last[part], 0.0)
-                        for side in range(2)
-                    ]
-                rows = jnp.concatenate(rows, axis=0).astype(BF16)
-                scattered[part, pair * 16 : pair * 16 + 16, lanes] = rows
-        return carry
-
-    lax.fori_loop(0, count // wide, scatter_chunk, 0)
-    hot = onehot[...]
-    summed = mm(scattered[0], hot, ((1,), (1,))) + mm(scattered[1], hot, ((1,), (1,)))
+        total = None
+        for part in range(2):
+            rows = [jnp.where(group == place, main[part], 0.0) for place in range(64)]
+            rows += [jnp.where(group == half * 8 + sub, last[part], 0.0) for half in range(8)]
+            rows = [
+                jnp.concatenate(rows[place : place + 2], axis=0).astype(BF16)
+                for place in range(0, 72, 2)
+            ]
+            product = mm(jnp.concatenate(rows, axis=0), hot, ((1,), (1,)))
+            total = product if total is None else total + product
+        if chunk == 0:
+            summed[...] = total
+        elif chunk < count // wide - 1:
+            summed[...] = summed[...] + total
+        else:
+            total = summed[...] + total
     for half in range(8):
         for side in range(2):
             lanes = slice(side * 128, side * 128 + 128)
-            out_ref[2 * half + side, 0:64, :] = summed[half * 64 : half * 64 + 64, lanes]
-            out_ref[2 * half + side, 64:72, :] = summed[
-                512 + half * 8 : 520 + half * 8, lanes
-            ]
+            out_ref[2 * half + side, 0:64, :] = total[half * 64 : half * 64 + 64, lanes]
+            out_ref[2 * half + side, 64:72, :] = total[512 + half * 8 : 520 + half * 8, lanes]
 
 
 def merge_kernel(arrived_ref, send_ref):
@@ -513,7 +513,7 @@
 
 
 def update_kernel(
-    ids_ref,
+    onehot_ref,
     cameras_ref,
     arrived_ref,
     picked_ref,
@@ -525,7 +525,6 @@
     new_second_ref,
     swap,
     turned,
-    onehot,
 ):
     lasts = []
     for pair in range(8):
@@ -545,11 +544,10 @@
         turned[pl.ds(row, 8, stride=ROWS), :] = raw_grads[row]
     for row in range(PARAMS, ROWS):
         turned[pl.ds(row, 8, stride=ROWS), :] = jnp.ones((8, 128), F32)
-    for pair in range(4):
-        onehot[:, pair * 256 : pair * 256 + 256] = seen_columns(ids_ref, pair * 4, 256)
     wide = jnp.concatenate([turned[pair * ROWS : pair * ROWS + ROWS, :] for pair in range(8)], axis=1)
-    hot = onehot[...]
-    summed = sum(mm(part, hot, ((1,), (1,))) for part in parts_of(wide, 3))
+    split = [part.astype(F32) for part in parts_of(wide, 3)]
+    three = mm(jnp.concatenate(split, axis=0).astype(BF16), onehot_ref[...], ((1,), (1,)))
+    summed = three[0:ROWS] + three[ROWS : 2 * ROWS] + three[2 * ROWS :]
     grad = summed[0:PARAMS, :]
     seen = summed[PARAMS : PARAMS + 1, :] > 0.5
     first = first_ref[...]
@@ -577,7 +575,7 @@
         out_shape=(f32_shape(512, 128), f32_shape(16, 8, 128)),
         in_specs=[VMEM, SMEM, VMEM],
         out_specs=(VMEM, VMEM),
-        scratch_shapes=[pltpu.VMEM((64, 128), F32)],
+        scratch_shapes=[pltpu.VMEM((192, 1024), BF16), pltpu.VMEM((64, 128), F32)],
         name="project",
     )(visible, cameras, params)
 
@@ -592,24 +590,36 @@
     )(arrived)
 
 
-def render_call(place, counts, lists, targets, everyone):
+def prepare_call(after, visible, lists):
+    return pl.pallas_call(
+        prepare_kernel,
+        out_shape=(
+            jax.ShapeDtypeStruct((1024, 1024), BF16),
+            jax.ShapeDtypeStruct((256, 2048), BF16),
+            jax.ShapeDtypeStruct((8, 2048), jnp.int32),
+            jax.ShapeDtypeStruct((8, 2048), jnp.int32),
+        ),
+        in_specs=[pl.BlockSpec(memory_space=pl.ANY), VMEM, VMEM],
+        out_specs=(VMEM, VMEM, VMEM, VMEM),
+        name="prepare",
+    )(after, visible, lists)
+
+
+def render_call(place, counts, onehot, lanes, groups, targets, everyone):
     return pl.pallas_call(
         render_kernel,
         out_shape=(f32_shape(3, 1, 512), f32_shape(16, 72, 128)),
-        in_specs=[SMEM, SMEM, VMEM, VMEM, VMEM],
+        in_specs=[SMEM, SMEM, VMEM, VMEM, VMEM, VMEM, VMEM],
         out_specs=(VMEM, VMEM),
         scratch_shapes=[
-            pltpu.VMEM((256, 2048), BF16),
-            pltpu.VMEM((8, 2048), jnp.int32),
-            pltpu.VMEM((8, 2048), jnp.int32),
             pltpu.VMEM((16, 2048), F32),
             pltpu.VMEM((2, 1024, 256), F32),
             pltpu.VMEM((2, 1024, 256), F32),
             pltpu.VMEM((2, 1024, 256), F32),
-            pltpu.VMEM((2, 576, 2048), BF16),
+            pltpu.VMEM((576, 256), F32),
         ],
         name="render",
-    )(place, counts, lists, targets, everyone)
+    )(place, counts, onehot, lanes, groups, targets, everyone)
 
 
 def merge_call(arrived):
@@ -622,7 +632,7 @@
     )(arrived)
 
 
-def update_call(visible, cameras, arrived, picked, params, first, second):
+def update_call(onehot, cameras, arrived, picked, params, first, second):
     shape = f32_shape(*params.shape)
     return pl.pallas_call(
         update_kernel,
@@ -632,10 +642,9 @@
         scratch_shapes=[
             pltpu.VMEM((64, 128), F32),
             pltpu.VMEM((512, 128), F32),
-            pltpu.VMEM((1024, 1024), BF16),
         ],
         name="update",
-    )(visible, cameras, arrived, picked, params, first, second)
+    )(onehot, cameras, arrived, picked, params, first, second)
 
 
 def kept(array):
@@ -648,14 +657,24 @@
 
 def shards(params, first, second, visible, cameras, tile_lists, tile_blocks, targets):
     picked, outgoing = project_call(visible, cameras, params)
-    everyone = exchanged(spread_call(exchanged(outgoing, "view")), "tile")
+    block = spread_call(exchanged(outgoing, "view"))
+    everyone = exchanged(block, "tile")
+    columns, onehot, lanes, groups = [
+        kept(table) for table in prepare_call(block, visible, tile_lists)
+    ]
     place = lax.axis_index("tile").astype(jnp.int32).reshape(1)
     image, sums = render_call(
-        place, tile_blocks, tile_lists, jnp.transpose(targets, (1, 0, 2)), everyone
+        place,
+        tile_blocks,
+        onehot,
+        lanes,
+        groups,
+        jnp.transpose(targets, (1, 0, 2)),
+        everyone,
     )
     returned = exchanged(merge_call(exchanged(sums, "tile")), "view")
     new_params, new_first, new_second = update_call(
-        visible, cameras, returned, kept(picked), kept(params), kept(first), kept(second)
+        columns, cameras, returned, kept(picked), kept(params), kept(first), kept(second)
     )
     return (new_params, new_first, new_second, jnp.transpose(image, (1, 0, 2)))
 

time: 89 us -> 91.3 us (1.026)
  local copies, waits for them, and re-layouts: 0.01 us -> 5.45 us
  waiting for transfers between devices: 11.6 us -> 7.88 us
    unnamed x8 -> x16, local copies, waits for them, and re-layouts: 0.01 us -> 5.45 us
    all_to_all x1, waiting for transfers between devices: 11.6 us -> 7.88 us  [exchanged(): return kept(lax.all_to_all(array, axis, 0, 0, tiled=True))]
    pallas_call x0 -> x1, Pallas kernels: none -> 3.73 us  [prepare_call(): pl.pallas_call(prepare_kernel, out_shape=(jax.ShapeDtypeStruct((1024, 102...]
    pallas_call x1, Pallas kernels: 14.4 us -> 13 us  [render_call(): pl.pallas_call(render_kernel, out_shape=(f32_shape(3, 1, 512), f32_shape(...]
    pallas_call x1, Pallas kernels: 4.34 us -> 3.08 us  [update_call(): pl.pallas_call(update_kernel, out_shape=(shape, shape, shape), in_specs=[...]
  transfers between devices with their start and end apart: 1 -> 1, of which waited for: 1 -> 1; matrix products, arithmetic and copies ran while one was open for 0% -> 0% of each run, Pallas kernels for 0% -> 4%
where the time goes in v3:
time: 91.3 us; the launch traced here: 90.5 us
  blocking collectives  45.6 us (50%)
  Pallas kernels  24.1 us (26%)
  waiting for transfers between devices  7.88 us (9%)
  starting transfers between devices  6.89 us (8%)
  local copies, waits for them, and re-layouts  5.45 us (6%)
    all_to_all x3, blocking collectives, exchanged(): return kept(lax.all_to_all(array, axis, 0, 0, tiled=True))  45.6 us
    pallas_call x1, Pallas kernels, render_call(): pl.pallas_call(render_kernel, out_shape=(f32_shape(3, 1, 512), f32_shape(...  13 us
    all_to_all x1, waiting for transfers between devices, exchanged(): return kept(lax.all_to_all(array, axis, 0, 0, tiled=True))  7.88 us
    all_to_all x1, starting transfers between devices, exchanged(): return kept(lax.all_to_all(array, axis, 0, 0, tiled=True))  6.89 us
    unnamed x16, local copies, waits for them, and re-layouts  5.45 us
    pallas_call x1, Pallas kernels, prepare_call(): pl.pallas_call(prepare_kernel, out_shape=(jax.ShapeDtypeStruct((1024, 102...  3.73 us
    pallas_call x1, Pallas kernels, update_call(): pl.pallas_call(update_kernel, out_shape=(shape, shape, shape), in_specs=[...  3.08 us
    pallas_call x1, Pallas kernels, project_call(): pl.pallas_call(project_kernel, out_shape=(f32_shape(512, 128), f32_shape(...  2.6 us
  transfers between devices with their start and end apart: 1, of which 1 were waited for; matrix products, arithmetic and copies ran while one was open for 0% of the time, Pallas kernels for 4%

profile of v3, /device:TPU:1, one launch (start us, length us, event | category | flops | bytes accessed | tf_op | source)
XLA Modules:
  0.0 90.5 jit_solution(815563250732634726)
XLA Ops:
  0.6 2.6 %project.1 = (f32[512,128]{1,0:T(8,128)}, f32[16,8,128]{2,1,0:T(8,128)}) custom-call(s32[16,64]{1,0:T(8,128)} %ids_ref.3, f32[16,11]{1,0:T(8,128)} %cameras_ref.3, f32[59,1024]{1,0:T(8,128)} %params_ref.3), custom_call_target="tpu_custom_call" | custom-call | tf_op jit(solution)/shard_map/project/pallas_call | solution.py:573
  3.2 17.7 %all_to_all.20.arrived_ref = f32[16,8,128]{2,1,0:T(8,128)S(1)} all-to-all(f32[16,8,128]{2,1,0:T(8,128)} %get-tuple-element.15), channel_id=1, replica_groups=mesh['view'=16,'tile'=16] {'view'}, dimensions={0} | all-to-all | bytes 131072 | tf_op jit(solution)/shard_map/all_to_all | solution.py:655
  21.0 0.9 %spread.1.after_ref = f32[16,72,128]{2,1,0:T(8,128)} custom-call(f32[16,8,128]{2,1,0:T(8,128)S(1)} %all_to_all.20.arrived_ref), custom_call_target="tpu_custom_call" | custom-call | tf_op jit(solution)/shard_map/spread/pallas_call | solution.py:584
  21.9 0.0 copy-start.4
  21.9 6.9 %all-to-all-start.1 = ((f32[16,72,128]{2,1,0:T(8,128)}), f32[16,72,128]{2,1,0:T(8,128)S(1)}, u32[]{:S(2)}, u32[]{:S(2)}) async-start(f32[16,72,128]{2,1,0:T(8,128)} %spread.1.after_ref), calls=%async_computation.1 | async-start | bytes 1179648 | tf_op jit(solution)/shard_map/all_to_all | solution.py:655
  28.8 0.0 copy-start.1
  28.8 0.0 copy-start.3
  28.8 3.7 %prepare.1 = (bf16[1024,1024]{1,0:T(8,128)(2,1)}, bf16[256,2048]{1,0:T(8,128)(2,1)}, s32[8,2048]{1,0:T(8,128)}, s32[8,2048]{1,0:T(8,128)}) custom-call(f32[16,72,128]{2,1,0:T(8,128)} %spread.1.after_ref, s32[16,64]{1,0:T(8,128)} %ids_ref.3, s32[1,2,1024]{2,1,0:T(2,128)} %lists_ref.1), custom_call_target="tpu_custom_call" | custom-call | tf_op jit(solution)/shard_map/prepare/pallas_call | solution.py:594
  32.6 7.9 %all-to-all-done.1.everyone_ref = f32[16,72,128]{2,1,0:T(8,128)S(1)} async-done(((f32[16,72,128]{2,1,0:T(8,128)}), f32[16,72,128]{2,1,0:T(8,128)S(1)}, u32[]{:S(2)}, u32[]{:S(2)}) %all-to-all-start.1) | async-done | bytes 589856 | tf_op jit(solution)/shard_map/all_to_all | solution.py:655
  40.5 0.0 copy-start.2
  40.5 1.2 %copy-done.2 = bf16[256,2048]{1,0:T(8,128)(2,1)S(1)} copy-done((bf16[256,2048]{1,0:T(8,128)(2,1)S(1)}, bf16[256,2048]{1,0:T(8,128)(2,1)}, u32[]{:S(2)}) %copy-start.2) | copy-done | bytes 1048600
  41.7 0.0 copy-start.6
  41.7 0.8 copy-done.6
  42.5 0.0 copy-start.7
  42.5 0.8 copy-done.7
  43.4 13.0 %render.1 = (f32[3,1,512]{2,1,0:T(1,128)}, f32[16,72,128]{2,1,0:T(8,128)}) custom-call(s32[1]{0:T(128)} %bitcast.place_ref, s32[1,2]{1,0:T(1,128)} %counts_ref.1, bf16[256,2048]{1,0:T(8,128)(2,1)S(1)} %copy-done.2, s32[8,2048]{1,0:T(8,128)S(1)} %copy-done.6, s32[8,2048]{1,0:T(8,128)S(1)} %copy-done.7, f32[3,1,512]{2,1,0:T(1,128)} %bitcast.3, ...), custom_call_target="tpu_custom_call" | custom-call | tf_op jit(solution)/shard_map/render/pallas_call | solution.py:609
  56.3 14.6 %all_to_all.21.arrived_ref = f32[16,72,128]{2,1,0:T(8,128)S(1)} all-to-all(f32[16,72,128]{2,1,0:T(8,128)} %get-tuple-element.20), channel_id=1, replica_groups=mesh['view'=16,'tile'=16] {'tile'}, dimensions={0} | all-to-all | bytes 1179648 | tf_op jit(solution)/shard_map/all_to_all | solution.py:655
  70.9 0.7 merge.1
  71.6 13.2 %all_to_all.22.arrived_ref = f32[16,8,128]{2,1,0:T(8,128)S(1)} all-to-all(f32[16,8,128]{2,1,0:T(8,128)} %merge.1), channel_id=1, replica_groups=mesh['view'=16,'tile'=16] {'view'}, dimensions={0} | all-to-all | bytes 131072 | tf_op jit(solution)/shard_map/all_to_all | solution.py:655
  84.9 0.0 copy-done.4
  84.9 0.0 copy-done.1
  84.9 0.0 copy-done.3
  84.9 0.0 copy-start
  84.9 1.6 %copy-done = bf16[1024,1024]{1,0:T(8,128)(2,1)S(1)} copy-done((bf16[1024,1024]{1,0:T(8,128)(2,1)S(1)}, bf16[1024,1024]{1,0:T(8,128)(2,1)}, u32[]{:S(2)}) %copy-start) | copy-done | bytes 2097176
  86.5 0.0 copy-start.5
  86.5 0.9 %copy-done.5 = f32[512,128]{1,0:T(8,128)S(1)} copy-done((f32[512,128]{1,0:T(8,128)S(1)}, f32[512,128]{1,0:T(8,128)}, u32[]{:S(2)}) %copy-start.5) | copy-done | bytes 262168
  87.4 3.1 %update.1 = (f32[59,1024]{1,0:T(8,128)}, f32[59,1024]{1,0:T(8,128)}, f32[59,1024]{1,0:T(8,128)}) custom-call(bf16[1024,1024]{1,0:T(8,128)(2,1)S(1)} %copy-done, f32[16,11]{1,0:T(8,128)} %cameras_ref.3, f32[16,8,128]{2,1,0:T(8,128)S(1)} %all_to_all.22.arrived_ref, f32[512,128]{1,0:T(8,128)S(1)} %copy-done.5, f32[59,1024]{1,0:T(8,128)S(1)} %copy-done.1, ...), custom_call_target="tpu_custom_call" | custom-call | tf_op jit(solution)/shard_map/update/pallas_call | solution.py:637
Async XLA Ops:
  21.9 63.0 %copy-start.4 = (f32[59,1024]{1,0:T(8,128)S(1)}, f32[59,1024]{1,0:T(8,128)}, u32[]{:S(2)}) copy-start(f32[59,1024]{1,0:T(8,128)} %second_ref.1) | copy-start | bytes 724996
  21.9 18.5 %all-to-all-start.1 = ((f32[16,72,128]{2,1,0:T(8,128)}), f32[16,72,128]{2,1,0:T(8,128)S(1)}, u32[]{:S(2)}, u32[]{:S(2)}) async-start(f32[16,72,128]{2,1,0:T(8,128)} %spread.1.after_ref), calls=%async_computation.1 | async-start | bytes 1179648 | tf_op jit(solution)/shard_map/all_to_all | solution.py:655
  28.8 56.1 %copy-start.1 = (f32[59,1024]{1,0:T(8,128)S(1)}, f32[59,1024]{1,0:T(8,128)}, u32[]{:S(2)}) copy-start(f32[59,1024]{1,0:T(8,128)} %params_ref.3) | copy-start | bytes 724996
  28.8 56.1 %copy-start.3 = (f32[59,1024]{1,0:T(8,128)S(1)}, f32[59,1024]{1,0:T(8,128)}, u32[]{:S(2)}) copy-start(f32[59,1024]{1,0:T(8,128)} %first_ref.1) | copy-start | bytes 724996
  40.5 1.2 %copy-start.2 = (bf16[256,2048]{1,0:T(8,128)(2,1)S(1)}, bf16[256,2048]{1,0:T(8,128)(2,1)}, u32[]{:S(2)}) copy-start(bf16[256,2048]{1,0:T(8,128)(2,1)} %get-tuple-element.17.onehot) | copy-start | bytes 3145732
  41.7 0.8 copy-start.6
  42.5 0.8 copy-start.7
  84.9 1.6 %copy-start = (bf16[1024,1024]{1,0:T(8,128)(2,1)S(1)}, bf16[1024,1024]{1,0:T(8,128)(2,1)}, u32[]{:S(2)}) copy-start(bf16[1024,1024]{1,0:T(8,128)(2,1)} %get-tuple-element.16.onehot_ref) | copy-start | bytes 6291460
  86.5 0.9 %copy-start.5 = (f32[512,128]{1,0:T(8,128)S(1)}, f32[512,128]{1,0:T(8,128)}, u32[]{:S(2)}) copy-start(f32[512,128]{1,0:T(8,128)} %get-tuple-element.21.picked_ref) | copy-start | bytes 786436

commit v4 on v3

--- a/solution.py
+++ b/solution.py
@@ -165,6 +165,7 @@
 PARAMS = 59
 ROWS = 64
 LOG2E = 1.4426950408889634
+MIB = 1 << 20
 
 
 def iota(shape, dim):
@@ -250,9 +251,12 @@
             out_ref[peer, 64 + pair : 65 + pair, :] = last
 
 
-def prepare_kernel(after_ref, ids_ref, lists_ref, columns_ref, onehot_ref, lanes_ref, groups_ref):
+def columns_kernel(after_ref, ids_ref, columns_ref):
     for pair in range(4):
         columns_ref[:, pair * 256 : pair * 256 + 256] = seen_columns(ids_ref, pair * 4, 256)
+
+
+def prepare_kernel(after_ref, lists_ref, onehot_ref, lanes_ref, groups_ref):
     turn = (iota((128, 1024), 0) == (iota((128, 1024), 1) >> 3)).astype(BF16)
     pick_block = iota((8, 1024), 0) == (iota((8, 1024), 1) & 7)
     for tile in range(2):
@@ -268,8 +272,8 @@
         lane_index = ((high_row >> 3) & 1) * 128 + low_row
         span = slice(tile * 1024, tile * 1024 + 1024)
         onehot_ref[:, span] = (iota((256, 1024), 0) == lane_index).astype(BF16)
-        lanes_ref[:, span] = jnp.broadcast_to(low_row, (8, 1024))
-        groups_ref[:, span] = jnp.broadcast_to(high_row, (8, 1024))
+        lanes_ref[:, span] = low_row
+        groups_ref[:, span] = high_row
 
 
 def render_kernel(
@@ -291,8 +295,8 @@
     count = 2048
     def gather_chunk(chunk, carry):
         lanes = pl.ds(pl.multiple_of(chunk * 128, 128), 128)
-        lane = lanes_of[:, lanes]
-        group = chosen[:, lanes]
+        lane = jnp.broadcast_to(lanes_of[:, lanes], (8, 128))
+        group = jnp.broadcast_to(chosen[:, lanes], (8, 128))
         sub = iota((8, 128), 0)
         zero = jnp.zeros((8, 128), F32)
         main = [zero, zero, zero, zero]
@@ -472,7 +476,7 @@
     for chunk in range(count // wide):
         lanes = slice(chunk * wide, chunk * wide + wide)
         group = chosen[:, lanes]
-        group = (group >> 4) * 8 + (group & 7)
+        group = jnp.broadcast_to((group >> 4) * 8 + (group & 7), (8, wide))
         sub = iota((8, wide), 0)
         hot = onehot[:, lanes]
         main = [part.astype(F32) for part in parts_of(picked[0:8, lanes], 2)]
@@ -576,6 +580,7 @@
         in_specs=[VMEM, SMEM, VMEM],
         out_specs=(VMEM, VMEM),
         scratch_shapes=[pltpu.VMEM((192, 1024), BF16), pltpu.VMEM((64, 128), F32)],
+        compiler_params=pltpu.CompilerParams(vmem_limit_bytes=12 * MIB),
         name="project",
     )(visible, cameras, params)
 
@@ -586,23 +591,35 @@
         out_shape=f32_shape(16, 72, 128),
         in_specs=[VMEM],
         out_specs=VMEM,
+        compiler_params=pltpu.CompilerParams(vmem_limit_bytes=6 * MIB),
         name="spread",
     )(arrived)
 
 
-def prepare_call(after, visible, lists):
+def columns_call(after, visible):
+    return pl.pallas_call(
+        columns_kernel,
+        out_shape=jax.ShapeDtypeStruct((1024, 1024), BF16),
+        in_specs=[pl.BlockSpec(memory_space=pl.ANY), VMEM],
+        out_specs=VMEM,
+        compiler_params=pltpu.CompilerParams(vmem_limit_bytes=8 * MIB),
+        name="columns",
+    )(after, visible)
+
+
+def prepare_call(after, lists):
     return pl.pallas_call(
         prepare_kernel,
         out_shape=(
-            jax.ShapeDtypeStruct((1024, 1024), BF16),
             jax.ShapeDtypeStruct((256, 2048), BF16),
-            jax.ShapeDtypeStruct((8, 2048), jnp.int32),
-            jax.ShapeDtypeStruct((8, 2048), jnp.int32),
+            jax.ShapeDtypeStruct((1, 2048), jnp.int32),
+            jax.ShapeDtypeStruct((1, 2048), jnp.int32),
         ),
-        in_specs=[pl.BlockSpec(memory_space=pl.ANY), VMEM, VMEM],
-        out_specs=(VMEM, VMEM, VMEM, VMEM),
+        in_specs=[pl.BlockSpec(memory_space=pl.ANY), VMEM],
+        out_specs=(VMEM, VMEM, VMEM),
+        compiler_params=pltpu.CompilerParams(vmem_limit_bytes=16 * MIB),
         name="prepare",
-    )(after, visible, lists)
+    )(after, lists)
 
 
 def render_call(place, counts, onehot, lanes, groups, targets, everyone):
@@ -618,6 +635,7 @@
             pltpu.VMEM((2, 1024, 256), F32),
             pltpu.VMEM((576, 256), F32),
         ],
+        compiler_params=pltpu.CompilerParams(vmem_limit_bytes=24 * MIB),
         name="render",
     )(place, counts, onehot, lanes, groups, targets, everyone)
 
@@ -628,6 +646,7 @@
         out_shape=f32_shape(16, 8, 128),
         in_specs=[VMEM],
         out_specs=VMEM,
+        compiler_params=pltpu.CompilerParams(vmem_limit_bytes=6 * MIB),
         name="merge",
     )(arrived)
 
@@ -643,6 +662,7 @@
             pltpu.VMEM((64, 128), F32),
             pltpu.VMEM((512, 128), F32),
         ],
+        compiler_params=pltpu.CompilerParams(vmem_limit_bytes=16 * MIB),
         name="update",
     )(onehot, cameras, arrived, picked, params, first, second)
 
@@ -659,9 +679,7 @@
     picked, outgoing = project_call(visible, cameras, params)
     block = spread_call(exchanged(outgoing, "view"))
     everyone = exchanged(block, "tile")
-    columns, onehot, lanes, groups = [
-        kept(table) for table in prepare_call(block, visible, tile_lists)
-    ]
+    onehot, lanes, groups = [kept(table) for table in prepare_call(block, tile_lists)]
     place = lax.axis_index("tile").astype(jnp.int32).reshape(1)
     image, sums = render_call(
         place,
@@ -672,7 +690,9 @@
         jnp.transpose(targets, (1, 0, 2)),
         everyone,
     )
-    returned = exchanged(merge_call(exchanged(sums, "tile")), "view")
+    merged = merge_call(exchanged(sums, "tile"))
+    returned = exchanged(merged, "view")
+    columns = kept(columns_call(merged, visible))
     new_params, new_first, new_second = update_call(
         columns, cameras, returned, kept(picked), kept(params), kept(first), kept(second)
     )

time: 91.3 us -> 85.3 us (0.934)
  blocking collectives: 45.6 us -> 31.9 us
  waiting for transfers between devices: 7.88 us -> 17.7 us
  starting transfers between devices: 6.89 us -> 12.2 us
  Pallas kernels: 24.1 us -> 19.9 us
  local copies, waits for them, and re-layouts: 5.45 us -> 2.38 us
    all_to_all x3 -> x2, blocking collectives: 45.6 us -> 31.9 us  [exchanged(): return kept(lax.all_to_all(array, axis, 0, 0, tiled=True))]
    all_to_all x1 -> x2, waiting for transfers between devices: 7.88 us -> 17.7 us  [exchanged(): return kept(lax.all_to_all(array, axis, 0, 0, tiled=True))]
    all_to_all x1 -> x2, starting transfers between devices: 6.89 us -> 12.2 us  [exchanged(): return kept(lax.all_to_all(array, axis, 0, 0, tiled=True))]
    unnamed x16 -> x22, local copies, waits for them, and re-layouts: 5.45 us -> 2.38 us
    pallas_call x1 -> x2, Pallas kernels: 3.73 us -> 1.68 us  [the longest x1 1.05 us: columns_call(): pl.pallas_call(columns_kernel, out_shape=jax.ShapeDtypeStruct((1024, 1024...]
    pallas_call x1, Pallas kernels: 13 us -> 12 us  [render_call(): pl.pallas_call(render_kernel, out_shape=(f32_shape(3, 1, 512), f32_shape(...]
    pallas_call x1, Pallas kernels: 2.6 us -> 1.64 us  [project_call(): pl.pallas_call(project_kernel, out_shape=(f32_shape(512, 128), f32_shape(...]
  transfers between devices with their start and end apart: 1 -> 2, of which waited for: 1 -> 2; matrix products, arithmetic and copies ran while one was open for 0% -> 0% of each run, Pallas kernels for 4% -> 2%
where the time goes in v4:
time: 85.3 us; the launch traced here: 84.9 us
  blocking collectives  31.9 us (37%)
  Pallas kernels  19.9 us (23%)
  waiting for transfers between devices  17.7 us (21%)
  starting transfers between devices  12.2 us (14%)
  local copies, waits for them, and re-layouts  2.38 us (3%)
    all_to_all x2, blocking collectives, exchanged(): return kept(lax.all_to_all(array, axis, 0, 0, tiled=True))  31.9 us
    all_to_all x2, waiting for transfers between devices, exchanged(): return kept(lax.all_to_all(array, axis, 0, 0, tiled=True))  17.7 us
    all_to_all x2, starting transfers between devices, exchanged(): return kept(lax.all_to_all(array, axis, 0, 0, tiled=True))  12.2 us
    pallas_call x1, Pallas kernels, render_call(): pl.pallas_call(render_kernel, out_shape=(f32_shape(3, 1, 512), f32_shape(...  12 us
    pallas_call x1, Pallas kernels, update_call(): pl.pallas_call(update_kernel, out_shape=(shape, shape, shape), in_specs=[...  2.95 us
    unnamed x22, local copies, waits for them, and re-layouts  2.38 us
  transfers between devices with their start and end apart: 2, of which 2 were waited for; matrix products, arithmetic and copies ran while one was open for 0% of the time, Pallas kernels for 2%

profile of v4, /device:TPU:1, one launch (start us, length us, event | category | flops | bytes accessed | tf_op | source)
XLA Modules:
  0.0 84.9 jit_solution(14793742698024821831)
XLA Ops:
  0.6 0.0 copy-start
  0.6 0.9 %copy-done = f32[59,1024]{1,0:T(8,128)S(1)} copy-done((f32[59,1024]{1,0:T(8,128)S(1)}, f32[59,1024]{1,0:T(8,128)}, u32[]{:S(2)}) %copy-start) | copy-done | bytes 241688
  1.6 0.0 copy-start.4
  1.6 0.7 copy-done.4
  2.3 0.0 copy-start.6
  2.3 0.7 copy-done.6
  3.0 0.0 copy-start.8
  3.0 0.0 copy-start.9
  3.0 0.0 copy-start.10
  3.0 1.6 %project.1 = (f32[512,128]{1,0:T(8,128)S(1)}, f32[16,8,128]{2,1,0:T(8,128)S(1)}) custom-call(s32[16,64]{1,0:T(8,128)S(1)} %copy-done.4, f32[16,11]{1,0:T(8,128)S(1)} %copy-done.6, f32[59,1024]{1,0:T(8,128)S(1)} %copy-done), custom_call_target="tpu_custom_call" | custom-call | tf_op jit(solution)/shard_map/project/pallas_call | solution.py:577
  4.6 17.5 %all_to_all.20.arrived_ref = f32[16,8,128]{2,1,0:T(8,128)S(1)} all-to-all(f32[16,8,128]{2,1,0:T(8,128)S(1)} %get-tuple-element.14), channel_id=1, replica_groups=mesh['view'=16,'tile'=16] {'view'}, dimensions={0} | all-to-all | bytes 131072 | tf_op jit(solution)/shard_map/all_to_all | solution.py:675
  22.2 1.0 %spread.1.after_ref = f32[16,72,128]{2,1,0:T(8,128)} custom-call(f32[16,8,128]{2,1,0:T(8,128)S(1)} %all_to_all.20.arrived_ref), custom_call_target="tpu_custom_call" | custom-call | tf_op jit(solution)/shard_map/spread/pallas_call | solution.py:589
  23.1 6.8 %all-to-all-start.1 = ((f32[16,72,128]{2,1,0:T(8,128)}), f32[16,72,128]{2,1,0:T(8,128)S(1)}, u32[]{:S(2)}, u32[]{:S(2)}) async-start(f32[16,72,128]{2,1,0:T(8,128)} %spread.1.after_ref), calls=%async_computation.1 | async-start | bytes 1179648 | tf_op jit(solution)/shard_map/all_to_all | solution.py:675
  29.9 0.0 copy-done.8
  29.9 0.0 copy-start.5
  29.9 0.6 prepare.1
  30.6 11.0 %all-to-all-done.1.everyone_ref = f32[16,72,128]{2,1,0:T(8,128)S(1)} async-done(((f32[16,72,128]{2,1,0:T(8,128)}), f32[16,72,128]{2,1,0:T(8,128)S(1)}, u32[]{:S(2)}, u32[]{:S(2)}) %all-to-all-start.1) | async-done | bytes 589856 | tf_op jit(solution)/shard_map/all_to_all | solution.py:675
  41.5 0.0 copy-done.9
  41.5 0.0 copy-done.10
  41.5 12.0 %render.1 = (f32[3,1,512]{2,1,0:T(1,128)}, f32[16,72,128]{2,1,0:T(8,128)S(1)}) custom-call(s32[1]{0:T(128)} %bitcast.place_ref, s32[1,2]{1,0:T(1,128)S(1)} %copy-done.10, bf16[256,2048]{1,0:T(8,128)(2,1)S(1)} %get-tuple-element.15.onehot, s32[1,2048]{1,0:T(1,128)S(1)} %get-tuple-element.16.lanes_of, s32[1,2048]{1,0:T(1,128)S(1)} %get-tuple-element.17.chosen, ...), custom_call_target="tpu_custom_call" | custom-call | tf_op jit(solution)/shard_map/render/pallas_call | solution.py:626
  53.5 0.0 copy-start.1
  53.5 0.0 copy-start.2
  53.5 0.0 copy-start.3
  53.5 0.0 copy-start.7
  53.6 14.4 %all_to_all.21.arrived_ref = f32[16,72,128]{2,1,0:T(8,128)S(1)} all-to-all(f32[16,72,128]{2,1,0:T(8,128)S(1)} %get-tuple-element.18), channel_id=1, replica_groups=mesh['view'=16,'tile'=16] {'tile'}, dimensions={0} | all-to-all | bytes 1179648 | tf_op jit(solution)/shard_map/all_to_all | solution.py:675
  67.9 0.7 merge.1.after_ref
  68.7 5.4 %all-to-all-start.3 = ((f32[16,8,128]{2,1,0:T(8,128)}), f32[16,8,128]{2,1,0:T(8,128)S(1)}, u32[]{:S(2)}, u32[]{:S(2)}) async-start(f32[16,8,128]{2,1,0:T(8,128)} %merge.1.after_ref), calls=%async_computation.3 | async-start | bytes 131072 | tf_op jit(solution)/shard_map/all_to_all | solution.py:675
  74.1 0.0 copy-done.5
  74.1 1.1 %columns.1.onehot_ref = bf16[1024,1024]{1,0:T(8,128)(2,1)S(1)} custom-call(f32[16,8,128]{2,1,0:T(8,128)} %merge.1.after_ref, s32[16,64]{1,0:T(8,128)S(1)} %copy-done.5), custom_call_target="tpu_custom_call" | custom-call | tf_op jit(solution)/shard_map/columns/pallas_call | solution.py:600
  75.1 6.8 %all-to-all-done.3.arrived_ref = f32[16,8,128]{2,1,0:T(8,128)S(1)} async-done(((f32[16,8,128]{2,1,0:T(8,128)}), f32[16,8,128]{2,1,0:T(8,128)S(1)}, u32[]{:S(2)}, u32[]{:S(2)}) %all-to-all-start.3) | async-done | bytes 65568 | tf_op jit(solution)/shard_map/all_to_all | solution.py:675
  81.9 0.0 copy-done.1
  81.9 0.0 copy-done.2
  81.9 0.0 copy-done.3
  81.9 0.0 copy-done.7
  81.9 2.9 %update.1 = (f32[59,1024]{1,0:T(8,128)}, f32[59,1024]{1,0:T(8,128)}, f32[59,1024]{1,0:T(8,128)}) custom-call(bf16[1024,1024]{1,0:T(8,128)(2,1)S(1)} %columns.1.onehot_ref, f32[16,11]{1,0:T(8,128)S(1)} %copy-done.7, f32[16,8,128]{2,1,0:T(8,128)S(1)} %all-to-all-done.3.arrived_ref, f32[512,128]{1,0:T(8,128)S(1)} %get-tuple-element.19.picked_ref, ...), custom_call_target="tpu_custom_call" | custom-call | tf_op jit(solution)/shard_map/update/pallas_call | solution.py:656
Async XLA Ops:
  0.6 1.0 %copy-start = (f32[59,1024]{1,0:T(8,128)S(1)}, f32[59,1024]{1,0:T(8,128)}, u32[]{:S(2)}) copy-start(f32[59,1024]{1,0:T(8,128)} %params_ref.3) | copy-start | bytes 724996
  1.6 0.7 copy-start.4
  2.3 0.7 copy-start.6
  3.0 26.9 %copy-start.8 = (s32[1,2,1024]{2,1,0:T(2,128)S(1)}, s32[1,2,1024]{2,1,0:T(2,128)}, u32[]{:S(2)}) copy-start(s32[1,2,1024]{2,1,0:T(2,128)} %lists_ref.1) | copy-start | bytes 24580
  3.0 38.6 %copy-start.9 = (f32[1,3,512]{2,0,1:T(1,128)S(1)}, f32[1,3,512]{2,0,1:T(1,128)}, u32[]{:S(2)}) copy-start(f32[1,3,512]{2,0,1:T(1,128)} %param.15) | copy-start | bytes 18436
  3.0 38.6 %copy-start.10 = (s32[1,2]{1,0:T(1,128)S(1)}, s32[1,2]{1,0:T(1,128)}, u32[]{:S(2)}) copy-start(s32[1,2]{1,0:T(1,128)} %counts_ref.1) | copy-start | bytes 28
  23.1 18.4 %all-to-all-start.1 = ((f32[16,72,128]{2,1,0:T(8,128)}), f32[16,72,128]{2,1,0:T(8,128)S(1)}, u32[]{:S(2)}, u32[]{:S(2)}) async-start(f32[16,72,128]{2,1,0:T(8,128)} %spread.1.after_ref), calls=%async_computation.1 | async-start | bytes 1179648 | tf_op jit(solution)/shard_map/all_to_all | solution.py:675
  29.9 44.2 %copy-start.5 = (s32[16,64]{1,0:T(8,128)S(1)}, s32[16,64]{1,0:T(8,128)}, u32[]{:S(2)}) copy-start(s32[16,64]{1,0:T(8,128)} %ids_ref.3) | copy-start | bytes 12292
  53.5 28.4 %copy-start.1 = (f32[59,1024]{1,0:T(8,128)S(1)}, f32[59,1024]{1,0:T(8,128)}, u32[]{:S(2)}) copy-start(f32[59,1024]{1,0:T(8,128)} %params_ref.3) | copy-start | bytes 724996
  53.5 28.4 %copy-start.2 = (f32[59,1024]{1,0:T(8,128)S(1)}, f32[59,1024]{1,0:T(8,128)}, u32[]{:S(2)}) copy-start(f32[59,1024]{1,0:T(8,128)} %first_ref.1) | copy-start | bytes 724996
  53.5 28.4 %copy-start.3 = (f32[59,1024]{1,0:T(8,128)S(1)}, f32[59,1024]{1,0:T(8,128)}, u32[]{:S(2)}) copy-start(f32[59,1024]{1,0:T(8,128)} %second_ref.1) | copy-start | bytes 724996
  53.5 28.4 %copy-start.7 = (f32[16,11]{1,0:T(8,128)S(1)}, f32[16,11]{1,0:T(8,128)}, u32[]{:S(2)}) copy-start(f32[16,11]{1,0:T(8,128)} %cameras_ref.3) | copy-start | bytes 2116
  68.7 13.2 %all-to-all-start.3 = ((f32[16,8,128]{2,1,0:T(8,128)}), f32[16,8,128]{2,1,0:T(8,128)S(1)}, u32[]{:S(2)}, u32[]{:S(2)}) async-start(f32[16,8,128]{2,1,0:T(8,128)} %merge.1.after_ref), calls=%async_computation.3 | async-start | bytes 131072 | tf_op jit(solution)/shard_map/all_to_all | solution.py:675

commit v5 on v4

--- a/solution.py
+++ b/solution.py
@@ -166,6 +166,7 @@
 ROWS = 64
 LOG2E = 1.4426950408889634
 MIB = 1 << 20
+MIXED = 8
 
 
 def iota(shape, dim):
@@ -291,32 +292,65 @@
     weights,
     shades,
     summed,
+    table,
 ):
     count = 2048
+    for half in range(MIXED // 2):
+        for side in range(2):
+            lanes = slice(side * 128, side * 128 + 128)
+            main = parts_of(everyone_ref[2 * half + side, 0:64, :], 3)
+            last = parts_of(everyone_ref[2 * half + side, 64:72, :], 3)
+            for part in range(3):
+                table[part, half * 64 : half * 64 + 64, lanes] = main[part]
+                start = MIXED * 32 + half * 8
+                table[part, start : start + 8, lanes] = last[part]
+
     def gather_chunk(chunk, carry):
-        lanes = pl.ds(pl.multiple_of(chunk * 128, 128), 128)
-        lane = jnp.broadcast_to(lanes_of[:, lanes], (8, 128))
-        group = jnp.broadcast_to(chosen[:, lanes], (8, 128))
+        lanes = pl.ds(pl.multiple_of(chunk * 256, 256), 256)
+        hot = onehot[:, lanes]
+        found = mm(table[0], hot, ((1,), (0,)))
+        found = found + mm(table[1], hot, ((1,), (0,)))
+        found = found + mm(table[2], hot, ((1,), (0,)))
+        both = jnp.broadcast_to(chosen[:, lanes], (8, 256))
+        pair = (both >> 4) * 8 + (both & 7)
+        sub = iota((8, 256), 0)
+        zero = jnp.zeros((8, 256), F32)
+        main = [zero, zero]
+        last = zero
+        for half in range(MIXED // 2):
+            for place in range(8):
+                start = half * 64 + place * 8
+                main[place % 2] = jnp.where(
+                    pair == half * 8 + place, found[start : start + 8, :], main[place % 2]
+                )
+            start = MIXED * 32 + half * 8
+            last = jnp.where(pair == half * 8 + sub, found[start : start + 8, :], last)
+        main = main[0] + main[1]
         sub = iota((8, 128), 0)
         zero = jnp.zeros((8, 128), F32)
-        main = [zero, zero, zero, zero]
-        last = [zero, zero]
-        for peer in range(16):
-            for place in range(8):
-                found = jnp.take_along_axis(
-                    everyone_ref[peer, place * 8 : place * 8 + 8, :], lane, axis=1
-                )
-                chain = place % 4
-                main[chain] = jnp.where(group == peer * 8 + place, found, main[chain])
-            found = jnp.take_along_axis(everyone_ref[peer, 64:72, :], lane, axis=1)
-            last[peer % 2] = jnp.where(group == peer * 8 + sub, found, last[peer % 2])
-        picked[0:8, lanes] = (main[0] + main[1]) + (main[2] + main[3])
-        picked[8:16, lanes] = jnp.broadcast_to(
-            jnp.sum(last[0] + last[1], axis=0, keepdims=True), (8, 128)
-        )
+        for side in range(2):
+            cut = slice(side * 128, side * 128 + 128)
+            lanes = pl.ds(pl.multiple_of(chunk * 256 + side * 128, 128), 128)
+            lane = jnp.broadcast_to(lanes_of[:, lanes], (8, 128))
+            group = both[:, cut]
+            chains = [main[:, cut], zero, zero, zero]
+            ends = [last[:, cut], zero]
+            for peer in range(MIXED, 16):
+                for place in range(8):
+                    value = jnp.take_along_axis(
+                        everyone_ref[peer, place * 8 : place * 8 + 8, :], lane, axis=1
+                    )
+                    chain = place % 4
+                    chains[chain] = jnp.where(group == peer * 8 + place, value, chains[chain])
+                value = jnp.take_along_axis(everyone_ref[peer, 64:72, :], lane, axis=1)
+                ends[peer % 2] = jnp.where(group == peer * 8 + sub, value, ends[peer % 2])
+            picked[0:8, lanes] = (chains[0] + chains[1]) + (chains[2] + chains[3])
+            picked[8:16, lanes] = jnp.broadcast_to(
+                jnp.sum(ends[0] + ends[1], axis=0, keepdims=True), (8, 128)
+            )
         return carry
 
-    lax.fori_loop(0, count // 128, gather_chunk, 0)
+    lax.fori_loop(0, count // 256, gather_chunk, 0)
 
     pixel = iota((8, PIX), 1)
     pixel_x = (pixel & (SIDE - 1)).astype(F32) + (0.5 - SIDE / 2)
@@ -375,7 +409,6 @@
                 alpha = jnp.exp2(alphas[tile, pl.ds(start, 8), :])
                 weight = alpha * held[tile]
                 held[tile] = held[tile] * (1.0 - alpha)
-                alphas[tile, pl.ds(start, 8), :] = alpha
                 weights[tile, pl.ds(start, 8), :] = weight
         return tuple(held)
 
@@ -433,7 +466,7 @@
         for inner in range(steps):
             start = pl.multiple_of((127 - (outer * steps + inner)) * 8, 8)
             for tile in range(2):
-                alpha = alphas[tile, pl.ds(start, 8), :]
+                alpha = jnp.exp2(alphas[tile, pl.ds(start, 8), :])
                 weight = weights[tile, pl.ds(start, 8), :] * ahead[tile]
                 shade = shades[tile, pl.ds(start, 8), :]
                 shades[tile, pl.ds(start, 8), :] = weight * (shade - held[tile])
@@ -529,6 +562,8 @@
     new_second_ref,
     swap,
     turned,
+    stage,
+    leaving,
 ):
     lasts = []
     for pair in range(8):
@@ -552,17 +587,32 @@
     split = [part.astype(F32) for part in parts_of(wide, 3)]
     three = mm(jnp.concatenate(split, axis=0).astype(BF16), onehot_ref[...], ((1,), (1,)))
     summed = three[0:ROWS] + three[ROWS : 2 * ROWS] + three[2 * ROWS :]
-    grad = summed[0:PARAMS, :]
     seen = summed[PARAMS : PARAMS + 1, :] > 0.5
-    first = first_ref[...]
-    second = second_ref[...]
-    params = params_ref[...]
-    moved_first = beta_first * first + (1.0 - beta_first) * grad
-    moved_second = beta_second * second + (1.0 - beta_second) * grad * grad
-    moved_params = params - learn_rate * moved_first / (jnp.sqrt(moved_second) + adam_eps)
-    new_first_ref[...] = jnp.where(seen, moved_first, first)
-    new_second_ref[...] = jnp.where(seen, moved_second, second)
-    new_params_ref[...] = jnp.where(seen, moved_params, params)
+    outs = (new_params_ref, new_first_ref, new_second_ref)
+    copies = []
+    for place, start in enumerate(range(0, PARAMS, 16)):
+        rows = slice(start, min(start + 16, PARAMS))
+        grad = summed[rows, :]
+        first = first_ref[rows, :]
+        second = second_ref[rows, :]
+        params = params_ref[rows, :]
+        moved_first = beta_first * first + (1.0 - beta_first) * grad
+        moved_second = beta_second * second + (1.0 - beta_second) * grad * grad
+        moved_params = params - learn_rate * moved_first / (jnp.sqrt(moved_second) + adam_eps)
+        values = (
+            jnp.where(seen, moved_params, params),
+            jnp.where(seen, moved_first, first),
+            jnp.where(seen, moved_second, second),
+        )
+        for kind in range(3):
+            stage[kind, rows, :] = values[kind]
+            copy = pltpu.make_async_copy(
+                stage.at[kind, rows, :], outs[kind].at[rows, :], leaving.at[kind, place]
+            )
+            copy.start()
+            copies.append(copy)
+    for copy in copies:
+        copy.wait()
 
 
 SMEM = pl.BlockSpec(memory_space=pltpu.SMEM)
@@ -634,6 +684,7 @@
             pltpu.VMEM((2, 1024, 256), F32),
             pltpu.VMEM((2, 1024, 256), F32),
             pltpu.VMEM((576, 256), F32),
+            pltpu.VMEM((3, MIXED * 36, 256), BF16),
         ],
         compiler_params=pltpu.CompilerParams(vmem_limit_bytes=24 * MIB),
         name="render",
@@ -657,10 +708,12 @@
         update_kernel,
         out_shape=(shape, shape, shape),
         in_specs=[VMEM, SMEM, VMEM, VMEM, VMEM, VMEM, VMEM],
-        out_specs=(VMEM, VMEM, VMEM),
+        out_specs=(pl.BlockSpec(memory_space=pl.ANY),) * 3,
         scratch_shapes=[
             pltpu.VMEM((64, 128), F32),
             pltpu.VMEM((512, 128), F32),
+            pltpu.VMEM((3, PARAMS, 1024), F32),
+            pltpu.SemaphoreType.DMA((3, 4)),
         ],
         compiler_params=pltpu.CompilerParams(vmem_limit_bytes=16 * MIB),
         name="update",
@@ -676,7 +729,9 @@
 
 
 def shards(params, first, second, visible, cameras, tile_lists, tile_blocks, targets):
-    picked, outgoing = project_call(visible, cameras, params)
+    picked, outgoing = project_call(
+        *[pltpu.with_memory_space_constraint(array, pltpu.HBM) for array in (visible, cameras, params)]
+    )
     block = spread_call(exchanged(outgoing, "view"))
     everyone = exchanged(block, "tile")
     onehot, lanes, groups = [kept(table) for table in prepare_call(block, tile_lists)]

time: 85.3 us -> 81.6 us (0.957)
  local copies, waits for them, and re-layouts: 2.38 us -> 0.04 us
  Pallas kernels: 19.9 us -> 18.6 us
    unnamed x22 -> x16, local copies, waits for them, and re-layouts: 2.38 us -> 0.04 us
    pallas_call x1, Pallas kernels: 12 us -> 10.2 us  [render_call(): pl.pallas_call(render_kernel, out_shape=(f32_shape(3, 1, 512), f32_shape(...]
where the time goes in v5:
time: 81.6 us; the launch traced here: 81.2 us
  blocking collectives  31.9 us (39%)
  Pallas kernels  18.6 us (23%)
  waiting for transfers between devices  17.7 us (22%)
  starting transfers between devices  12.2 us (15%)
    all_to_all x2, blocking collectives, exchanged(): return kept(lax.all_to_all(array, axis, 0, 0, tiled=True))  31.9 us
    all_to_all x2, waiting for transfers between devices, exchanged(): return kept(lax.all_to_all(array, axis, 0, 0, tiled=True))  17.7 us
    all_to_all x2, starting transfers between devices, exchanged(): return kept(lax.all_to_all(array, axis, 0, 0, tiled=True))  12.2 us
    pallas_call x1, Pallas kernels, render_call(): pl.pallas_call(render_kernel, out_shape=(f32_shape(3, 1, 512), f32_shape(...  10.2 us
    pallas_call x1, Pallas kernels, update_call(): pl.pallas_call(update_kernel, out_shape=(shape, shape, shape), in_specs=[...  3 us
    pallas_call x1, Pallas kernels, project_call(): pl.pallas_call(project_kernel, out_shape=(f32_shape(512, 128), f32_shape(...  1.98 us
  transfers between devices with their start and end apart: 2, of which 2 were waited for; matrix products, arithmetic and copies ran while one was open for 0% of the time, Pallas kernels for 2%

profile of v5, /device:TPU:1, one launch (start us, length us, event | category | flops | bytes accessed | tf_op | source)
XLA Modules:
  0.0 81.2 jit_solution(15459382185803357034)
XLA Ops:
  0.6 0.0 copy-start.5
  0.6 0.0 copy-start.6
  0.7 0.0 copy-start.7
  0.7 2.0 %project.1 = (f32[512,128]{1,0:T(8,128)S(1)}, f32[16,8,128]{2,1,0:T(8,128)S(1)}) custom-call(s32[16,64]{1,0:T(8,128)} %ids_ref.3, f32[16,11]{1,0:T(8,128)} %cameras_ref.3, f32[59,1024]{1,0:T(8,128)} %params_ref.3), custom_call_target="tpu_custom_call" | custom-call | tf_op jit(solution)/shard_map/project/pallas_call | solution.py:627
  2.6 17.5 %all_to_all.20.arrived_ref = f32[16,8,128]{2,1,0:T(8,128)S(1)} all-to-all(f32[16,8,128]{2,1,0:T(8,128)S(1)} %get-tuple-element.14), channel_id=1, replica_groups=mesh['view'=16,'tile'=16] {'view'}, dimensions={0} | all-to-all | bytes 131072 | tf_op jit(solution)/shard_map/all_to_all | solution.py:728
  20.2 1.0 %spread.1.after_ref = f32[16,72,128]{2,1,0:T(8,128)} custom-call(f32[16,8,128]{2,1,0:T(8,128)S(1)} %all_to_all.20.arrived_ref), custom_call_target="tpu_custom_call" | custom-call | tf_op jit(solution)/shard_map/spread/pallas_call | solution.py:639
  21.1 6.8 %all-to-all-start.1 = ((f32[16,72,128]{2,1,0:T(8,128)}), f32[16,72,128]{2,1,0:T(8,128)S(1)}, u32[]{:S(2)}, u32[]{:S(2)}) async-start(f32[16,72,128]{2,1,0:T(8,128)} %spread.1.after_ref), calls=%async_computation.1 | async-start | bytes 1179648 | tf_op jit(solution)/shard_map/all_to_all | solution.py:728
  27.9 0.0 copy-done.5
  27.9 0.0 copy-start.3
  27.9 0.6 prepare.1
  28.6 11.0 %all-to-all-done.1.everyone_ref = f32[16,72,128]{2,1,0:T(8,128)S(1)} async-done(((f32[16,72,128]{2,1,0:T(8,128)}), f32[16,72,128]{2,1,0:T(8,128)S(1)}, u32[]{:S(2)}, u32[]{:S(2)}) %all-to-all-start.1) | async-done | bytes 589856 | tf_op jit(solution)/shard_map/all_to_all | solution.py:728
  39.5 0.0 copy-done.6
  39.5 0.0 copy-done.7
  39.5 10.2 %render.1 = (f32[3,1,512]{2,1,0:T(1,128)}, f32[16,72,128]{2,1,0:T(8,128)S(1)}) custom-call(s32[1]{0:T(128)} %bitcast.place_ref, s32[1,2]{1,0:T(1,128)S(1)} %copy-done.7, bf16[256,2048]{1,0:T(8,128)(2,1)S(1)} %get-tuple-element.15.onehot, s32[1,2048]{1,0:T(1,128)S(1)} %get-tuple-element.16.lanes_of, s32[1,2048]{1,0:T(1,128)S(1)} %get-tuple-element.17.chosen, ...), custom_call_target="tpu_custom_call" | custom-call | tf_op jit(solution)/shard_map/render/pallas_call | solution.py:676
  49.8 0.0 copy-start
  49.8 0.0 copy-start.1
  49.8 0.0 copy-start.2
  49.8 0.0 copy-start.4
  49.8 14.4 %all_to_all.21.arrived_ref = f32[16,72,128]{2,1,0:T(8,128)S(1)} all-to-all(f32[16,72,128]{2,1,0:T(8,128)S(1)} %get-tuple-element.18), channel_id=1, replica_groups=mesh['view'=16,'tile'=16] {'tile'}, dimensions={0} | all-to-all | bytes 1179648 | tf_op jit(solution)/shard_map/all_to_all | solution.py:728
  64.2 0.7 merge.1.after_ref
  65.0 5.4 %all-to-all-start.3 = ((f32[16,8,128]{2,1,0:T(8,128)}), f32[16,8,128]{2,1,0:T(8,128)S(1)}, u32[]{:S(2)}, u32[]{:S(2)}) async-start(f32[16,8,128]{2,1,0:T(8,128)} %merge.1.after_ref), calls=%async_computation.3 | async-start | bytes 131072 | tf_op jit(solution)/shard_map/all_to_all | solution.py:728
  70.4 0.0 copy-done.3
  70.4 1.1 %columns.1.onehot_ref = bf16[1024,1024]{1,0:T(8,128)(2,1)S(1)} custom-call(f32[16,8,128]{2,1,0:T(8,128)} %merge.1.after_ref, s32[16,64]{1,0:T(8,128)S(1)} %copy-done.3), custom_call_target="tpu_custom_call" | custom-call | tf_op jit(solution)/shard_map/columns/pallas_call | solution.py:650
  71.4 6.8 %all-to-all-done.3.arrived_ref = f32[16,8,128]{2,1,0:T(8,128)S(1)} async-done(((f32[16,8,128]{2,1,0:T(8,128)}), f32[16,8,128]{2,1,0:T(8,128)S(1)}, u32[]{:S(2)}, u32[]{:S(2)}) %all-to-all-start.3) | async-done | bytes 65568 | tf_op jit(solution)/shard_map/all_to_all | solution.py:728
  78.2 0.0 copy-done
  78.2 0.0 copy-done.1
  78.2 0.0 copy-done.2
  78.2 0.0 copy-done.4
  78.2 3.0 %update.1 = (f32[59,1024]{1,0:T(8,128)}, f32[59,1024]{1,0:T(8,128)}, f32[59,1024]{1,0:T(8,128)}) custom-call(bf16[1024,1024]{1,0:T(8,128)(2,1)S(1)} %columns.1.onehot_ref, f32[16,11]{1,0:T(8,128)S(1)} %copy-done.4, f32[16,8,128]{2,1,0:T(8,128)S(1)} %all-to-all-done.3.arrived_ref, f32[512,128]{1,0:T(8,128)S(1)} %get-tuple-element.19.picked_ref, ...), custom_call_target="tpu_custom_call" | custom-call | tf_op jit(solution)/shard_map/update/pallas_call | solution.py:707
Async XLA Ops:
  0.6 27.3 %copy-start.5 = (s32[1,2,1024]{2,1,0:T(2,128)S(1)}, s32[1,2,1024]{2,1,0:T(2,128)}, u32[]{:S(2)}) copy-start(s32[1,2,1024]{2,1,0:T(2,128)} %lists_ref.1) | copy-start | bytes 24580
  0.6 38.9 %copy-start.6 = (f32[1,3,512]{2,0,1:T(1,128)S(1)}, f32[1,3,512]{2,0,1:T(1,128)}, u32[]{:S(2)}) copy-start(f32[1,3,512]{2,0,1:T(1,128)} %param.15) | copy-start | bytes 18436
  0.7 38.9 %copy-start.7 = (s32[1,2]{1,0:T(1,128)S(1)}, s32[1,2]{1,0:T(1,128)}, u32[]{:S(2)}) copy-start(s32[1,2]{1,0:T(1,128)} %counts_ref.1) | copy-start | bytes 28
  21.1 18.4 %all-to-all-start.1 = ((f32[16,72,128]{2,1,0:T(8,128)}), f32[16,72,128]{2,1,0:T(8,128)S(1)}, u32[]{:S(2)}, u32[]{:S(2)}) async-start(f32[16,72,128]{2,1,0:T(8,128)} %spread.1.after_ref), calls=%async_computation.1 | async-start | bytes 1179648 | tf_op jit(solution)/shard_map/all_to_all | solution.py:728
  27.9 42.5 %copy-start.3 = (s32[16,64]{1,0:T(8,128)S(1)}, s32[16,64]{1,0:T(8,128)}, u32[]{:S(2)}) copy-start(s32[16,64]{1,0:T(8,128)} %ids_ref.3) | copy-start | bytes 12292
  49.8 28.4 %copy-start = (f32[59,1024]{1,0:T(8,128)S(1)}, f32[59,1024]{1,0:T(8,128)}, u32[]{:S(2)}) copy-start(f32[59,1024]{1,0:T(8,128)} %params_ref.3) | copy-start | bytes 724996
  49.8 28.4 %copy-start.1 = (f32[59,1024]{1,0:T(8,128)S(1)}, f32[59,1024]{1,0:T(8,128)}, u32[]{:S(2)}) copy-start(f32[59,1024]{1,0:T(8,128)} %first_ref.1) | copy-start | bytes 724996
  49.8 28.4 %copy-start.2 = (f32[59,1024]{1,0:T(8,128)S(1)}, f32[59,1024]{1,0:T(8,128)}, u32[]{:S(2)}) copy-start(f32[59,1024]{1,0:T(8,128)} %second_ref.1) | copy-start | bytes 724996
  49.8 28.4 %copy-start.4 = (f32[16,11]{1,0:T(8,128)S(1)}, f32[16,11]{1,0:T(8,128)}, u32[]{:S(2)}) copy-start(f32[16,11]{1,0:T(8,128)} %cameras_ref.3) | copy-start | bytes 2116
  65.0 13.2 %all-to-all-start.3 = ((f32[16,8,128]{2,1,0:T(8,128)}), f32[16,8,128]{2,1,0:T(8,128)S(1)}, u32[]{:S(2)}, u32[]{:S(2)}) async-start(f32[16,8,128]{2,1,0:T(8,128)} %merge.1.after_ref), calls=%async_computation.3 | async-start | bytes 131072 | tf_op jit(solution)/shard_map/all_to_all | solution.py:728

commit v6 on v5

--- a/solution.py
+++ b/solution.py
@@ -217,7 +217,9 @@
     return [picked_ref[pl.ds(row, 8, stride=ROWS), :] for row in range(PARAMS)]
 
 
-def project_kernel(ids_ref, cameras_ref, params_ref, picked_ref, send_ref, split, swap):
+def project_kernel(
+    ids_ref, cameras_ref, params_ref, saved_ref, send_ref, split, swap, picked_ref, leaving
+):
     for place, part in enumerate(parts_of(params_ref[...], 3)):
         split[place * ROWS : place * ROWS + PARAMS, :] = part
     for pair in range(4):
@@ -226,6 +228,8 @@
         picked = three[0:ROWS] + three[ROWS : 2 * ROWS] + three[2 * ROWS :]
         picked_ref[pair * 128 : pair * 128 + ROWS, :] = picked[:, :128]
         picked_ref[pair * 128 + ROWS : pair * 128 + 2 * ROWS, :] = picked[:, 128:]
+    copy = pltpu.make_async_copy(picked_ref, saved_ref, leaving)
+    copy.start()
     values = project(raw_rows(picked_ref), camera_arrays(cameras_ref))
     for place in range(8):
         swap[place * 8 : place * 8 + 8, :] = values[place]
@@ -235,6 +239,7 @@
         last = jnp.broadcast_to(values[8][pair : pair + 1, :], (8, 128))
         send_ref[2 * pair] = jnp.where(low, main, pltpu.roll(last, 64, 1))
         send_ref[2 * pair + 1] = jnp.where(low, pltpu.roll(main, 64, 1), last)
+    copy.wait()
 
 
 def unpack_pair(even, odd):
@@ -252,12 +257,24 @@
             out_ref[peer, 64 + pair : 65 + pair, :] = last
 
 
-def columns_kernel(after_ref, ids_ref, columns_ref):
-    for pair in range(4):
-        columns_ref[:, pair * 256 : pair * 256 + 256] = seen_columns(ids_ref, pair * 4, 256)
-
-
-def prepare_kernel(after_ref, lists_ref, onehot_ref, lanes_ref, groups_ref):
+def as_columns(row):
+    return jnp.transpose(jnp.broadcast_to(row.astype(F32), (128, 128))).astype(jnp.int32)
+
+
+def columns_kernel(after_ref, ids_ref, cameras_ref, picked_ref, columns_ref, spread_ref):
+    for pair in range(8):
+        row = jnp.concatenate(
+            [ids_ref[2 * pair : 2 * pair + 1, :], ids_ref[2 * pair + 1 : 2 * pair + 2, :]], axis=1
+        )
+        column = as_columns(row)
+        for start in range(0, 1024, 128):
+            hot = (iota((128, 128), 1) + start == column).astype(BF16)
+            columns_ref[pair * 128 : pair * 128 + 128, start : start + 128] = hot
+    for place, array in enumerate(raw_rows(picked_ref) + camera_arrays(cameras_ref)):
+        spread_ref[place] = array
+
+
+def prepare_kernel(after_ref, lists_ref, onehot_ref, turned_ref, lanes_ref, groups_ref):
     turn = (iota((128, 1024), 0) == (iota((128, 1024), 1) >> 3)).astype(BF16)
     pick_block = iota((8, 1024), 0) == (iota((8, 1024), 1) & 7)
     for tile in range(2):
@@ -273,6 +290,12 @@
         lane_index = ((high_row >> 3) & 1) * 128 + low_row
         span = slice(tile * 1024, tile * 1024 + 1024)
         onehot_ref[:, span] = (iota((256, 1024), 0) == lane_index).astype(BF16)
+        for start in range(0, 1024, 128):
+            column = as_columns(lane_index[:, start : start + 128])
+            lanes = iota((128, 128), 1)
+            rows = slice(tile * 1024 + start, tile * 1024 + start + 128)
+            turned_ref[rows, 0:128] = (lanes == column).astype(BF16)
+            turned_ref[rows, 128:256] = (lanes + 128 == column).astype(BF16)
         lanes_ref[:, span] = low_row
         groups_ref[:, span] = high_row
 
@@ -281,6 +304,7 @@
     place_ref,
     counts_ref,
     onehot,
+    turned,
     lanes_of,
     chosen,
     targets_ref,
@@ -306,7 +330,7 @@
                 table[part, start : start + 8, lanes] = last[part]
 
     def gather_chunk(chunk, carry):
-        lanes = pl.ds(pl.multiple_of(chunk * 256, 256), 256)
+        lanes = pl.ds(chunk * 256, 256)
         hot = onehot[:, lanes]
         found = mm(table[0], hot, ((1,), (0,)))
         found = found + mm(table[1], hot, ((1,), (0,)))
@@ -330,7 +354,7 @@
         zero = jnp.zeros((8, 128), F32)
         for side in range(2):
             cut = slice(side * 128, side * 128 + 128)
-            lanes = pl.ds(pl.multiple_of(chunk * 256 + side * 128, 128), 128)
+            lanes = pl.ds(chunk * 256 + side * 128, 128)
             lane = jnp.broadcast_to(lanes_of[:, lanes], (8, 128))
             group = both[:, cut]
             chains = [main[:, cut], zero, zero, zero]
@@ -350,7 +374,8 @@
             )
         return carry
 
-    lax.fori_loop(0, count // 256, gather_chunk, 0)
+    for chunk in range(8):
+        gather_chunk(chunk, 0)
 
     pixel = iota((8, PIX), 1)
     pixel_x = (pixel & (SIDE - 1)).astype(F32) + (0.5 - SIDE / 2)
@@ -511,19 +536,18 @@
         group = chosen[:, lanes]
         group = jnp.broadcast_to((group >> 4) * 8 + (group & 7), (8, wide))
         sub = iota((8, wide), 0)
-        hot = onehot[:, lanes]
         main = [part.astype(F32) for part in parts_of(picked[0:8, lanes], 2)]
         last = [part.astype(F32) for part in parts_of(picked[8:16, lanes], 2)]
-        total = None
+        sides = []
         for part in range(2):
             rows = [jnp.where(group == place, main[part], 0.0) for place in range(64)]
             rows += [jnp.where(group == half * 8 + sub, last[part], 0.0) for half in range(8)]
-            rows = [
+            sides += [
                 jnp.concatenate(rows[place : place + 2], axis=0).astype(BF16)
                 for place in range(0, 72, 2)
             ]
-            product = mm(jnp.concatenate(rows, axis=0), hot, ((1,), (1,)))
-            total = product if total is None else total + product
+        total = mm(jnp.concatenate(sides, axis=0), turned[lanes, :], ((1,), (0,)))
+        total = total[0:576] + total[576:]
         if chunk == 0:
             summed[...] = total
         elif chunk < count // wide - 1:
@@ -551,9 +575,8 @@
 
 def update_kernel(
     onehot_ref,
-    cameras_ref,
+    spread_ref,
     arrived_ref,
-    picked_ref,
     params_ref,
     first_ref,
     second_ref,
@@ -576,8 +599,9 @@
     for pair in range(8):
         final = jnp.where(sub == pair, jnp.broadcast_to(lasts[pair], (8, 128)), final)
     slopes.append(final)
-    cameras = camera_arrays(cameras_ref)
-    _, pullback = jax.vjp(lambda source: project(source, cameras), raw_rows(picked_ref))
+    arrays = [spread_ref[place] for place in range(PARAMS + 11)]
+    cameras = arrays[PARAMS:]
+    _, pullback = jax.vjp(lambda source: project(source, cameras), arrays[:PARAMS])
     (raw_grads,) = pullback(slopes)
     for row in range(PARAMS):
         turned[pl.ds(row, 8, stride=ROWS), :] = raw_grads[row]
@@ -585,7 +609,7 @@
         turned[pl.ds(row, 8, stride=ROWS), :] = jnp.ones((8, 128), F32)
     wide = jnp.concatenate([turned[pair * ROWS : pair * ROWS + ROWS, :] for pair in range(8)], axis=1)
     split = [part.astype(F32) for part in parts_of(wide, 3)]
-    three = mm(jnp.concatenate(split, axis=0).astype(BF16), onehot_ref[...], ((1,), (1,)))
+    three = mm(jnp.concatenate(split, axis=0).astype(BF16), onehot_ref[...], ((1,), (0,)))
     summed = three[0:ROWS] + three[ROWS : 2 * ROWS] + three[2 * ROWS :]
     seen = summed[PARAMS : PARAMS + 1, :] > 0.5
     outs = (new_params_ref, new_first_ref, new_second_ref)
@@ -626,10 +650,15 @@
 def project_call(visible, cameras, params):
     return pl.pallas_call(
         project_kernel,
-        out_shape=(f32_shape(512, 128), f32_shape(16, 8, 128)),
+        out_shape=(pltpu.HBM((512, 128), F32), f32_shape(16, 8, 128)),
         in_specs=[VMEM, SMEM, VMEM],
-        out_specs=(VMEM, VMEM),
-        scratch_shapes=[pltpu.VMEM((192, 1024), BF16), pltpu.VMEM((64, 128), F32)],
+        out_specs=(pl.BlockSpec(memory_space=pltpu.HBM), VMEM),
+        scratch_shapes=[
+            pltpu.VMEM((192, 1024), BF16),
+            pltpu.VMEM((64, 128), F32),
+            pltpu.VMEM((512, 128), F32),
+            pltpu.SemaphoreType.DMA,
+        ],
         compiler_params=pltpu.CompilerParams(vmem_limit_bytes=12 * MIB),
         name="project",
     )(visible, cameras, params)
@@ -646,15 +675,15 @@
     )(arrived)
 
 
-def columns_call(after, visible):
+def columns_call(after, visible, cameras, picked):
     return pl.pallas_call(
         columns_kernel,
-        out_shape=jax.ShapeDtypeStruct((1024, 1024), BF16),
-        in_specs=[pl.BlockSpec(memory_space=pl.ANY), VMEM],
-        out_specs=VMEM,
+        out_shape=(jax.ShapeDtypeStruct((1024, 1024), BF16), f32_shape(PARAMS + 11, 8, 128)),
+        in_specs=[pl.BlockSpec(memory_space=pl.ANY), VMEM, SMEM, VMEM],
+        out_specs=(VMEM, VMEM),
         compiler_params=pltpu.CompilerParams(vmem_limit_bytes=8 * MIB),
         name="columns",
-    )(after, visible)
+    )(after, visible, cameras, picked)
 
 
 def prepare_call(after, lists):
@@ -662,21 +691,22 @@
         prepare_kernel,
         out_shape=(
             jax.ShapeDtypeStruct((256, 2048), BF16),
+            jax.ShapeDtypeStruct((2048, 256), BF16),
             jax.ShapeDtypeStruct((1, 2048), jnp.int32),
             jax.ShapeDtypeStruct((1, 2048), jnp.int32),
         ),
         in_specs=[pl.BlockSpec(memory_space=pl.ANY), VMEM],
-        out_specs=(VMEM, VMEM, VMEM),
+        out_specs=(VMEM, VMEM, VMEM, VMEM),
         compiler_params=pltpu.CompilerParams(vmem_limit_bytes=16 * MIB),
         name="prepare",
     )(after, lists)
 
 
-def render_call(place, counts, onehot, lanes, groups, targets, everyone):
+def render_call(place, counts, onehot, turned, lanes, groups, targets, everyone):
     return pl.pallas_call(
         render_kernel,
         out_shape=(f32_shape(3, 1, 512), f32_shape(16, 72, 128)),
-        in_specs=[SMEM, SMEM, VMEM, VMEM, VMEM, VMEM, VMEM],
+        in_specs=[SMEM, SMEM, VMEM, VMEM, VMEM, VMEM, VMEM, VMEM],
         out_specs=(VMEM, VMEM),
         scratch_shapes=[
             pltpu.VMEM((16, 2048), F32),
@@ -688,7 +718,7 @@
         ],
         compiler_params=pltpu.CompilerParams(vmem_limit_bytes=24 * MIB),
         name="render",
-    )(place, counts, onehot, lanes, groups, targets, everyone)
+    )(place, counts, onehot, turned, lanes, groups, targets, everyone)
 
 
 def merge_call(arrived):
@@ -702,12 +732,12 @@
     )(arrived)
 
 
-def update_call(onehot, cameras, arrived, picked, params, first, second):
+def update_call(onehot, spread, arrived, params, first, second):
     shape = f32_shape(*params.shape)
     return pl.pallas_call(
         update_kernel,
         out_shape=(shape, shape, shape),
-        in_specs=[VMEM, SMEM, VMEM, VMEM, VMEM, VMEM, VMEM],
+        in_specs=[VMEM] * 6,
         out_specs=(pl.BlockSpec(memory_space=pl.ANY),) * 3,
         scratch_shapes=[
             pltpu.VMEM((64, 128), F32),
@@ -717,7 +747,7 @@
         ],
         compiler_params=pltpu.CompilerParams(vmem_limit_bytes=16 * MIB),
         name="update",
-    )(onehot, cameras, arrived, picked, params, first, second)
+    )(onehot, spread, arrived, params, first, second)
 
 
 def kept(array):
@@ -734,12 +764,13 @@
     )
     block = spread_call(exchanged(outgoing, "view"))
     everyone = exchanged(block, "tile")
-    onehot, lanes, groups = [kept(table) for table in prepare_call(block, tile_lists)]
+    onehot, turned, lanes, groups = [kept(table) for table in prepare_call(block, tile_lists)]
     place = lax.axis_index("tile").astype(jnp.int32).reshape(1)
     image, sums = render_call(
         place,
         tile_blocks,
         onehot,
+        turned,
         lanes,
         groups,
         jnp.transpose(targets, (1, 0, 2)),
@@ -747,9 +778,9 @@
     )
     merged = merge_call(exchanged(sums, "tile"))
     returned = exchanged(merged, "view")
-    columns = kept(columns_call(merged, visible))
+    columns, rows = columns_call(merged, visible, cameras, picked)
     new_params, new_first, new_second = update_call(
-        columns, cameras, returned, kept(picked), kept(params), kept(first), kept(second)
+        kept(columns), kept(rows), returned, kept(params), kept(first), kept(second)
     )
     return (new_params, new_first, new_second, jnp.transpose(image, (1, 0, 2)))
 

time: 81.6 us -> 78.7 us (0.964)
  Pallas kernels: 18.6 us -> 16.5 us
    pallas_call x1, Pallas kernels: 10.2 us -> 7.83 us  [render_call(): pl.pallas_call(render_kernel, out_shape=(f32_shape(3, 1, 512), f32_shape(...]
    pallas_call x1, Pallas kernels: 3 us -> 2 us  [update_call(): pl.pallas_call(update_kernel, out_shape=(shape, shape, shape), in_specs=[...]
    pallas_call x2, Pallas kernels: 3.03 us -> 3.99 us  [the longest x1 2.57 us: project_call(): pl.pallas_call(project_kernel, out_shape=(pltpu.HBM((512, 128), F32), f32...]
  transfers between devices with their start and end apart: 2 -> 2, of which waited for: 2 -> 2; matrix products, arithmetic and copies ran while one was open for 0% -> 0% of each run, Pallas kernels for 2% -> 3%
where the time goes in v6:
time: 78.7 us; the launch traced here: 78.4 us
  blocking collectives  31.9 us (41%)
  waiting for transfers between devices  17 us (22%)
  Pallas kernels  16.5 us (21%)
  starting transfers between devices  12.2 us (16%)
    all_to_all x2, blocking collectives, exchanged(): return kept(lax.all_to_all(array, axis, 0, 0, tiled=True))  31.9 us
    all_to_all x2, waiting for transfers between devices, exchanged(): return kept(lax.all_to_all(array, axis, 0, 0, tiled=True))  17 us
    all_to_all x2, starting transfers between devices, exchanged(): return kept(lax.all_to_all(array, axis, 0, 0, tiled=True))  12.2 us
    pallas_call x1, Pallas kernels, render_call(): pl.pallas_call(render_kernel, out_shape=(f32_shape(3, 1, 512), f32_shape(...  7.83 us
    pallas_call x1, Pallas kernels, project_call(): pl.pallas_call(project_kernel, out_shape=(pltpu.HBM((512, 128), F32), f32...  2.57 us
    pallas_call x1, Pallas kernels, update_call(): pl.pallas_call(update_kernel, out_shape=(shape, shape, shape), in_specs=[...  2 us
  transfers between devices with their start and end apart: 2, of which 2 were waited for; matrix products, arithmetic and copies ran while one was open for 0% of the time, Pallas kernels for 3%

profile of v6, /device:TPU:1, one launch (start us, length us, event | category | flops | bytes accessed | tf_op | source)
XLA Modules:
  0.0 78.4 jit_solution(8056162230106876406)
XLA Ops:
  0.6 0.0 copy-start.6
  0.6 0.0 copy-start.7
  0.7 0.0 copy-start.8
  0.7 2.6 %project.1 = (f32[512,128]{1,0:T(8,128)}, f32[16,8,128]{2,1,0:T(8,128)S(1)}) custom-call(s32[16,64]{1,0:T(8,128)} %ids_ref.3, f32[16,11]{1,0:T(8,128)} %cameras_ref.3, f32[59,1024]{1,0:T(8,128)} %params_ref.3), custom_call_target="tpu_custom_call" | custom-call | tf_op jit(solution)/shard_map/project/pallas_call | solution.py:651
  3.2 17.5 %all_to_all.20.arrived_ref = f32[16,8,128]{2,1,0:T(8,128)S(1)} all-to-all(f32[16,8,128]{2,1,0:T(8,128)S(1)} %get-tuple-element.17), channel_id=1, replica_groups=mesh['view'=16,'tile'=16] {'view'}, dimensions={0} | all-to-all | bytes 131072 | tf_op jit(solution)/shard_map/all_to_all | solution.py:758
  20.8 1.0 %spread.1.after_ref = f32[16,72,128]{2,1,0:T(8,128)} custom-call(f32[16,8,128]{2,1,0:T(8,128)S(1)} %all_to_all.20.arrived_ref), custom_call_target="tpu_custom_call" | custom-call | tf_op jit(solution)/shard_map/spread/pallas_call | solution.py:668
  21.7 6.8 %all-to-all-start.1 = ((f32[16,72,128]{2,1,0:T(8,128)}), f32[16,72,128]{2,1,0:T(8,128)S(1)}, u32[]{:S(2)}, u32[]{:S(2)}) async-start(f32[16,72,128]{2,1,0:T(8,128)} %spread.1.after_ref), calls=%async_computation.1 | async-start | bytes 1179648 | tf_op jit(solution)/shard_map/all_to_all | solution.py:758
  28.5 0.0 copy-done.6
  28.5 0.9 %prepare.1 = (bf16[256,2048]{1,0:T(8,128)(2,1)S(1)}, bf16[2048,256]{1,0:T(8,128)(2,1)S(1)}, s32[1,2048]{1,0:T(1,128)S(1)}, s32[1,2048]{1,0:T(1,128)S(1)}) custom-call(f32[16,72,128]{2,1,0:T(8,128)} %spread.1.after_ref, s32[1,2,1024]{2,1,0:T(2,128)S(1)} %copy-done.6), custom_call_target="tpu_custom_call" | custom-call | tf_op jit(solution)/shard_map/prepare/pallas_call | solution.py:690
  29.5 10.7 %all-to-all-done.1.everyone_ref = f32[16,72,128]{2,1,0:T(8,128)S(1)} async-done(((f32[16,72,128]{2,1,0:T(8,128)}), f32[16,72,128]{2,1,0:T(8,128)S(1)}, u32[]{:S(2)}, u32[]{:S(2)}) %all-to-all-start.1) | async-done | bytes 589856 | tf_op jit(solution)/shard_map/all_to_all | solution.py:758
  40.1 0.0 copy-done.7
  40.1 0.0 copy-done.8
  40.1 0.0 copy-start.4
  40.1 0.0 copy-start.5
  40.2 0.0 copy-start
  40.2 7.8 %render.1 = (f32[3,1,512]{2,1,0:T(1,128)}, f32[16,72,128]{2,1,0:T(8,128)S(1)}) custom-call(s32[1]{0:T(128)} %bitcast.place_ref, s32[1,2]{1,0:T(1,128)S(1)} %copy-done.8, bf16[256,2048]{1,0:T(8,128)(2,1)S(1)} %get-tuple-element.18.onehot, bf16[2048,256]{1,0:T(8,128)(2,1)S(1)} %get-tuple-element.19.turned, s32[1,2048]{1,0:T(1,128)S(1)} %get-tuple-element.20.lanes_of, ...), custom_call_target="tpu_custom_call" | custom-call | tf_op jit(solution)/shard_map/render/pallas_call | solution.py:706
  48.0 0.0 copy-start.3
  48.0 0.0 copy-start.1
  48.0 0.0 copy-start.2
  48.0 14.4 %all_to_all.21.arrived_ref = f32[16,72,128]{2,1,0:T(8,128)S(1)} all-to-all(f32[16,72,128]{2,1,0:T(8,128)S(1)} %get-tuple-element.22), channel_id=1, replica_groups=mesh['view'=16,'tile'=16] {'tile'}, dimensions={0} | all-to-all | bytes 1179648 | tf_op jit(solution)/shard_map/all_to_all | solution.py:758
  62.4 0.7 merge.1.after_ref
  63.1 5.4 %all-to-all-start.3 = ((f32[16,8,128]{2,1,0:T(8,128)}), f32[16,8,128]{2,1,0:T(8,128)S(1)}, u32[]{:S(2)}, u32[]{:S(2)}) async-start(f32[16,8,128]{2,1,0:T(8,128)} %merge.1.after_ref), calls=%async_computation.3 | async-start | bytes 131072 | tf_op jit(solution)/shard_map/all_to_all | solution.py:758
  68.6 0.0 copy-done.4
  68.6 0.0 copy-done.5
  68.6 0.0 copy-done.3
  68.6 1.4 %columns.1 = (bf16[1024,1024]{1,0:T(8,128)(2,1)S(1)}, f32[70,8,128]{2,1,0:T(8,128)S(1)}) custom-call(f32[16,8,128]{2,1,0:T(8,128)} %merge.1.after_ref, s32[16,64]{1,0:T(8,128)S(1)} %copy-done.4, f32[16,11]{1,0:T(8,128)S(1)} %copy-done.5, f32[512,128]{1,0:T(8,128)S(1)} %copy-done.3), custom_call_target="tpu_custom_call" | custom-call | tf_op jit(solution)/shard_map/columns/pallas_call | solution.py:679
  70.0 6.4 %all-to-all-done.3.arrived_ref = f32[16,8,128]{2,1,0:T(8,128)S(1)} async-done(((f32[16,8,128]{2,1,0:T(8,128)}), f32[16,8,128]{2,1,0:T(8,128)S(1)}, u32[]{:S(2)}, u32[]{:S(2)}) %all-to-all-start.3) | async-done | bytes 65568 | tf_op jit(solution)/shard_map/all_to_all | solution.py:758
  76.4 0.0 copy-done
  76.4 0.0 copy-done.1
  76.4 0.0 copy-done.2
  76.4 2.0 %update.1 = (f32[59,1024]{1,0:T(8,128)}, f32[59,1024]{1,0:T(8,128)}, f32[59,1024]{1,0:T(8,128)}) custom-call(bf16[1024,1024]{1,0:T(8,128)(2,1)S(1)} %get-tuple-element.24.onehot_ref, f32[70,8,128]{2,1,0:T(8,128)S(1)} %get-tuple-element.25.spread_ref, f32[16,8,128]{2,1,0:T(8,128)S(1)} %all-to-all-done.3.arrived_ref, f32[59,1024]{1,0:T(8,128)S(1)} %copy-done, ...), custom_call_target="tpu_custom_call" | custom-call | tf_op jit(solution)/shard_map/update/pallas_call | solution.py:737
Async XLA Ops:
  0.6 27.9 %copy-start.6 = (s32[1,2,1024]{2,1,0:T(2,128)S(1)}, s32[1,2,1024]{2,1,0:T(2,128)}, u32[]{:S(2)}) copy-start(s32[1,2,1024]{2,1,0:T(2,128)} %lists_ref.1) | copy-start | bytes 24580
  0.6 39.5 %copy-start.7 = (f32[1,3,512]{2,0,1:T(1,128)S(1)}, f32[1,3,512]{2,0,1:T(1,128)}, u32[]{:S(2)}) copy-start(f32[1,3,512]{2,0,1:T(1,128)} %param.15) | copy-start | bytes 18436
  0.7 39.5 %copy-start.8 = (s32[1,2]{1,0:T(1,128)S(1)}, s32[1,2]{1,0:T(1,128)}, u32[]{:S(2)}) copy-start(s32[1,2]{1,0:T(1,128)} %counts_ref.1) | copy-start | bytes 28
  21.7 18.4 %all-to-all-start.1 = ((f32[16,72,128]{2,1,0:T(8,128)}), f32[16,72,128]{2,1,0:T(8,128)S(1)}, u32[]{:S(2)}, u32[]{:S(2)}) async-start(f32[16,72,128]{2,1,0:T(8,128)} %spread.1.after_ref), calls=%async_computation.1 | async-start | bytes 1179648 | tf_op jit(solution)/shard_map/all_to_all | solution.py:758
  40.1 28.4 %copy-start.4 = (s32[16,64]{1,0:T(8,128)S(1)}, s32[16,64]{1,0:T(8,128)}, u32[]{:S(2)}) copy-start(s32[16,64]{1,0:T(8,128)} %ids_ref.3) | copy-start | bytes 12292
  40.1 28.4 %copy-start.5 = (f32[16,11]{1,0:T(8,128)S(1)}, f32[16,11]{1,0:T(8,128)}, u32[]{:S(2)}) copy-start(f32[16,11]{1,0:T(8,128)} %cameras_ref.3) | copy-start | bytes 2116
  40.2 36.2 %copy-start = (f32[59,1024]{1,0:T(8,128)S(1)}, f32[59,1024]{1,0:T(8,128)}, u32[]{:S(2)}) copy-start(f32[59,1024]{1,0:T(8,128)} %params_ref.3) | copy-start | bytes 724996
  48.0 20.6 %copy-start.3 = (f32[512,128]{1,0:T(8,128)S(1)}, f32[512,128]{1,0:T(8,128)}, u32[]{:S(2)}) copy-start(f32[512,128]{1,0:T(8,128)} %get-tuple-element.23.picked_ref) | copy-start | bytes 786436
  48.0 28.4 %copy-start.1 = (f32[59,1024]{1,0:T(8,128)S(1)}, f32[59,1024]{1,0:T(8,128)}, u32[]{:S(2)}) copy-start(f32[59,1024]{1,0:T(8,128)} %first_ref.1) | copy-start | bytes 724996
  48.0 28.4 %copy-start.2 = (f32[59,1024]{1,0:T(8,128)S(1)}, f32[59,1024]{1,0:T(8,128)}, u32[]{:S(2)}) copy-start(f32[59,1024]{1,0:T(8,128)} %second_ref.1) | copy-start | bytes 724996
  63.1 13.2 %all-to-all-start.3 = ((f32[16,8,128]{2,1,0:T(8,128)}), f32[16,8,128]{2,1,0:T(8,128)S(1)}, u32[]{:S(2)}, u32[]{:S(2)}) async-start(f32[16,8,128]{2,1,0:T(8,128)} %merge.1.after_ref), calls=%async_computation.3 | async-start | bytes 131072 | tf_op jit(solution)/shard_map/all_to_all | solution.py:758

commit v7 on v6

--- a/solution.py
+++ b/solution.py
@@ -217,9 +217,7 @@
     return [picked_ref[pl.ds(row, 8, stride=ROWS), :] for row in range(PARAMS)]
 
 
-def project_kernel(
-    ids_ref, cameras_ref, params_ref, saved_ref, send_ref, split, swap, picked_ref, leaving
-):
+def pick_rows(ids_ref, params_ref, split, picked_ref):
     for place, part in enumerate(parts_of(params_ref[...], 3)):
         split[place * ROWS : place * ROWS + PARAMS, :] = part
     for pair in range(4):
@@ -228,8 +226,10 @@
         picked = three[0:ROWS] + three[ROWS : 2 * ROWS] + three[2 * ROWS :]
         picked_ref[pair * 128 : pair * 128 + ROWS, :] = picked[:, :128]
         picked_ref[pair * 128 + ROWS : pair * 128 + 2 * ROWS, :] = picked[:, 128:]
-    copy = pltpu.make_async_copy(picked_ref, saved_ref, leaving)
-    copy.start()
+
+
+def project_kernel(ids_ref, cameras_ref, params_ref, send_ref, split, swap, picked_ref):
+    pick_rows(ids_ref, params_ref, split, picked_ref)
     values = project(raw_rows(picked_ref), camera_arrays(cameras_ref))
     for place in range(8):
         swap[place * 8 : place * 8 + 8, :] = values[place]
@@ -239,7 +239,6 @@
         last = jnp.broadcast_to(values[8][pair : pair + 1, :], (8, 128))
         send_ref[2 * pair] = jnp.where(low, main, pltpu.roll(last, 64, 1))
         send_ref[2 * pair + 1] = jnp.where(low, pltpu.roll(main, 64, 1), last)
-    copy.wait()
 
 
 def unpack_pair(even, odd):
@@ -261,7 +260,7 @@
     return jnp.transpose(jnp.broadcast_to(row.astype(F32), (128, 128))).astype(jnp.int32)
 
 
-def columns_kernel(after_ref, ids_ref, cameras_ref, picked_ref, columns_ref, spread_ref):
+def columns_kernel(after_ref, ids_ref, columns_ref):
     for pair in range(8):
         row = jnp.concatenate(
             [ids_ref[2 * pair : 2 * pair + 1, :], ids_ref[2 * pair + 1 : 2 * pair + 2, :]], axis=1
@@ -270,11 +269,26 @@
         for start in range(0, 1024, 128):
             hot = (iota((128, 128), 1) + start == column).astype(BF16)
             columns_ref[pair * 128 : pair * 128 + 128, start : start + 128] = hot
+
+
+def prepare_kernel(
+    after_ref,
+    ids_ref,
+    cameras_ref,
+    params_ref,
+    lists_ref,
+    rows_ref,
+    onehot_ref,
+    turned_ref,
+    lanes_ref,
+    groups_ref,
+    split,
+    picked_ref,
+):
+    pick_rows(ids_ref, params_ref, split, picked_ref)
     for place, array in enumerate(raw_rows(picked_ref) + camera_arrays(cameras_ref)):
-        spread_ref[place] = array
-
-
-def prepare_kernel(after_ref, lists_ref, onehot_ref, turned_ref, lanes_ref, groups_ref):
+        rows_ref[place] = array
+
     turn = (iota((128, 1024), 0) == (iota((128, 1024), 1) >> 3)).astype(BF16)
     pick_block = iota((8, 1024), 0) == (iota((8, 1024), 1) & 7)
     for tile in range(2):
@@ -503,7 +517,7 @@
 
     for tile in range(2):
         moments = sum(
-            mm(basis_once, part, ((1,), (1,))) for part in parts_of(shades[tile], 3)
+            mm(basis_once, part, ((1,), (1,))) for part in parts_of(shades[tile], 2)
         )
         tints = sum(mm(blame[tile], part, ((1,), (1,))) for part in parts_of(weights[tile], 2))
         tints = tints[0:8, :] + tints[8:16, :]
@@ -650,14 +664,13 @@
 def project_call(visible, cameras, params):
     return pl.pallas_call(
         project_kernel,
-        out_shape=(pltpu.HBM((512, 128), F32), f32_shape(16, 8, 128)),
+        out_shape=f32_shape(16, 8, 128),
         in_specs=[VMEM, SMEM, VMEM],
-        out_specs=(pl.BlockSpec(memory_space=pltpu.HBM), VMEM),
+        out_specs=VMEM,
         scratch_shapes=[
             pltpu.VMEM((192, 1024), BF16),
             pltpu.VMEM((64, 128), F32),
             pltpu.VMEM((512, 128), F32),
-            pltpu.SemaphoreType.DMA,
         ],
         compiler_params=pltpu.CompilerParams(vmem_limit_bytes=12 * MIB),
         name="project",
@@ -675,31 +688,33 @@
     )(arrived)
 
 
-def columns_call(after, visible, cameras, picked):
+def columns_call(after, visible):
     return pl.pallas_call(
         columns_kernel,
-        out_shape=(jax.ShapeDtypeStruct((1024, 1024), BF16), f32_shape(PARAMS + 11, 8, 128)),
-        in_specs=[pl.BlockSpec(memory_space=pl.ANY), VMEM, SMEM, VMEM],
-        out_specs=(VMEM, VMEM),
+        out_shape=jax.ShapeDtypeStruct((1024, 1024), BF16),
+        in_specs=[pl.BlockSpec(memory_space=pl.ANY), VMEM],
+        out_specs=VMEM,
         compiler_params=pltpu.CompilerParams(vmem_limit_bytes=8 * MIB),
         name="columns",
-    )(after, visible, cameras, picked)
-
-
-def prepare_call(after, lists):
+    )(after, visible)
+
+
+def prepare_call(after, visible, cameras, params, lists):
     return pl.pallas_call(
         prepare_kernel,
         out_shape=(
+            f32_shape(PARAMS + 11, 8, 128),
             jax.ShapeDtypeStruct((256, 2048), BF16),
             jax.ShapeDtypeStruct((2048, 256), BF16),
             jax.ShapeDtypeStruct((1, 2048), jnp.int32),
             jax.ShapeDtypeStruct((1, 2048), jnp.int32),
         ),
-        in_specs=[pl.BlockSpec(memory_space=pl.ANY), VMEM],
-        out_specs=(VMEM, VMEM, VMEM, VMEM),
+        in_specs=[pl.BlockSpec(memory_space=pl.ANY), VMEM, SMEM, VMEM, VMEM],
+        out_specs=(VMEM, VMEM, VMEM, VMEM, VMEM),
+        scratch_shapes=[pltpu.VMEM((192, 1024), BF16), pltpu.VMEM((512, 128), F32)],
         compiler_params=pltpu.CompilerParams(vmem_limit_bytes=16 * MIB),
         name="prepare",
-    )(after, lists)
+    )(after, visible, cameras, params, lists)
 
 
 def render_call(place, counts, onehot, turned, lanes, groups, targets, everyone):
@@ -759,12 +774,14 @@
 
 
 def shards(params, first, second, visible, cameras, tile_lists, tile_blocks, targets):
-    picked, outgoing = project_call(
+    outgoing = project_call(
         *[pltpu.with_memory_space_constraint(array, pltpu.HBM) for array in (visible, cameras, params)]
     )
     block = spread_call(exchanged(outgoing, "view"))
     everyone = exchanged(block, "tile")
-    onehot, turned, lanes, groups = [kept(table) for table in prepare_call(block, tile_lists)]
+    rows, onehot, turned, lanes, groups = [
+        kept(table) for table in prepare_call(block, visible, cameras, params, tile_lists)
+    ]
     place = lax.axis_index("tile").astype(jnp.int32).reshape(1)
     image, sums = render_call(
         place,
@@ -778,9 +795,9 @@
     )
     merged = merge_call(exchanged(sums, "tile"))
     returned = exchanged(merged, "view")
-    columns, rows = columns_call(merged, visible, cameras, picked)
+    columns = columns_call(merged, visible)
     new_params, new_first, new_second = update_call(
-        kept(columns), kept(rows), returned, kept(params), kept(first), kept(second)
+        kept(columns), rows, returned, kept(params), kept(first), kept(second)
     )
     return (new_params, new_first, new_second, jnp.transpose(image, (1, 0, 2)))
 

time: 78.7 us -> 77.9 us (0.990)
  transfers between devices with their start and end apart: 2 -> 2, of which waited for: 2 -> 2; matrix products, arithmetic and copies ran while one was open for 0% -> 0% of each run, Pallas kernels for 3% -> 4%
where the time goes in v7:
time: 77.9 us; the launch traced here: 77.5 us
  blocking collectives  31.9 us (41%)
  waiting for transfers between devices  16.5 us (21%)
  Pallas kernels  16.1 us (21%)
  starting transfers between devices  12.2 us (16%)
  between operations  0.79 us (1%)
    all_to_all x2, blocking collectives, exchanged(): return kept(lax.all_to_all(array, axis, 0, 0, tiled=True))  31.9 us
    all_to_all x2, waiting for transfers between devices, exchanged(): return kept(lax.all_to_all(array, axis, 0, 0, tiled=True))  16.5 us
    all_to_all x2, starting transfers between devices, exchanged(): return kept(lax.all_to_all(array, axis, 0, 0, tiled=True))  12.2 us
    pallas_call x1, Pallas kernels, render_call(): pl.pallas_call(render_kernel, out_shape=(f32_shape(3, 1, 512), f32_shape(...  7.54 us
    pallas_call x1, Pallas kernels, prepare_call(): pl.pallas_call(prepare_kernel, out_shape=(f32_shape(PARAMS + 11, 8, 128),...  2.32 us
    pallas_call x1, Pallas kernels, update_call(): pl.pallas_call(update_kernel, out_shape=(shape, shape, shape), in_specs=[...  2 us
    pallas_call x1, Pallas kernels, project_call(): pl.pallas_call(project_kernel, out_shape=f32_shape(16, 8, 128), in_specs=...  1.99 us
  transfers between devices with their start and end apart: 2, of which 2 were waited for; matrix products, arithmetic and copies ran while one was open for 0% of the time, Pallas kernels for 4%

profile of v7, /device:TPU:1, one launch (start us, length us, event | category | flops | bytes accessed | tf_op | source)
XLA Modules:
  0.0 77.5 jit_solution(14522895409628098120)
XLA Ops:
  0.6 0.0 copy-start.5
  0.6 0.0 copy-start
  0.7 0.0 copy-start.6
  0.7 0.0 copy-start.7
  0.7 0.0 copy-start.8
  0.7 0.0 copy-start.9
  0.7 2.0 %project.1 = f32[16,8,128]{2,1,0:T(8,128)S(1)} custom-call(s32[16,64]{1,0:T(8,128)} %ids_ref.5, f32[16,11]{1,0:T(8,128)} %cameras_ref.3, f32[59,1024]{1,0:T(8,128)} %params_ref.5), custom_call_target="tpu_custom_call" | custom-call | tf_op jit(solution)/shard_map/project/pallas_call | solution.py:665
  2.7 17.5 %all_to_all.20.arrived_ref = f32[16,8,128]{2,1,0:T(8,128)S(1)} all-to-all(f32[16,8,128]{2,1,0:T(8,128)S(1)} %project.1), channel_id=1, replica_groups=mesh['view'=16,'tile'=16] {'view'}, dimensions={0} | all-to-all | bytes 131072 | tf_op jit(solution)/shard_map/all_to_all | solution.py:773
  20.2 1.0 %spread.1.after_ref = f32[16,72,128]{2,1,0:T(8,128)} custom-call(f32[16,8,128]{2,1,0:T(8,128)S(1)} %all_to_all.20.arrived_ref), custom_call_target="tpu_custom_call" | custom-call | tf_op jit(solution)/shard_map/spread/pallas_call | solution.py:681
  21.2 6.8 %all-to-all-start.1 = ((f32[16,72,128]{2,1,0:T(8,128)}), f32[16,72,128]{2,1,0:T(8,128)S(1)}, u32[]{:S(2)}, u32[]{:S(2)}) async-start(f32[16,72,128]{2,1,0:T(8,128)} %spread.1.after_ref), calls=%async_computation.1 | async-start | bytes 1179648 | tf_op jit(solution)/shard_map/all_to_all | solution.py:773
  27.9 0.0 copy-done.5
  28.0 0.0 copy-done
  28.0 0.0 copy-done.6
  28.0 0.0 copy-done.7
  28.0 2.3 %prepare.1 = (f32[70,8,128]{2,1,0:T(8,128)S(1)}, bf16[256,2048]{1,0:T(8,128)(2,1)S(1)}, bf16[2048,256]{1,0:T(8,128)(2,1)S(1)}, s32[1,2048]{1,0:T(1,128)S(1)}, s32[1,2048]{1,0:T(1,128)S(1)}) custom-call(f32[16,72,128]{2,1,0:T(8,128)} %spread.1.after_ref, s32[16,64]{1,0:T(8,128)S(1)} %copy-done.5, f32[16,11]{1,0:T(8,128)S(1)} %copy-done.6, ...), custom_call_target="tpu_custom_call" | custom-call | tf_op jit(solution)/shard_map/prepare/pallas_call | solution.py:703
  30.3 0.0 copy-start.1
  30.3 9.3 %all-to-all-done.1.everyone_ref = f32[16,72,128]{2,1,0:T(8,128)S(1)} async-done(((f32[16,72,128]{2,1,0:T(8,128)}), f32[16,72,128]{2,1,0:T(8,128)S(1)}, u32[]{:S(2)}, u32[]{:S(2)}) %all-to-all-start.1) | async-done | bytes 589856 | tf_op jit(solution)/shard_map/all_to_all | solution.py:773
  39.6 0.0 copy-done.8
  39.6 0.0 copy-done.9
  39.6 7.5 %render.1 = (f32[3,1,512]{2,1,0:T(1,128)}, f32[16,72,128]{2,1,0:T(8,128)S(1)}) custom-call(s32[1]{0:T(128)} %bitcast.place_ref, s32[1,2]{1,0:T(1,128)S(1)} %copy-done.9, bf16[256,2048]{1,0:T(8,128)(2,1)S(1)} %get-tuple-element.14.onehot, bf16[2048,256]{1,0:T(8,128)(2,1)S(1)} %get-tuple-element.15.turned, s32[1,2048]{1,0:T(1,128)S(1)} %get-tuple-element.16.lanes_of, ...), custom_call_target="tpu_custom_call" | custom-call | tf_op jit(solution)/shard_map/render/pallas_call | solution.py:721
  47.1 0.0 copy-start.3
  47.1 0.0 copy-start.4
  47.2 14.4 %all_to_all.21.arrived_ref = f32[16,72,128]{2,1,0:T(8,128)S(1)} all-to-all(f32[16,72,128]{2,1,0:T(8,128)S(1)} %get-tuple-element.18), channel_id=1, replica_groups=mesh['view'=16,'tile'=16] {'tile'}, dimensions={0} | all-to-all | bytes 1179648 | tf_op jit(solution)/shard_map/all_to_all | solution.py:773
  61.5 0.7 merge.1.after_ref
  62.3 0.0 copy-done.1
  62.3 5.4 %all-to-all-start.3 = ((f32[16,8,128]{2,1,0:T(8,128)}), f32[16,8,128]{2,1,0:T(8,128)S(1)}, u32[]{:S(2)}, u32[]{:S(2)}) async-start(f32[16,8,128]{2,1,0:T(8,128)} %merge.1.after_ref), calls=%async_computation.3 | async-start | bytes 131072 | tf_op jit(solution)/shard_map/all_to_all | solution.py:773
  67.7 0.0 copy-start.2
  67.7 0.6 columns.1.onehot_ref
  68.3 7.2 %all-to-all-done.3.arrived_ref = f32[16,8,128]{2,1,0:T(8,128)S(1)} async-done(((f32[16,8,128]{2,1,0:T(8,128)}), f32[16,8,128]{2,1,0:T(8,128)S(1)}, u32[]{:S(2)}, u32[]{:S(2)}) %all-to-all-start.3) | async-done | bytes 65568 | tf_op jit(solution)/shard_map/all_to_all | solution.py:773
  75.5 0.0 copy-done.3
  75.5 0.0 copy-done.4
  75.5 0.0 copy-done.2
  75.5 2.0 %update.1 = (f32[59,1024]{1,0:T(8,128)}, f32[59,1024]{1,0:T(8,128)}, f32[59,1024]{1,0:T(8,128)}) custom-call(bf16[1024,1024]{1,0:T(8,128)(2,1)S(1)} %columns.1.onehot_ref, f32[70,8,128]{2,1,0:T(8,128)S(1)} %copy-done.2, f32[16,8,128]{2,1,0:T(8,128)S(1)} %all-to-all-done.3.arrived_ref, f32[59,1024]{1,0:T(8,128)S(1)} %copy-done, f32[59,1024]{1,0:T(8,128)S(1)} %copy-done.3, ...), custom_call_target="tpu_custom_call" | custom-call | tf_op jit(solution)/shard_map/update/pallas_call | solution.py:752
Async XLA Ops:
  0.6 27.3 %copy-start.5 = (s32[16,64]{1,0:T(8,128)S(1)}, s32[16,64]{1,0:T(8,128)}, u32[]{:S(2)}) copy-start(s32[16,64]{1,0:T(8,128)} %ids_ref.5) | copy-start | bytes 12292
  0.6 27.3 %copy-start = (f32[59,1024]{1,0:T(8,128)S(1)}, f32[59,1024]{1,0:T(8,128)}, u32[]{:S(2)}) copy-start(f32[59,1024]{1,0:T(8,128)} %params_ref.5) | copy-start | bytes 724996
  0.7 27.3 %copy-start.6 = (f32[16,11]{1,0:T(8,128)S(1)}, f32[16,11]{1,0:T(8,128)}, u32[]{:S(2)}) copy-start(f32[16,11]{1,0:T(8,128)} %cameras_ref.3) | copy-start | bytes 2116
  0.7 27.3 %copy-start.7 = (s32[1,2,1024]{2,1,0:T(2,128)S(1)}, s32[1,2,1024]{2,1,0:T(2,128)}, u32[]{:S(2)}) copy-start(s32[1,2,1024]{2,1,0:T(2,128)} %lists_ref.1) | copy-start | bytes 24580
  0.7 38.9 %copy-start.8 = (f32[1,3,512]{2,0,1:T(1,128)S(1)}, f32[1,3,512]{2,0,1:T(1,128)}, u32[]{:S(2)}) copy-start(f32[1,3,512]{2,0,1:T(1,128)} %param.15) | copy-start | bytes 18436
  0.7 38.9 %copy-start.9 = (s32[1,2]{1,0:T(1,128)S(1)}, s32[1,2]{1,0:T(1,128)}, u32[]{:S(2)}) copy-start(s32[1,2]{1,0:T(1,128)} %counts_ref.1) | copy-start | bytes 28
  21.2 18.4 %all-to-all-start.1 = ((f32[16,72,128]{2,1,0:T(8,128)}), f32[16,72,128]{2,1,0:T(8,128)S(1)}, u32[]{:S(2)}, u32[]{:S(2)}) async-start(f32[16,72,128]{2,1,0:T(8,128)} %spread.1.after_ref), calls=%async_computation.1 | async-start | bytes 1179648 | tf_op jit(solution)/shard_map/all_to_all | solution.py:773
  30.3 31.9 %copy-start.1 = (f32[70,8,128]{2,1,0:T(8,128)}, f32[70,8,128]{2,1,0:T(8,128)S(1)}, u32[]{:S(2)}) copy-start(f32[70,8,128]{2,1,0:T(8,128)S(1)} %get-tuple-element.19.spread_ref) | copy-start | bytes 860164
  47.1 28.4 %copy-start.3 = (f32[59,1024]{1,0:T(8,128)S(1)}, f32[59,1024]{1,0:T(8,128)}, u32[]{:S(2)}) copy-start(f32[59,1024]{1,0:T(8,128)} %first_ref.1) | copy-start | bytes 724996
  47.1 28.4 %copy-start.4 = (f32[59,1024]{1,0:T(8,128)S(1)}, f32[59,1024]{1,0:T(8,128)}, u32[]{:S(2)}) copy-start(f32[59,1024]{1,0:T(8,128)} %second_ref.1) | copy-start | bytes 724996
  62.3 13.2 %all-to-all-start.3 = ((f32[16,8,128]{2,1,0:T(8,128)}), f32[16,8,128]{2,1,0:T(8,128)S(1)}, u32[]{:S(2)}, u32[]{:S(2)}) async-start(f32[16,8,128]{2,1,0:T(8,128)} %merge.1.after_ref), calls=%async_computation.3 | async-start | bytes 131072 | tf_op jit(solution)/shard_map/all_to_all | solution.py:773
  67.7 7.8 %copy-start.2 = (f32[70,8,128]{2,1,0:T(8,128)S(1)}, f32[70,8,128]{2,1,0:T(8,128)}, u32[]{:S(2)}) copy-start(f32[70,8,128]{2,1,0:T(8,128)} %copy-done.1) | copy-start | bytes 860164

commit v8 on v7

--- a/solution.py
+++ b/solution.py
@@ -166,7 +166,7 @@
 ROWS = 64
 LOG2E = 1.4426950408889634
 MIB = 1 << 20
-MIXED = 8
+MIXED = 6
 
 
 def iota(shape, dim):
@@ -248,7 +248,7 @@
     return main, last[0:1, :]
 
 
-def spread_kernel(arrived_ref, out_ref):
+def spread_kernel(after_ref, place_ref, arrived_ref, out_ref):
     for pair in range(8):
         main, last = unpack_pair(arrived_ref[2 * pair], arrived_ref[2 * pair + 1])
         for peer in range(16):
@@ -260,7 +260,12 @@
     return jnp.transpose(jnp.broadcast_to(row.astype(F32), (128, 128))).astype(jnp.int32)
 
 
-def columns_kernel(after_ref, ids_ref, columns_ref):
+def columns_kernel(
+    after_ref, ids_ref, cameras_ref, params_ref, columns_ref, rows_ref, split, picked_ref
+):
+    pick_rows(ids_ref, params_ref, split, picked_ref)
+    for place, array in enumerate(raw_rows(picked_ref) + camera_arrays(cameras_ref)):
+        rows_ref[place] = array
     for pair in range(8):
         row = jnp.concatenate(
             [ids_ref[2 * pair : 2 * pair + 1, :], ids_ref[2 * pair + 1 : 2 * pair + 2, :]], axis=1
@@ -273,21 +278,12 @@
 
 def prepare_kernel(
     after_ref,
-    ids_ref,
-    cameras_ref,
-    params_ref,
     lists_ref,
-    rows_ref,
     onehot_ref,
     turned_ref,
     lanes_ref,
     groups_ref,
-    split,
-    picked_ref,
 ):
-    pick_rows(ids_ref, params_ref, split, picked_ref)
-    for place, array in enumerate(raw_rows(picked_ref) + camera_arrays(cameras_ref)):
-        rows_ref[place] = array
 
     turn = (iota((128, 1024), 0) == (iota((128, 1024), 1) >> 3)).astype(BF16)
     pick_block = iota((8, 1024), 0) == (iota((8, 1024), 1) & 7)
@@ -438,7 +434,7 @@
         alphas[tile] = mm(coefficients, basis_three, ((0,), (0,)))
         colour_rows.append(stacked(colour, 1024))
 
-    steps = 8
+    steps = 16
 
     def advance(outer, held):
         held = list(held)
@@ -677,44 +673,43 @@
     )(visible, cameras, params)
 
 
-def spread_call(arrived):
+def spread_call(after, place, arrived):
     return pl.pallas_call(
         spread_kernel,
         out_shape=f32_shape(16, 72, 128),
-        in_specs=[VMEM],
+        in_specs=[pl.BlockSpec(memory_space=pl.ANY), SMEM, VMEM],
         out_specs=VMEM,
         compiler_params=pltpu.CompilerParams(vmem_limit_bytes=6 * MIB),
         name="spread",
-    )(arrived)
-
-
-def columns_call(after, visible):
+    )(after, place, arrived)
+
+
+def columns_call(after, visible, cameras, params):
     return pl.pallas_call(
         columns_kernel,
-        out_shape=jax.ShapeDtypeStruct((1024, 1024), BF16),
-        in_specs=[pl.BlockSpec(memory_space=pl.ANY), VMEM],
-        out_specs=VMEM,
-        compiler_params=pltpu.CompilerParams(vmem_limit_bytes=8 * MIB),
+        out_shape=(jax.ShapeDtypeStruct((1024, 1024), BF16), f32_shape(PARAMS + 11, 8, 128)),
+        in_specs=[pl.BlockSpec(memory_space=pl.ANY), VMEM, SMEM, VMEM],
+        out_specs=(VMEM, VMEM),
+        scratch_shapes=[pltpu.VMEM((192, 1024), BF16), pltpu.VMEM((512, 128), F32)],
+        compiler_params=pltpu.CompilerParams(vmem_limit_bytes=12 * MIB),
         name="columns",
-    )(after, visible)
-
-
-def prepare_call(after, visible, cameras, params, lists):
+    )(after, visible, cameras, params)
+
+
+def prepare_call(after, lists):
     return pl.pallas_call(
         prepare_kernel,
         out_shape=(
-            f32_shape(PARAMS + 11, 8, 128),
             jax.ShapeDtypeStruct((256, 2048), BF16),
             jax.ShapeDtypeStruct((2048, 256), BF16),
             jax.ShapeDtypeStruct((1, 2048), jnp.int32),
             jax.ShapeDtypeStruct((1, 2048), jnp.int32),
         ),
-        in_specs=[pl.BlockSpec(memory_space=pl.ANY), VMEM, SMEM, VMEM, VMEM],
-        out_specs=(VMEM, VMEM, VMEM, VMEM, VMEM),
-        scratch_shapes=[pltpu.VMEM((192, 1024), BF16), pltpu.VMEM((512, 128), F32)],
+        in_specs=[pl.BlockSpec(memory_space=pl.ANY), VMEM],
+        out_specs=(VMEM, VMEM, VMEM, VMEM),
         compiler_params=pltpu.CompilerParams(vmem_limit_bytes=16 * MIB),
         name="prepare",
-    )(after, visible, cameras, params, lists)
+    )(after, lists)
 
 
 def render_call(place, counts, onehot, turned, lanes, groups, targets, everyone):
@@ -774,15 +769,14 @@
 
 
 def shards(params, first, second, visible, cameras, tile_lists, tile_blocks, targets):
-    outgoing = project_call(
-        *[pltpu.with_memory_space_constraint(array, pltpu.HBM) for array in (visible, cameras, params)]
-    )
-    block = spread_call(exchanged(outgoing, "view"))
-    everyone = exchanged(block, "tile")
-    rows, onehot, turned, lanes, groups = [
-        kept(table) for table in prepare_call(block, visible, cameras, params, tile_lists)
+    held = [
+        pltpu.with_memory_space_constraint(array, pltpu.HBM)
+        for array in (visible, cameras, params, tile_lists)
     ]
+    outgoing = project_call(*held[:3])
+    onehot, turned, lanes, groups = [kept(table) for table in prepare_call(outgoing, held[3])]
     place = lax.axis_index("tile").astype(jnp.int32).reshape(1)
+    everyone = exchanged(spread_call(groups, place, exchanged(outgoing, "view")), "tile")
     image, sums = render_call(
         place,
         tile_blocks,
@@ -795,9 +789,9 @@
     )
     merged = merge_call(exchanged(sums, "tile"))
     returned = exchanged(merged, "view")
-    columns = columns_call(merged, visible)
+    columns, rows = columns_call(merged, visible, cameras, kept(params))
     new_params, new_first, new_second = update_call(
-        kept(columns), rows, returned, kept(params), kept(first), kept(second)
+        kept(columns), kept(rows), returned, kept(params), kept(first), kept(second)
     )
     return (new_params, new_first, new_second, jnp.transpose(image, (1, 0, 2)))
 

time: 77.9 us -> 77.6 us (level)
  waiting for transfers between devices: 16.5 us -> 11.9 us
  starting transfers between devices: 12.2 us -> 15.5 us
    all_to_all x2, waiting for transfers between devices: 16.5 us -> 11.9 us  [exchanged(): return kept(lax.all_to_all(array, axis, 0, 0, tiled=True))]
    all_to_all x2, starting transfers between devices: 12.2 us -> 15.5 us  [exchanged(): return kept(lax.all_to_all(array, axis, 0, 0, tiled=True))]
    pallas_call x1, Pallas kernels: 0.95 us -> 0.13 us  [spread_call(): pl.pallas_call(spread_kernel, out_shape=f32_shape(16, 72, 128), in_specs=...]
  transfers between devices with their start and end apart: 2 -> 2, of which waited for: 2 -> 2; matrix products, arithmetic and copies ran while one was open for 0% -> 0% of each run, Pallas kernels for 4% -> 5%
where the time goes in v8:
time: 77.6 us; the launch traced here: 77.2 us
  blocking collectives  32.3 us (42%)
  Pallas kernels  16.8 us (22%)
  starting transfers between devices  15.5 us (20%)
  waiting for transfers between devices  11.9 us (15%)
    all_to_all x2, blocking collectives, exchanged(): return kept(lax.all_to_all(array, axis, 0, 0, tiled=True))  32.3 us
    all_to_all x2, starting transfers between devices, exchanged(): return kept(lax.all_to_all(array, axis, 0, 0, tiled=True))  15.5 us
    all_to_all x2, waiting for transfers between devices, exchanged(): return kept(lax.all_to_all(array, axis, 0, 0, tiled=True))  11.9 us
    pallas_call x1, Pallas kernels, render_call(): pl.pallas_call(render_kernel, out_shape=(f32_shape(3, 1, 512), f32_shape(...  7.67 us
    pallas_call x1, Pallas kernels, project_call(): pl.pallas_call(project_kernel, out_shape=f32_shape(16, 8, 128), in_specs=...  2.6 us
    pallas_call x1, Pallas kernels, update_call(): pl.pallas_call(update_kernel, out_shape=(shape, shape, shape), in_specs=[...  2.01 us
    pallas_call x1, Pallas kernels, columns_call(): pl.pallas_call(columns_kernel, out_shape=(jax.ShapeDtypeStruct((1024, 102...  2.01 us
    pallas_call x1, Pallas kernels, prepare_call(): pl.pallas_call(prepare_kernel, out_shape=(jax.ShapeDtypeStruct((256, 2048...  1.64 us
  transfers between devices with their start and end apart: 2, of which 2 were waited for; matrix products, arithmetic and copies ran while one was open for 0% of the time, Pallas kernels for 5%

profile of v8, /device:TPU:1, one launch (start us, length us, event | category | flops | bytes accessed | tf_op | source)
XLA Modules:
  0.0 77.2 jit_solution(16468454513139969262)
XLA Ops:
  0.6 0.0 copy-start.5
  0.6 0.0 copy-start.6
  0.7 2.6 %project.1.after_ref = f32[16,8,128]{2,1,0:T(8,128)} custom-call(s32[16,64]{1,0:T(8,128)} %ids_ref.3, f32[16,11]{1,0:T(8,128)} %cameras_ref.3, f32[59,1024]{1,0:T(8,128)} %params_ref.5), custom_call_target="tpu_custom_call" | custom-call | tf_op jit(solution)/shard_map/project/pallas_call | solution.py:661
  3.3 10.0 %all-to-all-start = ((f32[16,8,128]{2,1,0:T(8,128)}), f32[16,8,128]{2,1,0:T(8,128)S(1)}, u32[]{:S(2)}, u32[]{:S(2)}) async-start(f32[16,8,128]{2,1,0:T(8,128)} %project.1.after_ref), calls=%async_computation | async-start | bytes 131072 | tf_op jit(solution)/shard_map/all_to_all | solution.py:768
  13.2 1.6 %prepare.1 = (bf16[256,2048]{1,0:T(8,128)(2,1)S(1)}, bf16[2048,256]{1,0:T(8,128)(2,1)S(1)}, s32[1,2048]{1,0:T(1,128)S(1)}, s32[1,2048]{1,0:T(1,128)S(1)}) custom-call(f32[16,8,128]{2,1,0:T(8,128)} %project.1.after_ref, s32[1,2,1024]{2,1,0:T(2,128)} %lists_ref.1), custom_call_target="tpu_custom_call" | custom-call | tf_op jit(solution)/shard_map/prepare/pallas_call | solution.py:700
  14.9 6.1 %all-to-all-done.arrived_ref = f32[16,8,128]{2,1,0:T(8,128)S(1)} async-done(((f32[16,8,128]{2,1,0:T(8,128)}), f32[16,8,128]{2,1,0:T(8,128)S(1)}, u32[]{:S(2)}, u32[]{:S(2)}) %all-to-all-start) | async-done | bytes 65568 | tf_op jit(solution)/shard_map/all_to_all | solution.py:768
  21.0 0.1 spread.1
  21.1 18.2 %all_to_all.20.everyone_ref = f32[16,72,128]{2,1,0:T(8,128)S(1)} all-to-all(f32[16,72,128]{2,1,0:T(8,128)S(1)} %spread.1), channel_id=1, replica_groups=mesh['view'=16,'tile'=16] {'tile'}, dimensions={0} | all-to-all | bytes 1179648 | tf_op jit(solution)/shard_map/all_to_all | solution.py:768
  39.3 0.0 copy-done.5
  39.3 0.0 copy-done.6
  39.3 0.0 copy-start
  39.3 0.0 copy-start.3
  39.3 0.0 copy-start.4
  39.4 0.0 copy-start.1
  39.4 0.0 copy-start.2
  39.4 7.7 %render.1 = (f32[3,1,512]{2,1,0:T(1,128)}, f32[16,72,128]{2,1,0:T(8,128)S(1)}) custom-call(s32[1]{0:T(128)} %bitcast.place_ref, s32[1,2]{1,0:T(1,128)S(1)} %copy-done.6, bf16[256,2048]{1,0:T(8,128)(2,1)S(1)} %get-tuple-element.15.onehot, bf16[2048,256]{1,0:T(8,128)(2,1)S(1)} %get-tuple-element.16.turned, s32[1,2048]{1,0:T(1,128)S(1)} %get-tuple-element.17.lanes_of, ...), custom_call_target="tpu_custom_call" | custom-call | tf_op jit(solution)/shard_map/render/pallas_call | solution.py:716
  47.1 14.1 %all_to_all.21.arrived_ref = f32[16,72,128]{2,1,0:T(8,128)S(1)} all-to-all(f32[16,72,128]{2,1,0:T(8,128)S(1)} %get-tuple-element.19), channel_id=1, replica_groups=mesh['view'=16,'tile'=16] {'tile'}, dimensions={0} | all-to-all | bytes 1179648 | tf_op jit(solution)/shard_map/all_to_all | solution.py:768
  61.1 0.7 merge.1.after_ref
  61.9 5.5 %all-to-all-start.3 = ((f32[16,8,128]{2,1,0:T(8,128)}), f32[16,8,128]{2,1,0:T(8,128)S(1)}, u32[]{:S(2)}, u32[]{:S(2)}) async-start(f32[16,8,128]{2,1,0:T(8,128)} %merge.1.after_ref), calls=%async_computation.3 | async-start | bytes 131072 | tf_op jit(solution)/shard_map/all_to_all | solution.py:768
  67.4 0.0 copy-done
  67.4 0.0 copy-done.3
  67.4 0.0 copy-done.4
  67.4 2.0 %columns.1 = (bf16[1024,1024]{1,0:T(8,128)(2,1)S(1)}, f32[70,8,128]{2,1,0:T(8,128)S(1)}) custom-call(f32[16,8,128]{2,1,0:T(8,128)} %merge.1.after_ref, s32[16,64]{1,0:T(8,128)S(1)} %copy-done.3, f32[16,11]{1,0:T(8,128)S(1)} %copy-done.4, f32[59,1024]{1,0:T(8,128)S(1)} %copy-done), custom_call_target="tpu_custom_call" | custom-call | tf_op jit(solution)/shard_map/columns/pallas_call | solution.py:688
  69.4 5.8 %all-to-all-done.3.arrived_ref = f32[16,8,128]{2,1,0:T(8,128)S(1)} async-done(((f32[16,8,128]{2,1,0:T(8,128)}), f32[16,8,128]{2,1,0:T(8,128)S(1)}, u32[]{:S(2)}, u32[]{:S(2)}) %all-to-all-start.3) | async-done | bytes 65568 | tf_op jit(solution)/shard_map/all_to_all | solution.py:768
  75.2 0.0 copy-done.1
  75.2 0.0 copy-done.2
  75.2 2.0 %update.1 = (f32[59,1024]{1,0:T(8,128)}, f32[59,1024]{1,0:T(8,128)}, f32[59,1024]{1,0:T(8,128)}) custom-call(bf16[1024,1024]{1,0:T(8,128)(2,1)S(1)} %get-tuple-element.20.onehot_ref, f32[70,8,128]{2,1,0:T(8,128)S(1)} %get-tuple-element.21.spread_ref, f32[16,8,128]{2,1,0:T(8,128)S(1)} %all-to-all-done.3.arrived_ref, f32[59,1024]{1,0:T(8,128)S(1)} %copy-done, ...), custom_call_target="tpu_custom_call" | custom-call | tf_op jit(solution)/shard_map/update/pallas_call | solution.py:747
Async XLA Ops:
  0.6 38.7 %copy-start.5 = (f32[1,3,512]{2,0,1:T(1,128)S(1)}, f32[1,3,512]{2,0,1:T(1,128)}, u32[]{:S(2)}) copy-start(f32[1,3,512]{2,0,1:T(1,128)} %param.15) | copy-start | bytes 18436
  0.6 38.7 %copy-start.6 = (s32[1,2]{1,0:T(1,128)S(1)}, s32[1,2]{1,0:T(1,128)}, u32[]{:S(2)}) copy-start(s32[1,2]{1,0:T(1,128)} %counts_ref.1) | copy-start | bytes 28
  3.3 17.7 %all-to-all-start = ((f32[16,8,128]{2,1,0:T(8,128)}), f32[16,8,128]{2,1,0:T(8,128)S(1)}, u32[]{:S(2)}, u32[]{:S(2)}) async-start(f32[16,8,128]{2,1,0:T(8,128)} %project.1.after_ref), calls=%async_computation | async-start | bytes 131072 | tf_op jit(solution)/shard_map/all_to_all | solution.py:768
  39.3 28.1 %copy-start = (f32[59,1024]{1,0:T(8,128)S(1)}, f32[59,1024]{1,0:T(8,128)}, u32[]{:S(2)}) copy-start(f32[59,1024]{1,0:T(8,128)} %params_ref.5) | copy-start | bytes 724996
  39.3 28.1 %copy-start.3 = (s32[16,64]{1,0:T(8,128)S(1)}, s32[16,64]{1,0:T(8,128)}, u32[]{:S(2)}) copy-start(s32[16,64]{1,0:T(8,128)} %ids_ref.3) | copy-start | bytes 12292
  39.3 28.1 %copy-start.4 = (f32[16,11]{1,0:T(8,128)S(1)}, f32[16,11]{1,0:T(8,128)}, u32[]{:S(2)}) copy-start(f32[16,11]{1,0:T(8,128)} %cameras_ref.3) | copy-start | bytes 2116
  39.4 35.9 %copy-start.1 = (f32[59,1024]{1,0:T(8,128)S(1)}, f32[59,1024]{1,0:T(8,128)}, u32[]{:S(2)}) copy-start(f32[59,1024]{1,0:T(8,128)} %first_ref.1) | copy-start | bytes 724996
  39.4 35.9 %copy-start.2 = (f32[59,1024]{1,0:T(8,128)S(1)}, f32[59,1024]{1,0:T(8,128)}, u32[]{:S(2)}) copy-start(f32[59,1024]{1,0:T(8,128)} %second_ref.1) | copy-start | bytes 724996
  61.9 13.3 %all-to-all-start.3 = ((f32[16,8,128]{2,1,0:T(8,128)}), f32[16,8,128]{2,1,0:T(8,128)S(1)}, u32[]{:S(2)}, u32[]{:S(2)}) async-start(f32[16,8,128]{2,1,0:T(8,128)} %merge.1.after_ref), calls=%async_computation.3 | async-start | bytes 131072 | tf_op jit(solution)/shard_map/all_to_all | solution.py:768

commit v9 on v8

--- a/solution.py
+++ b/solution.py
@@ -166,7 +166,7 @@
 ROWS = 64
 LOG2E = 1.4426950408889634
 MIB = 1 << 20
-MIXED = 6
+MIXED = 8
 
 
 def iota(shape, dim):
@@ -228,7 +228,7 @@
         picked_ref[pair * 128 + ROWS : pair * 128 + 2 * ROWS, :] = picked[:, 128:]
 
 
-def project_kernel(ids_ref, cameras_ref, params_ref, send_ref, split, swap, picked_ref):
+def project_kernel(place_ref, ids_ref, cameras_ref, params_ref, send_ref, split, swap, picked_ref):
     pick_rows(ids_ref, params_ref, split, picked_ref)
     values = project(raw_rows(picked_ref), camera_arrays(cameras_ref))
     for place in range(8):
@@ -248,7 +248,7 @@
     return main, last[0:1, :]
 
 
-def spread_kernel(after_ref, place_ref, arrived_ref, out_ref):
+def spread_kernel(arrived_ref, out_ref):
     for pair in range(8):
         main, last = unpack_pair(arrived_ref[2 * pair], arrived_ref[2 * pair + 1])
         for peer in range(16):
@@ -434,7 +434,7 @@
         alphas[tile] = mm(coefficients, basis_three, ((0,), (0,)))
         colour_rows.append(stacked(colour, 1024))
 
-    steps = 16
+    steps = 8
 
     def advance(outer, held):
         held = list(held)
@@ -657,11 +657,11 @@
     return jax.ShapeDtypeStruct(shape, F32)
 
 
-def project_call(visible, cameras, params):
+def project_call(place, visible, cameras, params):
     return pl.pallas_call(
         project_kernel,
         out_shape=f32_shape(16, 8, 128),
-        in_specs=[VMEM, SMEM, VMEM],
+        in_specs=[SMEM, VMEM, SMEM, VMEM],
         out_specs=VMEM,
         scratch_shapes=[
             pltpu.VMEM((192, 1024), BF16),
@@ -670,18 +670,18 @@
         ],
         compiler_params=pltpu.CompilerParams(vmem_limit_bytes=12 * MIB),
         name="project",
-    )(visible, cameras, params)
-
-
-def spread_call(after, place, arrived):
+    )(place, visible, cameras, params)
+
+
+def spread_call(arrived):
     return pl.pallas_call(
         spread_kernel,
         out_shape=f32_shape(16, 72, 128),
-        in_specs=[pl.BlockSpec(memory_space=pl.ANY), SMEM, VMEM],
+        in_specs=[VMEM],
         out_specs=VMEM,
         compiler_params=pltpu.CompilerParams(vmem_limit_bytes=6 * MIB),
         name="spread",
-    )(after, place, arrived)
+    )(arrived)
 
 
 def columns_call(after, visible, cameras, params):
@@ -769,14 +769,16 @@
 
 
 def shards(params, first, second, visible, cameras, tile_lists, tile_blocks, targets):
+    place = lax.axis_index("tile").astype(jnp.int32).reshape(1)
     held = [
         pltpu.with_memory_space_constraint(array, pltpu.HBM)
-        for array in (visible, cameras, params, tile_lists)
+        for array in (visible, cameras, params)
     ]
-    outgoing = project_call(*held[:3])
-    onehot, turned, lanes, groups = [kept(table) for table in prepare_call(outgoing, held[3])]
-    place = lax.axis_index("tile").astype(jnp.int32).reshape(1)
-    everyone = exchanged(spread_call(groups, place, exchanged(outgoing, "view")), "tile")
+    outgoing = project_call(place, *held)
+    everyone = exchanged(spread_call(exchanged(outgoing, "view")), "tile")
+    onehot, turned, lanes, groups = [
+        kept(table) for table in prepare_call(everyone, kept(tile_lists))
+    ]
     image, sums = render_call(
         place,
         tile_blocks,

time: 77.6 us -> 77.6 us (level)
  blocking collectives: 32.3 us -> 49.8 us
  starting transfers between devices: 15.5 us -> 5.51 us
  waiting for transfers between devices: 11.9 us -> 5.78 us
  Pallas kernels: 16.8 us -> 15.4 us
    all_to_all x2 -> x3, blocking collectives: 32.3 us -> 49.8 us  [exchanged(): return kept(lax.all_to_all(array, axis, 0, 0, tiled=True))]
    all_to_all x2 -> x1, starting transfers between devices: 15.5 us -> 5.51 us  [exchanged(): return kept(lax.all_to_all(array, axis, 0, 0, tiled=True))]
    all_to_all x2 -> x1, waiting for transfers between devices: 11.9 us -> 5.78 us  [exchanged(): return kept(lax.all_to_all(array, axis, 0, 0, tiled=True))]
  transfers between devices with their start and end apart: 2 -> 1, of which waited for: 2 -> 1; matrix products, arithmetic and copies ran while one was open for 0% -> 0% of each run, Pallas kernels for 5% -> 3%
where the time goes in v9:
time: 77.6 us; the launch traced here: 77.3 us
  blocking collectives  49.8 us (64%)
  Pallas kernels  15.4 us (20%)
  waiting for transfers between devices  5.78 us (7%)
  starting transfers between devices  5.51 us (7%)
  between operations  0.78 us (1%)
    all_to_all x3, blocking collectives, exchanged(): return kept(lax.all_to_all(array, axis, 0, 0, tiled=True))  49.8 us
    pallas_call x1, Pallas kernels, render_call(): pl.pallas_call(render_kernel, out_shape=(f32_shape(3, 1, 512), f32_shape(...  7.57 us
    all_to_all x1, waiting for transfers between devices, exchanged(): return kept(lax.all_to_all(array, axis, 0, 0, tiled=True))  5.78 us
    all_to_all x1, starting transfers between devices, exchanged(): return kept(lax.all_to_all(array, axis, 0, 0, tiled=True))  5.51 us
    pallas_call x1, Pallas kernels, columns_call(): pl.pallas_call(columns_kernel, out_shape=(jax.ShapeDtypeStruct((1024, 102...  2.01 us
    pallas_call x1, Pallas kernels, update_call(): pl.pallas_call(update_kernel, out_shape=(shape, shape, shape), in_specs=[...  2 us
    pallas_call x1, Pallas kernels, project_call(): pl.pallas_call(project_kernel, out_shape=f32_shape(16, 8, 128), in_specs=...  1.97 us
  transfers between devices with their start and end apart: 1, of which 1 were waited for; matrix products, arithmetic and copies ran while one was open for 0% of the time, Pallas kernels for 3%

profile of v9, /device:TPU:1, one launch (start us, length us, event | category | flops | bytes accessed | tf_op | source)
XLA Modules:
  0.0 77.3 jit_solution(4365430494609210616)
XLA Ops:
  0.6 0.0 copy-start.5
  0.6 0.0 copy-start.6
  0.7 0.0 copy-start.7
  0.7 2.0 %project.1 = f32[16,8,128]{2,1,0:T(8,128)S(1)} custom-call(s32[1]{0:T(128)} %bitcast.place_ref, s32[16,64]{1,0:T(8,128)} %ids_ref.3, f32[16,11]{1,0:T(8,128)} %cameras_ref.3, f32[59,1024]{1,0:T(8,128)} %params_ref.5), custom_call_target="tpu_custom_call" | custom-call | tf_op jit(solution)/shard_map/project/pallas_call | solution.py:661
  2.6 17.5 %all_to_all.20.arrived_ref = f32[16,8,128]{2,1,0:T(8,128)S(1)} all-to-all(f32[16,8,128]{2,1,0:T(8,128)S(1)} %project.1), channel_id=1, replica_groups=mesh['view'=16,'tile'=16] {'view'}, dimensions={0} | all-to-all | bytes 131072 | tf_op jit(solution)/shard_map/all_to_all | solution.py:768
  20.2 0.1 spread.1
  20.3 18.2 %all_to_all.21.after_ref.everyone_ref = f32[16,72,128]{2,1,0:T(8,128)S(1)} all-to-all(f32[16,72,128]{2,1,0:T(8,128)S(1)} %spread.1), channel_id=1, replica_groups=mesh['view'=16,'tile'=16] {'tile'}, dimensions={0} | all-to-all | bytes 1179648 | tf_op jit(solution)/shard_map/all_to_all | solution.py:768
  38.5 0.0 copy-done.5
  38.5 0.9 %prepare.1 = (bf16[256,2048]{1,0:T(8,128)(2,1)S(1)}, bf16[2048,256]{1,0:T(8,128)(2,1)S(1)}, s32[1,2048]{1,0:T(1,128)S(1)}, s32[1,2048]{1,0:T(1,128)S(1)}) custom-call(f32[16,72,128]{2,1,0:T(8,128)S(1)} %all_to_all.21.after_ref.everyone_ref, s32[1,2,1024]{2,1,0:T(2,128)S(1)} %copy-done.5), custom_call_target="tpu_custom_call" | custom-call | tf_op jit(solution)/shard_map/prepare/pallas_call | solution.py:700
  39.5 0.0 copy-done.6
  39.5 0.0 copy-done.7
  39.5 0.0 copy-start
  39.5 0.0 copy-start.3
  39.5 0.0 copy-start.4
  39.5 0.0 copy-start.1
  39.5 0.0 copy-start.2
  39.6 7.6 %render.1 = (f32[3,1,512]{2,1,0:T(1,128)}, f32[16,72,128]{2,1,0:T(8,128)S(1)}) custom-call(s32[1]{0:T(128)} %bitcast.place_ref, s32[1,2]{1,0:T(1,128)S(1)} %copy-done.7, bf16[256,2048]{1,0:T(8,128)(2,1)S(1)} %get-tuple-element.15.onehot, bf16[2048,256]{1,0:T(8,128)(2,1)S(1)} %get-tuple-element.16.turned, s32[1,2048]{1,0:T(1,128)S(1)} %get-tuple-element.17.lanes_of, ...), custom_call_target="tpu_custom_call" | custom-call | tf_op jit(solution)/shard_map/render/pallas_call | solution.py:716
  47.1 14.1 %all_to_all.22.arrived_ref = f32[16,72,128]{2,1,0:T(8,128)S(1)} all-to-all(f32[16,72,128]{2,1,0:T(8,128)S(1)} %get-tuple-element.19), channel_id=1, replica_groups=mesh['view'=16,'tile'=16] {'tile'}, dimensions={0} | all-to-all | bytes 1179648 | tf_op jit(solution)/shard_map/all_to_all | solution.py:768
  61.2 0.7 merge.1.after_ref
  61.9 5.5 %all-to-all-start.3 = ((f32[16,8,128]{2,1,0:T(8,128)}), f32[16,8,128]{2,1,0:T(8,128)S(1)}, u32[]{:S(2)}, u32[]{:S(2)}) async-start(f32[16,8,128]{2,1,0:T(8,128)} %merge.1.after_ref), calls=%async_computation.3 | async-start | bytes 131072 | tf_op jit(solution)/shard_map/all_to_all | solution.py:768
  67.5 0.0 copy-done
  67.5 0.0 copy-done.3
  67.5 0.0 copy-done.4
  67.5 2.0 %columns.1 = (bf16[1024,1024]{1,0:T(8,128)(2,1)S(1)}, f32[70,8,128]{2,1,0:T(8,128)S(1)}) custom-call(f32[16,8,128]{2,1,0:T(8,128)} %merge.1.after_ref, s32[16,64]{1,0:T(8,128)S(1)} %copy-done.3, f32[16,11]{1,0:T(8,128)S(1)} %copy-done.4, f32[59,1024]{1,0:T(8,128)S(1)} %copy-done), custom_call_target="tpu_custom_call" | custom-call | tf_op jit(solution)/shard_map/columns/pallas_call | solution.py:688
  69.5 5.8 %all-to-all-done.3.arrived_ref = f32[16,8,128]{2,1,0:T(8,128)S(1)} async-done(((f32[16,8,128]{2,1,0:T(8,128)}), f32[16,8,128]{2,1,0:T(8,128)S(1)}, u32[]{:S(2)}, u32[]{:S(2)}) %all-to-all-start.3) | async-done | bytes 65568 | tf_op jit(solution)/shard_map/all_to_all | solution.py:768
  75.3 0.0 copy-done.1
  75.3 0.0 copy-done.2
  75.3 2.0 %update.1 = (f32[59,1024]{1,0:T(8,128)}, f32[59,1024]{1,0:T(8,128)}, f32[59,1024]{1,0:T(8,128)}) custom-call(bf16[1024,1024]{1,0:T(8,128)(2,1)S(1)} %get-tuple-element.20.onehot_ref, f32[70,8,128]{2,1,0:T(8,128)S(1)} %get-tuple-element.21.spread_ref, f32[16,8,128]{2,1,0:T(8,128)S(1)} %all-to-all-done.3.arrived_ref, f32[59,1024]{1,0:T(8,128)S(1)} %copy-done, ...), custom_call_target="tpu_custom_call" | custom-call | tf_op jit(solution)/shard_map/update/pallas_call | solution.py:747
Async XLA Ops:
  0.6 37.9 %copy-start.5 = (s32[1,2,1024]{2,1,0:T(2,128)S(1)}, s32[1,2,1024]{2,1,0:T(2,128)}, u32[]{:S(2)}) copy-start(s32[1,2,1024]{2,1,0:T(2,128)} %lists_ref.1) | copy-start | bytes 24580
  0.6 38.8 %copy-start.6 = (f32[1,3,512]{2,0,1:T(1,128)S(1)}, f32[1,3,512]{2,0,1:T(1,128)}, u32[]{:S(2)}) copy-start(f32[1,3,512]{2,0,1:T(1,128)} %param.15) | copy-start | bytes 18436
  0.7 38.8 %copy-start.7 = (s32[1,2]{1,0:T(1,128)S(1)}, s32[1,2]{1,0:T(1,128)}, u32[]{:S(2)}) copy-start(s32[1,2]{1,0:T(1,128)} %counts_ref.1) | copy-start | bytes 28
  39.5 28.0 %copy-start = (f32[59,1024]{1,0:T(8,128)S(1)}, f32[59,1024]{1,0:T(8,128)}, u32[]{:S(2)}) copy-start(f32[59,1024]{1,0:T(8,128)} %params_ref.5) | copy-start | bytes 724996
  39.5 28.0 %copy-start.3 = (s32[16,64]{1,0:T(8,128)S(1)}, s32[16,64]{1,0:T(8,128)}, u32[]{:S(2)}) copy-start(s32[16,64]{1,0:T(8,128)} %ids_ref.3) | copy-start | bytes 12292
  39.5 28.0 %copy-start.4 = (f32[16,11]{1,0:T(8,128)S(1)}, f32[16,11]{1,0:T(8,128)}, u32[]{:S(2)}) copy-start(f32[16,11]{1,0:T(8,128)} %cameras_ref.3) | copy-start | bytes 2116
  39.5 35.8 %copy-start.1 = (f32[59,1024]{1,0:T(8,128)S(1)}, f32[59,1024]{1,0:T(8,128)}, u32[]{:S(2)}) copy-start(f32[59,1024]{1,0:T(8,128)} %first_ref.1) | copy-start | bytes 724996
  39.5 35.7 %copy-start.2 = (f32[59,1024]{1,0:T(8,128)S(1)}, f32[59,1024]{1,0:T(8,128)}, u32[]{:S(2)}) copy-start(f32[59,1024]{1,0:T(8,128)} %second_ref.1) | copy-start | bytes 724996
  61.9 13.3 %all-to-all-start.3 = ((f32[16,8,128]{2,1,0:T(8,128)}), f32[16,8,128]{2,1,0:T(8,128)S(1)}, u32[]{:S(2)}, u32[]{:S(2)}) async-start(f32[16,8,128]{2,1,0:T(8,128)} %merge.1.after_ref), calls=%async_computation.3 | async-start | bytes 131072 | tf_op jit(solution)/shard_map/all_to_all | solution.py:768
